TPU v7x, 8 devices: a whole 2x2x1 slice. The times are simulated.
8 devices in a mesh: dp: 1 (over z), gp: 8 (over y, x, core).
Axes of the slice: x: 2, y: 2, z: 1, core: 2. Of those that a mesh axis runs over, the one named last changes fastest.
Arguments:
- x_prev: float32 [8192, 84], P(('dp', 'gp'))
- x_cur: float32 [8192, 84], P(('dp', 'gp'))
- forcing: float32 [8192, 2, 5], P(('dp', 'gp'))
- grid_static: float32 [8192, 5], P(('dp', 'gp'))
- g2m_feat: float32 [8192, 4], P(('dp', 'gp'))
- m2g_feat: float32 [8192, 4], P(('dp', 'gp'))
- mesh_feat: float32 [4096, 3], P(('dp', 'gp'))
- mesh_edge_feat: float32 [4096, 6, 4], P(('dp', 'gp'))
- norm_stats: float32 [4, 84], replicated
- w_grid_in: bfloat16 [178, 512], replicated
- w_mesh_in: bfloat16 [3, 512], replicated
- w_eemb_in: bfloat16 [3, 4, 512], replicated
- w_embed_out: bfloat16 [5, 512, 512], replicated
- w_edge_in: bfloat16 [18, 1536, 512], replicated
- w_edge_out: bfloat16 [18, 512, 512], replicated
- w_node_in: bfloat16 [18, 1024, 512], replicated
- w_node_out: bfloat16 [18, 512, 512], replicated
- w_grid_self: bfloat16 [2, 512, 512], replicated
- w_out_hidden: bfloat16 [512, 512], replicated
- w_out_final: bfloat16 [512, 84], replicated
Outputs:
- output 1: float32 [8192, 84], P(('dp', 'gp'))
- output 2: float32 [8192, 84], P(('dp', 'gp'))
All inputs are finite; a program needn't handle non-finite values.
Results may differ from a plain program's by a relative error of at most 0.00822618.
Values are sent between devices in bfloat16 or wider.
A program may use at most 1 GiB of HBM per device.

v0:
```python
import jax
import jax.numpy as jnp
from jax import lax
from jax.sharding import PartitionSpec as P


def layer_norm(values):
    centre = jnp.mean(values, axis=-1, keepdims=True)
    centred = values - centre
    spread = jnp.mean(centred * centred, axis=-1, keepdims=True)
    return centred * lax.rsqrt(spread + 1e-5)


def matmul_f32(values, weight):
    return jnp.dot(values, weight, preferred_element_type=jnp.float32)


def mlp_tail(pre_act, w_second):
    hidden = jax.nn.silu(pre_act).astype(jnp.bfloat16)
    return layer_norm(matmul_f32(hidden, w_second))


def residual(base, update):
    return (base.astype(jnp.float32) + update).astype(jnp.bfloat16)


def embed_static(features, w_first, w_second):
    return mlp_tail(matmul_f32(features.astype(jnp.bfloat16), w_first), w_second).astype(jnp.bfloat16)


def solution(mesh):
    group_size = mesh.shape["gp"]
    quarter_hop = group_size // 4
    row_spec = P(("dp", "gp"))
    edge_spec = P(("dp", "gp"), None, None)
    whole = P()

    def shift_pairs(hop_count):
        return [(source, (source + hop_count) % group_size) for source in range(group_size)]

    def local_run(x_prev, x_cur, forcing, grid_static, g2m_feat, m2g_feat, mesh_feat, mesh_edge_feat, norm_stats, w_grid_in, w_mesh_in, w_eemb_in, w_embed_out, w_edge_in, w_edge_out, w_node_in, w_node_out, w_grid_self, w_out_hidden, w_out_final):
        grid_dev = x_prev.shape[0]
        mesh_dev = mesh_feat.shape[0]
        grid_ratio = grid_dev // mesh_dev
        half_shard = mesh_dev // 2
        half_rows = half_shard * grid_ratio
        latent = w_embed_out.shape[-1]
        blocks = w_edge_in.shape[0]
        mesh_lat = embed_static(mesh_feat, w_mesh_in, w_embed_out[1])
        g2m_lat = embed_static(g2m_feat, w_eemb_in[0], w_embed_out[2])
        m2g_lat = embed_static(m2g_feat, w_eemb_in[1], w_embed_out[3])
        edge_base = embed_static(mesh_edge_feat, w_eemb_in[2], w_embed_out[4])
        in_mean = norm_stats[0]
        in_std = norm_stats[1]
        diff_mean = norm_stats[2]
        diff_std = norm_stats[3]
        state_prev = x_prev
        state_cur = x_cur
        outputs = []
        for step_idx in range(2):
            features = jnp.concatenate([(state_prev - in_mean) / in_std, (state_cur - in_mean) / in_std, forcing[:, step_idx, :], grid_static], axis=1)
            grid_lat = embed_static(features, w_grid_in, w_embed_out[0])
            from_prev = lax.ppermute(grid_lat[grid_dev - half_rows:], "gp", shift_pairs(1))
            senders = jnp.concatenate([from_prev, grid_lat[:grid_dev - half_rows]], axis=0)
            w_first = w_edge_in[0]
            recv_term = matmul_f32(mesh_lat, w_first[2 * latent:])
            pre_act = matmul_f32(g2m_lat, w_first[:latent]) + matmul_f32(senders, w_first[latent:2 * latent])
            pre_act = (pre_act.reshape(mesh_dev, grid_ratio, latent) + recv_term[:, None, :]).reshape(grid_dev, latent)
            enc_edge = residual(g2m_lat, mlp_tail(pre_act, w_edge_out[0]))
            enc_sum = jnp.sum(enc_edge.reshape(mesh_dev, grid_ratio, latent), axis=1, dtype=jnp.float32).astype(jnp.bfloat16)
            node_w = w_node_in[0]
            mesh_cur = residual(mesh_lat, mlp_tail(matmul_f32(mesh_lat, node_w[:latent]) + matmul_f32(enc_sum, node_w[latent:]), w_node_out[0]))
            grid_cur = residual(grid_lat, mlp_tail(matmul_f32(grid_lat, w_grid_self[0]), w_grid_self[1]))
            edge_lat = edge_base
            for layer_idx in range(1, blocks - 1):
                prev_tail = lax.ppermute(mesh_cur[mesh_dev - half_shard:], "gp", shift_pairs(1))
                next_head = lax.ppermute(mesh_cur[:half_shard], "gp", shift_pairs(-1))
                far_plus = lax.ppermute(mesh_cur, "gp", shift_pairs(-quarter_hop))
                far_minus = lax.ppermute(mesh_cur, "gp", shift_pairs(quarter_hop))
                w_layer = w_edge_in[layer_idx]
                extended = jnp.concatenate([prev_tail, mesh_cur, next_head, far_plus, far_minus], axis=0)
                send_proj = matmul_f32(extended, w_layer[latent:2 * latent])
                send_term = jnp.stack([
                    send_proj[half_shard + 1:half_shard + 1 + mesh_dev],
                    send_proj[half_shard - 1:half_shard - 1 + mesh_dev],
                    send_proj[2 * half_shard:2 * half_shard + mesh_dev],
                    send_proj[:mesh_dev],
                    send_proj[2 * mesh_dev:3 * mesh_dev],
                    send_proj[3 * mesh_dev:4 * mesh_dev]], axis=1)
                recv_term = matmul_f32(mesh_cur, w_layer[2 * latent:])
                pre_act = jnp.einsum("nkc,cd->nkd", edge_lat, w_layer[:latent], preferred_element_type=jnp.float32) + send_term + recv_term[:, None, :]
                edge_lat = residual(edge_lat, mlp_tail(pre_act, w_edge_out[layer_idx]))
                edge_sum = jnp.sum(edge_lat, axis=1, dtype=jnp.float32).astype(jnp.bfloat16)
                node_w = w_node_in[layer_idx]
                mesh_cur = residual(mesh_cur, mlp_tail(matmul_f32(mesh_cur, node_w[:latent]) + matmul_f32(edge_sum, node_w[latent:]), w_node_out[layer_idx]))
            head_next = lax.ppermute(mesh_cur[:half_shard], "gp", shift_pairs(-1))
            mesh_send = jnp.concatenate([mesh_cur[half_shard:], head_next], axis=0)
            w_last = w_edge_in[blocks - 1]
            send_term = matmul_f32(mesh_send, w_last[latent:2 * latent])
            pre_act = matmul_f32(m2g_lat, w_last[:latent]) + matmul_f32(grid_cur, w_last[2 * latent:])
            pre_act = (pre_act.reshape(mesh_dev, grid_ratio, latent) + send_term[:, None, :]).reshape(grid_dev, latent)
            dec_edge = residual(m2g_lat, mlp_tail(pre_act, w_edge_out[blocks - 1]))
            node_w = w_node_in[blocks - 1]
            grid_out = residual(grid_cur, mlp_tail(matmul_f32(grid_cur, node_w[:latent]) + matmul_f32(dec_edge, node_w[latent:]), w_node_out[blocks - 1]))
            hidden = jax.nn.silu(matmul_f32(grid_out, w_out_hidden)).astype(jnp.bfloat16)
            prediction = matmul_f32(hidden, w_out_final)
            state_next = state_cur + diff_std * prediction + diff_mean
            outputs.append(state_next)
            state_prev, state_cur = state_cur, state_next
        return outputs[0], outputs[1]

    in_specs = (row_spec, row_spec, edge_spec, row_spec, row_spec, row_spec, row_spec, edge_spec, whole) + (whole,) * 11
    return jax.shard_map(local_run, mesh=mesh, in_specs=in_specs, out_specs=(row_spec, row_spec), check_vma=False)
```

profile of v0, /device:TPU:0, one launch (start us, length us, event | category | flops | bytes accessed | tf_op | source)
XLA Modules:
  0.0 2311.1 jit_solution(17892920557318059099)
XLA Ops:
  99.3 23.6 %collective-permute-done.1 = bf16[256,512]{1,0:T(8,128)(2,1)S(1)} collective-permute-done((bf16[256,512]{1,0:T(8,128)(2,1)S(1)}, bf16[256,512]{1,0:T(8,128)(2,1)S(1)}, u32[]{:S(2)}, u32[]{:S(2)}) %collective-permute-start.1) | collective-permute-done | bytes 262176 | tf_op jit(solution)/shard_map/ppermute | solution.py:76
  154.7 20.5 collective-permute-done.5
  188.5 11.0 fusion.1442
  221.9 20.3 collective-permute-done.9
  255.6 11.0 fusion.1448
  288.4 21.6 collective-permute-done.13
  356.0 20.8 collective-permute-done.17
  390.2 11.4 fusion.1460
  423.2 19.8 collective-permute-done.21
  456.4 11.1 fusion.1466
  490.3 20.1 collective-permute-done.25
  523.8 11.3 fusion.1472
  556.9 20.0 collective-permute-done.29
  590.2 11.0 fusion.1478
  624.9 20.1 collective-permute-done.33
  691.1 20.9 collective-permute-done.37
  759.0 20.0 collective-permute-done.41
  792.4 11.3 fusion.1496
  825.9 21.2 collective-permute-done.45
  860.4 11.4 fusion.1502
  894.6 19.8 collective-permute-done.49
  927.8 11.0 fusion.1508
  961.3 20.2 collective-permute-done.53
  994.9 11.2 fusion.1514
  1029.9 20.6 collective-permute-done.57
  1063.8 11.1 fusion.1520
  1095.5 20.8 collective-permute-done.61
  1234.1 17.6 collective-permute-done.67
  1285.5 22.4 collective-permute-done.71
  1354.0 19.3 collective-permute-done.75
  1419.4 20.9 collective-permute-done.79
  1486.5 20.1 collective-permute-done.83
  1520.0 11.3 fusion.1574
  1552.9 20.2 collective-permute-done.87
  1586.5 11.1 fusion.1580
  1620.5 20.3 collective-permute-done.91
  1654.2 11.2 fusion.1586
  1686.9 20.0 collective-permute-done.95
  1754.6 20.3 collective-permute-done.99
  1820.8 19.9 collective-permute-done.103
  1888.4 20.5 collective-permute-done.107
  1922.3 11.2 fusion.1610
  1955.0 20.0 collective-permute-done.111
  1988.5 11.4 fusion.1616
  2022.5 20.3 collective-permute-done.115
  2088.9 21.1 collective-permute-done.119
  2156.1 20.5 collective-permute-done.123
  2221.5 20.0 collective-permute-done.127
  (1313 shorter events, 1474.2 us)
Async XLA Ops:
  9.8 59.6 %collective-permute-start = (bf16[512,512]{0,1:T(8,128)(2,1)}, bf16[512,512]{0,1:T(8,128)(2,1)}, u32[]{:S(2)}, u32[]{:S(2)}) collective-permute-start(bf16[512,512]{0,1:T(8,128)(2,1)} %get-tuple-element.64), channel_id=1, source_target_pairs={{0,1},{1,2},{2,3},{3,4},{4,5},{5,6},{6,7},{7,0}} | collective-permute-start | bytes 1572872 | tf_op jit(solution)/shard_map/ppermute | solution.py:63
  89.2 33.7 %collective-permute-start.3 = (bf16[512,512]{1,0:T(8,128)(2,1)S(1)}, bf16[512,512]{1,0:T(8,128)(2,1)S(1)}, u32[]{:S(2)}, u32[]{:S(2)}) collective-permute-start(bf16[512,512]{1,0:T(8,128)(2,1)S(1)} %fusion.115), channel_id=1, source_target_pairs={{0,6},{1,7},{2,0},{3,1},{4,2},{5,3},{6,4},{7,5}} | collective-permute-start | bytes 1572872 | tf_op jit(solution)/shard_map/ppermute | solution.py:78
  92.7 30.3 %collective-permute-start.4 = (bf16[512,512]{1,0:T(8,128)(2,1)S(1)}, bf16[512,512]{1,0:T(8,128)(2,1)S(1)}, u32[]{:S(2)}, u32[]{:S(2)}) collective-permute-start(bf16[512,512]{1,0:T(8,128)(2,1)S(1)} %fusion.115), channel_id=1, source_target_pairs={{0,2},{1,3},{2,4},{3,5},{4,6},{5,7},{6,0},{7,1}} | collective-permute-start | bytes 1572872 | tf_op jit(solution)/shard_map/ppermute | solution.py:79
  146.0 31.5 %collective-permute-start.7 = (bf16[512,512]{1,0:T(8,128)(2,1)S(1)}, bf16[512,512]{1,0:T(8,128)(2,1)S(1)}, u32[]{:S(2)}, u32[]{:S(2)}) collective-permute-start(bf16[512,512]{1,0:T(8,128)(2,1)S(1)} %add_convert_fusion.75), channel_id=1, source_target_pairs={{0,6},{1,7},{2,0},{3,1},{4,2},{5,3},{6,4},{7,5}} | collective-permute-start | bytes 1572872 | tf_op jit(solution)/shard_map/ppermute | solution.py:78
  147.5 30.8 %collective-permute-start.8 = (bf16[512,512]{1,0:T(8,128)(2,1)S(1)}, bf16[512,512]{1,0:T(8,128)(2,1)S(1)}, u32[]{:S(2)}, u32[]{:S(2)}) collective-permute-start(bf16[512,512]{1,0:T(8,128)(2,1)S(1)} %add_convert_fusion.75), channel_id=1, source_target_pairs={{0,2},{1,3},{2,4},{3,5},{4,6},{5,7},{6,0},{7,1}} | collective-permute-start | bytes 1572872 | tf_op jit(solution)/shard_map/ppermute | solution.py:79
  212.6 31.9 %collective-permute-start.11 = (bf16[512,512]{1,0:T(8,128)(2,1)S(1)}, bf16[512,512]{1,0:T(8,128)(2,1)S(1)}, u32[]{:S(2)}, u32[]{:S(2)}) collective-permute-start(bf16[512,512]{1,0:T(8,128)(2,1)S(1)} %add_convert_fusion.74), channel_id=1, source_target_pairs={{0,6},{1,7},{2,0},{3,1},{4,2},{5,3},{6,4},{7,5}} | collective-permute-start | bytes 1572872 | tf_op jit(solution)/shard_map/ppermute | solution.py:78
  279.5 32.8 %collective-permute-start.15 = (bf16[512,512]{1,0:T(8,128)(2,1)S(1)}, bf16[512,512]{1,0:T(8,128)(2,1)S(1)}, u32[]{:S(2)}, u32[]{:S(2)}) collective-permute-start(bf16[512,512]{1,0:T(8,128)(2,1)S(1)} %add_convert_fusion.73), channel_id=1, source_target_pairs={{0,6},{1,7},{2,0},{3,1},{4,2},{5,3},{6,4},{7,5}} | collective-permute-start | bytes 1572872 | tf_op jit(solution)/shard_map/ppermute | solution.py:78
  280.4 32.8 %collective-permute-start.16 = (bf16[512,512]{1,0:T(8,128)(2,1)S(1)}, bf16[512,512]{1,0:T(8,128)(2,1)S(1)}, u32[]{:S(2)}, u32[]{:S(2)}) collective-permute-start(bf16[512,512]{1,0:T(8,128)(2,1)S(1)} %add_convert_fusion.73), channel_id=1, source_target_pairs={{0,2},{1,3},{2,4},{3,5},{4,6},{5,7},{6,0},{7,1}} | collective-permute-start | bytes 1572872 | tf_op jit(solution)/shard_map/ppermute | solution.py:79
  347.3 31.8 %collective-permute-start.19 = (bf16[512,512]{1,0:T(8,128)(2,1)S(1)}, bf16[512,512]{1,0:T(8,128)(2,1)S(1)}, u32[]{:S(2)}, u32[]{:S(2)}) collective-permute-start(bf16[512,512]{1,0:T(8,128)(2,1)S(1)} %add_convert_fusion.72), channel_id=1, source_target_pairs={{0,6},{1,7},{2,0},{3,1},{4,2},{5,3},{6,4},{7,5}} | collective-permute-start | bytes 1572872 | tf_op jit(solution)/shard_map/ppermute | solution.py:78
  348.0 31.9 %collective-permute-start.20 = (bf16[512,512]{1,0:T(8,128)(2,1)S(1)}, bf16[512,512]{1,0:T(8,128)(2,1)S(1)}, u32[]{:S(2)}, u32[]{:S(2)}) collective-permute-start(bf16[512,512]{1,0:T(8,128)(2,1)S(1)} %add_convert_fusion.72), channel_id=1, source_target_pairs={{0,2},{1,3},{2,4},{3,5},{4,6},{5,7},{6,0},{7,1}} | collective-permute-start | bytes 1572872 | tf_op jit(solution)/shard_map/ppermute | solution.py:79
  414.6 30.8 %collective-permute-start.23 = (bf16[512,512]{1,0:T(8,128)(2,1)S(1)}, bf16[512,512]{1,0:T(8,128)(2,1)S(1)}, u32[]{:S(2)}, u32[]{:S(2)}) collective-permute-start(bf16[512,512]{1,0:T(8,128)(2,1)S(1)} %add_convert_fusion.71), channel_id=1, source_target_pairs={{0,6},{1,7},{2,0},{3,1},{4,2},{5,3},{6,4},{7,5}} | collective-permute-start | bytes 1572872 | tf_op jit(solution)/shard_map/ppermute | solution.py:78
  414.6 31.6 %collective-permute-start.24 = (bf16[512,512]{1,0:T(8,128)(2,1)S(1)}, bf16[512,512]{1,0:T(8,128)(2,1)S(1)}, u32[]{:S(2)}, u32[]{:S(2)}) collective-permute-start(bf16[512,512]{1,0:T(8,128)(2,1)S(1)} %add_convert_fusion.71), channel_id=1, source_target_pairs={{0,2},{1,3},{2,4},{3,5},{4,6},{5,7},{6,0},{7,1}} | collective-permute-start | bytes 1572872 | tf_op jit(solution)/shard_map/ppermute | solution.py:79
  480.4 32.3 %collective-permute-start.27 = (bf16[512,512]{1,0:T(8,128)(2,1)S(1)}, bf16[512,512]{1,0:T(8,128)(2,1)S(1)}, u32[]{:S(2)}, u32[]{:S(2)}) collective-permute-start(bf16[512,512]{1,0:T(8,128)(2,1)S(1)} %add_convert_fusion.70), channel_id=1, source_target_pairs={{0,6},{1,7},{2,0},{3,1},{4,2},{5,3},{6,4},{7,5}} | collective-permute-start | bytes 1572872 | tf_op jit(solution)/shard_map/ppermute | solution.py:78
  482.0 31.5 %collective-permute-start.28 = (bf16[512,512]{1,0:T(8,128)(2,1)S(1)}, bf16[512,512]{1,0:T(8,128)(2,1)S(1)}, u32[]{:S(2)}, u32[]{:S(2)}) collective-permute-start(bf16[512,512]{1,0:T(8,128)(2,1)S(1)} %add_convert_fusion.70), channel_id=1, source_target_pairs={{0,2},{1,3},{2,4},{3,5},{4,6},{5,7},{6,0},{7,1}} | collective-permute-start | bytes 1572872 | tf_op jit(solution)/shard_map/ppermute | solution.py:79
  548.0 31.2 %collective-permute-start.31 = (bf16[512,512]{1,0:T(8,128)(2,1)S(1)}, bf16[512,512]{1,0:T(8,128)(2,1)S(1)}, u32[]{:S(2)}, u32[]{:S(2)}) collective-permute-start(bf16[512,512]{1,0:T(8,128)(2,1)S(1)} %add_convert_fusion.69), channel_id=1, source_target_pairs={{0,6},{1,7},{2,0},{3,1},{4,2},{5,3},{6,4},{7,5}} | collective-permute-start | bytes 1572872 | tf_op jit(solution)/shard_map/ppermute | solution.py:78
  549.0 31.0 %collective-permute-start.32 = (bf16[512,512]{1,0:T(8,128)(2,1)S(1)}, bf16[512,512]{1,0:T(8,128)(2,1)S(1)}, u32[]{:S(2)}, u32[]{:S(2)}) collective-permute-start(bf16[512,512]{1,0:T(8,128)(2,1)S(1)} %add_convert_fusion.69), channel_id=1, source_target_pairs={{0,2},{1,3},{2,4},{3,5},{4,6},{5,7},{6,0},{7,1}} | collective-permute-start | bytes 1572872 | tf_op jit(solution)/shard_map/ppermute | solution.py:79
  614.6 32.8 %collective-permute-start.35 = (bf16[512,512]{1,0:T(8,128)(2,1)S(1)}, bf16[512,512]{1,0:T(8,128)(2,1)S(1)}, u32[]{:S(2)}, u32[]{:S(2)}) collective-permute-start(bf16[512,512]{1,0:T(8,128)(2,1)S(1)} %add_convert_fusion.68), channel_id=1, source_target_pairs={{0,6},{1,7},{2,0},{3,1},{4,2},{5,3},{6,4},{7,5}} | collective-permute-start | bytes 1572872 | tf_op jit(solution)/shard_map/ppermute | solution.py:78
  617.5 30.7 %collective-permute-start.36 = (bf16[512,512]{1,0:T(8,128)(2,1)S(1)}, bf16[512,512]{1,0:T(8,128)(2,1)S(1)}, u32[]{:S(2)}, u32[]{:S(2)}) collective-permute-start(bf16[512,512]{1,0:T(8,128)(2,1)S(1)} %add_convert_fusion.68), channel_id=1, source_target_pairs={{0,2},{1,3},{2,4},{3,5},{4,6},{5,7},{6,0},{7,1}} | collective-permute-start | bytes 1572872 | tf_op jit(solution)/shard_map/ppermute | solution.py:79
  682.4 31.9 %collective-permute-start.39 = (bf16[512,512]{1,0:T(8,128)(2,1)S(1)}, bf16[512,512]{1,0:T(8,128)(2,1)S(1)}, u32[]{:S(2)}, u32[]{:S(2)}) collective-permute-start(bf16[512,512]{1,0:T(8,128)(2,1)S(1)} %add_convert_fusion.67), channel_id=1, source_target_pairs={{0,6},{1,7},{2,0},{3,1},{4,2},{5,3},{6,4},{7,5}} | collective-permute-start | bytes 1572872 | tf_op jit(solution)/shard_map/ppermute | solution.py:78
  684.1 31.0 %collective-permute-start.40 = (bf16[512,512]{1,0:T(8,128)(2,1)S(1)}, bf16[512,512]{1,0:T(8,128)(2,1)S(1)}, u32[]{:S(2)}, u32[]{:S(2)}) collective-permute-start(bf16[512,512]{1,0:T(8,128)(2,1)S(1)} %add_convert_fusion.67), channel_id=1, source_target_pairs={{0,2},{1,3},{2,4},{3,5},{4,6},{5,7},{6,0},{7,1}} | collective-permute-start | bytes 1572872 | tf_op jit(solution)/shard_map/ppermute | solution.py:79
  749.4 31.9 %collective-permute-start.43 = (bf16[512,512]{1,0:T(8,128)(2,1)S(1)}, bf16[512,512]{1,0:T(8,128)(2,1)S(1)}, u32[]{:S(2)}, u32[]{:S(2)}) collective-permute-start(bf16[512,512]{1,0:T(8,128)(2,1)S(1)} %add_convert_fusion.66), channel_id=1, source_target_pairs={{0,6},{1,7},{2,0},{3,1},{4,2},{5,3},{6,4},{7,5}} | collective-permute-start | bytes 1572872 | tf_op jit(solution)/shard_map/ppermute | solution.py:78
  816.6 32.7 %collective-permute-start.47 = (bf16[512,512]{1,0:T(8,128)(2,1)S(1)}, bf16[512,512]{1,0:T(8,128)(2,1)S(1)}, u32[]{:S(2)}, u32[]{:S(2)}) collective-permute-start(bf16[512,512]{1,0:T(8,128)(2,1)S(1)} %add_convert_fusion.65), channel_id=1, source_target_pairs={{0,6},{1,7},{2,0},{3,1},{4,2},{5,3},{6,4},{7,5}} | collective-permute-start | bytes 1572872 | tf_op jit(solution)/shard_map/ppermute | solution.py:78
  819.3 30.9 %collective-permute-start.48 = (bf16[512,512]{1,0:T(8,128)(2,1)S(1)}, bf16[512,512]{1,0:T(8,128)(2,1)S(1)}, u32[]{:S(2)}, u32[]{:S(2)}) collective-permute-start(bf16[512,512]{1,0:T(8,128)(2,1)S(1)} %add_convert_fusion.65), channel_id=1, source_target_pairs={{0,2},{1,3},{2,4},{3,5},{4,6},{5,7},{6,0},{7,1}} | collective-permute-start | bytes 1572872 | tf_op jit(solution)/shard_map/ppermute | solution.py:79
  884.8 32.0 %collective-permute-start.51 = (bf16[512,512]{1,0:T(8,128)(2,1)S(1)}, bf16[512,512]{1,0:T(8,128)(2,1)S(1)}, u32[]{:S(2)}, u32[]{:S(2)}) collective-permute-start(bf16[512,512]{1,0:T(8,128)(2,1)S(1)} %add_convert_fusion.64), channel_id=1, source_target_pairs={{0,6},{1,7},{2,0},{3,1},{4,2},{5,3},{6,4},{7,5}} | collective-permute-start | bytes 1572872 | tf_op jit(solution)/shard_map/ppermute | solution.py:78
  951.9 31.9 %collective-permute-start.55 = (bf16[512,512]{1,0:T(8,128)(2,1)S(1)}, bf16[512,512]{1,0:T(8,128)(2,1)S(1)}, u32[]{:S(2)}, u32[]{:S(2)}) collective-permute-start(bf16[512,512]{1,0:T(8,128)(2,1)S(1)} %add_convert_fusion.63), channel_id=1, source_target_pairs={{0,6},{1,7},{2,0},{3,1},{4,2},{5,3},{6,4},{7,5}} | collective-permute-start | bytes 1572872 | tf_op jit(solution)/shard_map/ppermute | solution.py:78
  1019.2 33.6 %collective-permute-start.59 = (bf16[512,512]{1,0:T(8,128)(2,1)S(1)}, bf16[512,512]{1,0:T(8,128)(2,1)S(1)}, u32[]{:S(2)}, u32[]{:S(2)}) collective-permute-start(bf16[512,512]{1,0:T(8,128)(2,1)S(1)} %add_convert_fusion.62), channel_id=1, source_target_pairs={{0,6},{1,7},{2,0},{3,1},{4,2},{5,3},{6,4},{7,5}} | collective-permute-start | bytes 1572872 | tf_op jit(solution)/shard_map/ppermute | solution.py:78
  1087.8 30.8 %collective-permute-start.63 = (bf16[512,512]{1,0:T(8,128)(2,1)S(1)}, bf16[512,512]{1,0:T(8,128)(2,1)S(1)}, u32[]{:S(2)}, u32[]{:S(2)}) collective-permute-start(bf16[512,512]{1,0:T(8,128)(2,1)S(1)} %add_convert_fusion.61), channel_id=1, source_target_pairs={{0,6},{1,7},{2,0},{3,1},{4,2},{5,3},{6,4},{7,5}} | collective-permute-start | bytes 1572872 | tf_op jit(solution)/shard_map/ppermute | solution.py:78
  1276.3 33.9 %collective-permute-start.73 = (bf16[512,512]{1,0:T(8,128)(2,1)S(1)}, bf16[512,512]{1,0:T(8,128)(2,1)S(1)}, u32[]{:S(2)}, u32[]{:S(2)}) collective-permute-start(bf16[512,512]{1,0:T(8,128)(2,1)S(1)} %add_convert_fusion.59), channel_id=1, source_target_pairs={{0,6},{1,7},{2,0},{3,1},{4,2},{5,3},{6,4},{7,5}} | collective-permute-start | bytes 1572872 | tf_op jit(solution)/shard_map/ppermute | solution.py:78
  1277.5 33.6 %collective-permute-start.74 = (bf16[512,512]{1,0:T(8,128)(2,1)S(1)}, bf16[512,512]{1,0:T(8,128)(2,1)S(1)}, u32[]{:S(2)}, u32[]{:S(2)}) collective-permute-start(bf16[512,512]{1,0:T(8,128)(2,1)S(1)} %add_convert_fusion.59), channel_id=1, source_target_pairs={{0,2},{1,3},{2,4},{3,5},{4,6},{5,7},{6,0},{7,1}} | collective-permute-start | bytes 1572872 | tf_op jit(solution)/shard_map/ppermute | solution.py:79
  1410.5 32.1 %collective-permute-start.81 = (bf16[512,512]{1,0:T(8,128)(2,1)S(1)}, bf16[512,512]{1,0:T(8,128)(2,1)S(1)}, u32[]{:S(2)}, u32[]{:S(2)}) collective-permute-start(bf16[512,512]{1,0:T(8,128)(2,1)S(1)} %add_convert_fusion.57), channel_id=1, source_target_pairs={{0,6},{1,7},{2,0},{3,1},{4,2},{5,3},{6,4},{7,5}} | collective-permute-start | bytes 1572872 | tf_op jit(solution)/shard_map/ppermute | solution.py:78
  1410.5 32.9 %collective-permute-start.82 = (bf16[512,512]{1,0:T(8,128)(2,1)S(1)}, bf16[512,512]{1,0:T(8,128)(2,1)S(1)}, u32[]{:S(2)}, u32[]{:S(2)}) collective-permute-start(bf16[512,512]{1,0:T(8,128)(2,1)S(1)} %add_convert_fusion.57), channel_id=1, source_target_pairs={{0,2},{1,3},{2,4},{3,5},{4,6},{5,7},{6,0},{7,1}} | collective-permute-start | bytes 1572872 | tf_op jit(solution)/shard_map/ppermute | solution.py:79
  1477.5 31.4 %collective-permute-start.85 = (bf16[512,512]{1,0:T(8,128)(2,1)S(1)}, bf16[512,512]{1,0:T(8,128)(2,1)S(1)}, u32[]{:S(2)}, u32[]{:S(2)}) collective-permute-start(bf16[512,512]{1,0:T(8,128)(2,1)S(1)} %add_convert_fusion.56), channel_id=1, source_target_pairs={{0,6},{1,7},{2,0},{3,1},{4,2},{5,3},{6,4},{7,5}} | collective-permute-start | bytes 1572872 | tf_op jit(solution)/shard_map/ppermute | solution.py:78
  1544.2 31.2 %collective-permute-start.89 = (bf16[512,512]{1,0:T(8,128)(2,1)S(1)}, bf16[512,512]{1,0:T(8,128)(2,1)S(1)}, u32[]{:S(2)}, u32[]{:S(2)}) collective-permute-start(bf16[512,512]{1,0:T(8,128)(2,1)S(1)} %add_convert_fusion.55), channel_id=1, source_target_pairs={{0,6},{1,7},{2,0},{3,1},{4,2},{5,3},{6,4},{7,5}} | collective-permute-start | bytes 1572872 | tf_op jit(solution)/shard_map/ppermute | solution.py:78
  1544.2 32.0 %collective-permute-start.90 = (bf16[512,512]{1,0:T(8,128)(2,1)S(1)}, bf16[512,512]{1,0:T(8,128)(2,1)S(1)}, u32[]{:S(2)}, u32[]{:S(2)}) collective-permute-start(bf16[512,512]{1,0:T(8,128)(2,1)S(1)} %add_convert_fusion.55), channel_id=1, source_target_pairs={{0,2},{1,3},{2,4},{3,5},{4,6},{5,7},{6,0},{7,1}} | collective-permute-start | bytes 1572872 | tf_op jit(solution)/shard_map/ppermute | solution.py:79
  1610.5 32.6 %collective-permute-start.93 = (bf16[512,512]{1,0:T(8,128)(2,1)S(1)}, bf16[512,512]{1,0:T(8,128)(2,1)S(1)}, u32[]{:S(2)}, u32[]{:S(2)}) collective-permute-start(bf16[512,512]{1,0:T(8,128)(2,1)S(1)} %add_convert_fusion.54), channel_id=1, source_target_pairs={{0,6},{1,7},{2,0},{3,1},{4,2},{5,3},{6,4},{7,5}} | collective-permute-start | bytes 1572872 | tf_op jit(solution)/shard_map/ppermute | solution.py:78
  1678.2 30.9 %collective-permute-start.97 = (bf16[512,512]{1,0:T(8,128)(2,1)S(1)}, bf16[512,512]{1,0:T(8,128)(2,1)S(1)}, u32[]{:S(2)}, u32[]{:S(2)}) collective-permute-start(bf16[512,512]{1,0:T(8,128)(2,1)S(1)} %add_convert_fusion.53), channel_id=1, source_target_pairs={{0,6},{1,7},{2,0},{3,1},{4,2},{5,3},{6,4},{7,5}} | collective-permute-start | bytes 1572872 | tf_op jit(solution)/shard_map/ppermute | solution.py:78
  1678.3 31.7 %collective-permute-start.98 = (bf16[512,512]{1,0:T(8,128)(2,1)S(1)}, bf16[512,512]{1,0:T(8,128)(2,1)S(1)}, u32[]{:S(2)}, u32[]{:S(2)}) collective-permute-start(bf16[512,512]{1,0:T(8,128)(2,1)S(1)} %add_convert_fusion.53), channel_id=1, source_target_pairs={{0,2},{1,3},{2,4},{3,5},{4,6},{5,7},{6,0},{7,1}} | collective-permute-start | bytes 1572872 | tf_op jit(solution)/shard_map/ppermute | solution.py:79
  1744.5 32.7 %collective-permute-start.101 = (bf16[512,512]{1,0:T(8,128)(2,1)S(1)}, bf16[512,512]{1,0:T(8,128)(2,1)S(1)}, u32[]{:S(2)}, u32[]{:S(2)}) collective-permute-start(bf16[512,512]{1,0:T(8,128)(2,1)S(1)} %add_convert_fusion.52), channel_id=1, source_target_pairs={{0,6},{1,7},{2,0},{3,1},{4,2},{5,3},{6,4},{7,5}} | collective-permute-start | bytes 1572872 | tf_op jit(solution)/shard_map/ppermute | solution.py:78
  1812.1 30.9 %collective-permute-start.105 = (bf16[512,512]{1,0:T(8,128)(2,1)S(1)}, bf16[512,512]{1,0:T(8,128)(2,1)S(1)}, u32[]{:S(2)}, u32[]{:S(2)}) collective-permute-start(bf16[512,512]{1,0:T(8,128)(2,1)S(1)} %add_convert_fusion.51), channel_id=1, source_target_pairs={{0,6},{1,7},{2,0},{3,1},{4,2},{5,3},{6,4},{7,5}} | collective-permute-start | bytes 1572872 | tf_op jit(solution)/shard_map/ppermute | solution.py:78
  1812.1 31.7 %collective-permute-start.106 = (bf16[512,512]{1,0:T(8,128)(2,1)S(1)}, bf16[512,512]{1,0:T(8,128)(2,1)S(1)}, u32[]{:S(2)}, u32[]{:S(2)}) collective-permute-start(bf16[512,512]{1,0:T(8,128)(2,1)S(1)} %add_convert_fusion.51), channel_id=1, source_target_pairs={{0,2},{1,3},{2,4},{3,5},{4,6},{5,7},{6,0},{7,1}} | collective-permute-start | bytes 1572872 | tf_op jit(solution)/shard_map/ppermute | solution.py:79
  1878.1 33.1 %collective-permute-start.109 = (bf16[512,512]{1,0:T(8,128)(2,1)S(1)}, bf16[512,512]{1,0:T(8,128)(2,1)S(1)}, u32[]{:S(2)}, u32[]{:S(2)}) collective-permute-start(bf16[512,512]{1,0:T(8,128)(2,1)S(1)} %add_convert_fusion.50), channel_id=1, source_target_pairs={{0,6},{1,7},{2,0},{3,1},{4,2},{5,3},{6,4},{7,5}} | collective-permute-start | bytes 1572872 | tf_op jit(solution)/shard_map/ppermute | solution.py:78
  1946.4 31.0 %collective-permute-start.113 = (bf16[512,512]{1,0:T(8,128)(2,1)S(1)}, bf16[512,512]{1,0:T(8,128)(2,1)S(1)}, u32[]{:S(2)}, u32[]{:S(2)}) collective-permute-start(bf16[512,512]{1,0:T(8,128)(2,1)S(1)} %add_convert_fusion.49), channel_id=1, source_target_pairs={{0,6},{1,7},{2,0},{3,1},{4,2},{5,3},{6,4},{7,5}} | collective-permute-start | bytes 1572872 | tf_op jit(solution)/shard_map/ppermute | solution.py:78
  1946.8 31.4 %collective-permute-start.114 = (bf16[512,512]{1,0:T(8,128)(2,1)S(1)}, bf16[512,512]{1,0:T(8,128)(2,1)S(1)}, u32[]{:S(2)}, u32[]{:S(2)}) collective-permute-start(bf16[512,512]{1,0:T(8,128)(2,1)S(1)} %add_convert_fusion.49), channel_id=1, source_target_pairs={{0,2},{1,3},{2,4},{3,5},{4,6},{5,7},{6,0},{7,1}} | collective-permute-start | bytes 1572872 | tf_op jit(solution)/shard_map/ppermute | solution.py:79
  2012.7 32.4 %collective-permute-start.117 = (bf16[512,512]{1,0:T(8,128)(2,1)S(1)}, bf16[512,512]{1,0:T(8,128)(2,1)S(1)}, u32[]{:S(2)}, u32[]{:S(2)}) collective-permute-start(bf16[512,512]{1,0:T(8,128)(2,1)S(1)} %add_convert_fusion.48), channel_id=1, source_target_pairs={{0,6},{1,7},{2,0},{3,1},{4,2},{5,3},{6,4},{7,5}} | collective-permute-start | bytes 1572872 | tf_op jit(solution)/shard_map/ppermute | solution.py:78
  2080.2 32.0 %collective-permute-start.121 = (bf16[512,512]{1,0:T(8,128)(2,1)S(1)}, bf16[512,512]{1,0:T(8,128)(2,1)S(1)}, u32[]{:S(2)}, u32[]{:S(2)}) collective-permute-start(bf16[512,512]{1,0:T(8,128)(2,1)S(1)} %add_convert_fusion.47), channel_id=1, source_target_pairs={{0,6},{1,7},{2,0},{3,1},{4,2},{5,3},{6,4},{7,5}} | collective-permute-start | bytes 1572872 | tf_op jit(solution)/shard_map/ppermute | solution.py:78
  2080.2 32.9 %collective-permute-start.122 = (bf16[512,512]{1,0:T(8,128)(2,1)S(1)}, bf16[512,512]{1,0:T(8,128)(2,1)S(1)}, u32[]{:S(2)}, u32[]{:S(2)}) collective-permute-start(bf16[512,512]{1,0:T(8,128)(2,1)S(1)} %add_convert_fusion.47), channel_id=1, source_target_pairs={{0,2},{1,3},{2,4},{3,5},{4,6},{5,7},{6,0},{7,1}} | collective-permute-start | bytes 1572872 | tf_op jit(solution)/shard_map/ppermute | solution.py:79
  2147.4 31.4 %collective-permute-start.125 = (bf16[512,512]{1,0:T(8,128)(2,1)S(1)}, bf16[512,512]{1,0:T(8,128)(2,1)S(1)}, u32[]{:S(2)}, u32[]{:S(2)}) collective-permute-start(bf16[512,512]{1,0:T(8,128)(2,1)S(1)} %add_convert_fusion.46), channel_id=1, source_target_pairs={{0,6},{1,7},{2,0},{3,1},{4,2},{5,3},{6,4},{7,5}} | collective-permute-start | bytes 1572872 | tf_op jit(solution)/shard_map/ppermute | solution.py:78
  2148.6 31.1 %collective-permute-start.126 = (bf16[512,512]{1,0:T(8,128)(2,1)S(1)}, bf16[512,512]{1,0:T(8,128)(2,1)S(1)}, u32[]{:S(2)}, u32[]{:S(2)}) collective-permute-start(bf16[512,512]{1,0:T(8,128)(2,1)S(1)} %add_convert_fusion.46), channel_id=1, source_target_pairs={{0,2},{1,3},{2,4},{3,5},{4,6},{5,7},{6,0},{7,1}} | collective-permute-start | bytes 1572872 | tf_op jit(solution)/shard_map/ppermute | solution.py:79
  (178 other events, 4333.9 us)
where the time goes:
time: 2320 us; the launch traced here: 2310 us
  matrix products  748 us (32%)
  waiting for transfers between devices  661 us (28%)
  other arithmetic  366 us (16%)
  local copies, waits for them, and re-layouts  357 us (15%)
  starting transfers between devices  174 us (8%)
    dot_general x186, matrix products, matmul_f32(): return jnp.dot(values, weight, preferred_element_type=jnp.float32)  740 us
    ppermute x32, waiting for transfers between devices, local_run(): lax.ppermute(mesh_cur[mesh_dev - half_shard:], 'gp', shift_pairs(1))  654 us
    unnamed x477, local copies, waits for them, and re-layouts  275 us
    reduce_sum x32, other arithmetic, local_run(): edge_sum = jnp.sum(edge_lat, axis=1, dtype=jnp.float32).astype(jnp.bfloat16)  186 us
    reduce_sum x80, other arithmetic, layer_norm(): spread = jnp.mean(centred * centred, axis=-1, keepdims=True)  146 us
    ppermute x32, starting transfers between devices, local_run(): next_head = lax.ppermute(mesh_cur[:half_shard], 'gp', shift_pairs(-1))  83.3 us
    ppermute x32, starting transfers between devices, local_run(): far_plus = lax.ppermute(mesh_cur, 'gp', shift_pairs(-quarter_hop))  55.3 us
  transfers between devices with their start and end apart: 132, of which 36 were waited for; matrix products, arithmetic and copies ran while one was open for 12% of the time, Pallas kernels for 0%

commit v1 on v0

v1 whole, which is shorter than its diff:
```python
import functools

import jax
import jax.numpy as jnp
from jax import lax
from jax.experimental import pallas as pl
from jax.experimental.pallas import tpu as pltpu
from jax.sharding import PartitionSpec as P

F32 = jnp.float32
BF16 = jnp.bfloat16

RUNS = 16
RUN = 32
ROWS = RUNS * RUN
LAT = 512
VARS = 84
PAD = 48
TILE = 256
TILES = ROWS // TILE
CH = 32
RING = 8
LAYERS = 16
BLOCKS = LAYERS + 2
FAR = ((2, 1), (3, -1), (4, 4), (5, -4))
NEAR = ((0, 1), (1, -1))


def dot(a, b):
    return jnp.dot(a, b, preferred_element_type=F32)


def silu(pre):
    return pre * jax.nn.sigmoid(pre)


def norm(y):
    centred = y - jnp.mean(y, axis=-1, keepdims=True)
    return centred * lax.rsqrt(jnp.mean(centred * centred, axis=-1, keepdims=True) + 1e-5)


def ring_place(dev):
    high = lax.div(dev, 4)
    return high * (4 + lax.rem(dev + 2, 4)) + (1 - high) * dev


def chunks():
    return range(0, TILE, CH)


def get_tiles(ref, rows):
    return jnp.concatenate([ref[j, rows, :] for j in range(ref.shape[0])], axis=1)


def set_tiles(ref, rows, value):
    for j in range(ref.shape[0]):
        ref[j, rows, :] = value[:, 128 * j:128 * j + 128]


def kernel(g_in, mf_in, xc_in, stats, wemb, w_embed_out, w_edge_in, w_edge_out, w_node_in, w_node_out, w_grid_self,
           w_out_hidden, w_out_final, out0, out1,
           g_buf, mf_buf, xc_buf, x_buf, gf, feat, we, weo, wei, wedo, wni, wno, wself, woh, wof,
           edge_base, edge, h_mesh, h, hf, g2m, m2g, v, vc, proj, recv, acc, hid, hid2, esum, dec,
           send_buf, halo_buf,
           in_send, in_recv, w_sem, big_sem, halo_send, halo_recv, out_send, out_recv):
    me = lax.axis_index("gp")
    place = ring_place(me)

    def at(dev):
        return {"gp": dev}

    mesh_id = pl.DeviceIdType.MESH

    def block_copies(block, slot):
        return [
            pltpu.make_async_copy(w_edge_in.at[block], wei.at[slot], big_sem.at[slot, 0]),
            pltpu.make_async_copy(w_edge_out.at[block], wedo.at[slot], big_sem.at[slot, 1]),
            pltpu.make_async_copy(w_node_in.at[block], wni.at[slot], big_sem.at[slot, 2]),
            pltpu.make_async_copy(w_node_out.at[block], wno.at[slot], big_sem.at[slot, 3]),
        ]

    small = [
        pltpu.make_async_copy(wemb, we, w_sem.at[0]),
        pltpu.make_async_copy(w_embed_out, weo, w_sem.at[1]),
        pltpu.make_async_copy(w_grid_self, wself, w_sem.at[2]),
        pltpu.make_async_copy(w_out_hidden, woh, w_sem.at[3]),
        pltpu.make_async_copy(w_out_final, wof, w_sem.at[4]),
    ]
    for copy in small:
        copy.start()
    for copy in block_copies(0, 0):
        copy.start()

    barrier = pltpu.get_barrier_semaphore()
    for hop in range(1, RING):
        pl.semaphore_signal(barrier, inc=1, device_id=at(lax.rem(me + hop, RING)), device_id_type=mesh_id)
    pl.semaphore_wait(barrier, RING - 1)

    parts = ((mf_in, mf_buf), (g_in, g_buf), (xc_in, xc_buf))

    def in_copy(part, hop):
        src, dst = parts[part]
        target = lax.rem(me + hop, RING)
        src = src.at[:, ring_place(target)]
        dst = dst.at[pl.ds(2 * me, 2)]
        if hop == 0:
            return pltpu.make_async_copy(src, dst, in_recv.at[part, 0])
        return pltpu.make_async_remote_copy(src_ref=src, dst_ref=dst, send_sem=in_send.at[part, hop],
                                            recv_sem=in_recv.at[part, hop], device_id=at(target),
                                            device_id_type=mesh_id)

    in_copies = [[in_copy(part, hop) for hop in range(RING)] for part in range(3)]
    for part in range(3):
        for copy in in_copies[part]:
            copy.start()

    def wait_in(part):
        in_copies[part][0].wait()
        for hop in range(1, RING):
            in_copies[part][hop].wait_recv()

    def pipeline(items):
        depth = max(len(item) for item in items)
        for beat in range(len(items) + depth - 1):
            for stage in range(depth):
                index = beat - stage
                if 0 <= index < len(items) and stage < len(items[index]):
                    items[index][stage](index)

    def embed_item(load, w_first, second, store):
        def first(i):
            pre = dot(load(), we[w_first])
            for c in chunks():
                hid[i % 2, pl.ds(c, CH), :] = silu(pre[c:c + CH]).astype(BF16)

        def last(i):
            y = dot(hid[i % 2], weo[second])
            for c in chunks():
                store(c, norm(y[c:c + CH]).astype(BF16))

        return [first, last]

    def mesh_features(t):
        runs = range(t * TILE // RUN, (t + 1) * TILE // RUN)
        return jnp.concatenate([mf_buf[(q + 1) % RUNS] for q in runs], axis=0)

    wait_in(0)
    for copy in small[:2]:
        copy.wait()
    items = []
    for t in range(TILES):
        def store_mesh(c, value, t=t):
            h_mesh[pl.ds(t * TILE + c, CH), :] = value
        items.append(embed_item(lambda t=t: mesh_features(t), 0, 1, store_mesh))
        for p in range(2):
            def store_g2m(c, value, t=t, p=p):
                g2m[p, pl.ds(t * TILE + c, CH), :] = value
            items.append(embed_item(lambda t=t: mesh_features(t), 1 + p, 2, store_g2m))
        for k in range(6):
            def store_edge(c, value, t=t, k=k):
                edge_base[k, pl.ds(t * TILE + c, CH), :] = value
            items.append(embed_item(lambda t=t: mesh_features(t), 3 + k, 4, store_edge))
    pipeline(items)

    wait_in(1)
    for q in range(RUNS):
        set_tiles(gf, pl.ds(q * 2 * RUN, 2 * RUN), g_buf[q].astype(F32))
    for q in range(RUNS):
        for p in range(2):
            feat[p, pl.ds(q * RUN, RUN), :] = get_tiles(gf, pl.ds(q * 2 * RUN + p, RUN, stride=2)).astype(BF16)
    items = []
    for t in range(TILES):
        for p in range(2):
            def store_m2g(c, value, t=t, p=p):
                m2g[p, pl.ds(t * TILE + c, CH), :] = value
            items.append(embed_item(lambda t=t, p=p: feat[p, pl.ds(t * TILE, TILE), pl.ds(0, 128)], 9, 3, store_m2g))
    pipeline(items)
    for copy in small[2:]:
        copy.wait()

    left = ring_place(lax.rem(place + RING - 1, RING))
    right = ring_place(lax.rem(place + 1, RING))

    def halo_copies(slot):
        return [
            pltpu.make_async_remote_copy(src_ref=send_buf.at[side], dst_ref=halo_buf.at[slot, side],
                                         send_sem=halo_send.at[side], recv_sem=halo_recv.at[slot, side],
                                         device_id=at(target), device_id_type=mesh_id)
            for side, target in ((0, left), (1, right))
        ]

    def send_halo(slot):
        first = get_tiles(hf, pl.ds(0, RUNS, stride=RUN))
        final = get_tiles(hf, pl.ds(RUN - 1, RUNS, stride=RUN))
        first_on = jnp.concatenate([first[1:], first[:1]], axis=0)
        final_back = jnp.concatenate([final[-1:], final[:-1]], axis=0)
        send_buf[0] = jnp.where(place == 0, first_on, first).astype(BF16)
        send_buf[1] = jnp.where(place == RING - 1, final_back, final).astype(BF16)
        for copy in halo_copies(slot):
            copy.start()

    def node_item(t, base, slot, sums):
        rows = pl.ds(t * TILE, TILE)

        def first(i):
            pre = dot(base[rows, :], wni[slot, pl.ds(0, LAT), :]) + dot(sums[rows, :], wni[slot, pl.ds(LAT, LAT), :])
            for c in chunks():
                hid2[t, pl.ds(c, CH), :] = silu(pre[c:c + CH]).astype(BF16)

        def last(i):
            y = dot(hid2[t], wno[slot])
            for c in chunks():
                part = pl.ds(t * TILE + c, CH)
                value = (base[part, :].astype(F32) + norm(y[c:c + CH])).astype(BF16)
                h[part, :] = value
                set_tiles(hf, part, value.astype(F32))

        return [first, last]

    def proj_rows(q, offset):
        return get_tiles(proj, pl.ds(q * PAD + 8 + offset, RUN))

    def layer(block, slot, halo_slot, more):
        w_edge = wei.at[slot]
        for t in range(TILES):
            out = dot(h[pl.ds(t * TILE, TILE), :], w_edge[pl.ds(LAT, LAT), :])
            for c in range(0, TILE, RUN):
                set_tiles(proj, pl.ds((t * TILE + c) // RUN * PAD + 8, RUN), out[c:c + RUN])
            recv[pl.ds(t * TILE, TILE), :] = dot(h[pl.ds(t * TILE, TILE), :], w_edge[pl.ds(2 * LAT, LAT), :])

        def edge_item(t, k, run_shift, offset, first_one, final_one):
            def first(i):
                pre = dot(edge[k, pl.ds(t * TILE, TILE), :], w_edge[pl.ds(0, LAT), :])
                for c in chunks():
                    q = (t * TILE + c) // RUN
                    sender = proj_rows((q + run_shift) % RUNS, offset)
                    value = pre[c:c + CH] + (sender + recv[pl.ds(t * TILE + c, CH), :])
                    hid[i % 2, pl.ds(c, CH), :] = silu(value).astype(BF16)

            def last(i):
                y = dot(hid[i % 2], wedo[slot])
                for c in chunks():
                    part = pl.ds(t * TILE + c, CH)
                    value = (edge[k, part, :].astype(F32) + norm(y[c:c + CH])).astype(BF16)
                    edge[k, part, :] = value
                    total = value.astype(F32)
                    if not first_one:
                        total = total + acc[part, :]
                    if final_one:
                        esum[part, :] = total.astype(BF16)
                    else:
                        acc[part, :] = total

            return [first, last]

        def halo(i):
            for side, copy in enumerate(halo_copies(halo_slot)):
                copy.wait()
            rows = jnp.concatenate([halo_buf[halo_slot, 0], halo_buf[halo_slot, 1]], axis=0)
            out = dot(rows, w_edge[pl.ds(LAT, LAT), :])
            set_tiles(proj, pl.ds(8 + RUN, RUNS, stride=PAD), out[:RUNS])
            set_tiles(proj, pl.ds(7, RUNS, stride=PAD), out[RUNS:])

        far = [edge_item(t, k, s, 0, n == 0, False) for t in range(TILES) for n, (k, s) in enumerate(FAR)]
        near = [edge_item(t, k, 0, s, False, n == 1) for t in range(TILES) for n, (k, s) in enumerate(NEAR)]
        node = [node_item(t, h, slot, esum) for t in range(TILES)]
        edges = far + near
        for n, item in enumerate(edges):
            if n == len(far):
                halo(n)
            item[0](n)
            if n:
                edges[n - 1][1](n - 1)
            if n > len(far) and (n - len(far)) % 2 == 0:
                node[(n - len(far)) // 2 - 1][0](n)
            if n > len(far) + 1 and (n - len(far)) % 2 == 1:
                node[(n - len(far) - 1) // 2 - 1][1](n)
        edges[-1][1](len(edges) - 1)
        node[-1][0](0)
        node[-1][1](0)

        @pl.when(more)
        def _():
            send_halo(1 - halo_slot)

    def encoder(step, slot):
        w_edge = wei.at[slot]
        for k in range(6):
            for c in range(0, ROWS, 128):
                edge[k, pl.ds(c, 128), :] = edge_base[k, pl.ds(c, 128), :]
        for t in range(TILES):
            recv[pl.ds(t * TILE, TILE), :] = dot(h_mesh[pl.ds(t * TILE, TILE), :], w_edge[pl.ds(2 * LAT, LAT), :])
        items = []
        for t in range(TILES):
            for p in range(2):
                rows = pl.ds(t * TILE, TILE)

                def in_first(i, rows=rows, p=p):
                    pre = dot(feat[p, rows, :], we[pl.ds(10 + 2 * step, 2)].reshape(256, LAT))
                    for c in chunks():
                        hid[i % 2, pl.ds(c, CH), :] = silu(pre[c:c + CH]).astype(BF16)

                def in_last(i, t=t, p=p):
                    y = dot(hid[i % 2], weo[0])
                    for c in chunks():
                        v[p, pl.ds(t * TILE + c, CH), :] = norm(y[c:c + CH]).astype(BF16)

                def edge_first(i, rows=rows, t=t, p=p):
                    pre = dot(g2m[p, rows, :], w_edge[pl.ds(0, LAT), :]) + dot(v[p, rows, :], w_edge[pl.ds(LAT, LAT), :])
                    for c in chunks():
                        value = pre[c:c + CH] + recv[pl.ds(t * TILE + c, CH), :]
                        hid2[i % 2, pl.ds(c, CH), :] = silu(value).astype(BF16)

                def edge_last(i, t=t, p=p):
                    y = dot(hid2[i % 2], wedo[slot])
                    for c in chunks():
                        part = pl.ds(t * TILE + c, CH)
                        total = (g2m[p, part, :].astype(F32) + norm(y[c:c + CH])).astype(BF16).astype(F32)
                        if p == 0:
                            acc[part, :] = total
                        else:
                            esum[part, :] = (acc[part, :] + total).astype(BF16)

                items.append([in_first, in_last, edge_first, edge_last])
        pipeline(items)
        pipeline([node_item(t, h_mesh, slot, esum) for t in range(TILES)])
        send_halo(0)
        items = []
        for t in range(TILES):
            for p in range(2):
                rows = pl.ds(t * TILE, TILE)

                def self_first(i, rows=rows, p=p):
                    pre = dot(v[p, rows, :], wself[0])
                    for c in chunks():
                        hid[i % 2, pl.ds(c, CH), :] = silu(pre[c:c + CH]).astype(BF16)

                def self_last(i, t=t, p=p):
                    y = dot(hid[i % 2], wself[1])
                    for c in chunks():
                        part = pl.ds(t * TILE + c, CH)
                        vc[p, part, :] = (v[p, part, :].astype(F32) + norm(y[c:c + CH])).astype(BF16)

                items.append([self_first, self_last])
        pipeline(items)

    def out_copies(step, out):
        copies = []
        for hop in range(RING):
            target = lax.rem(me + hop, RING)
            src, dst = x_buf.at[step + 1, pl.ds(2 * target, 2)], out.at[:, place]
            if hop == 0:
                copies.append(pltpu.make_async_copy(src, dst, out_recv.at[step, hop]))
            else:
                copies.append(pltpu.make_async_remote_copy(
                    src_ref=src, dst_ref=dst, send_sem=out_send.at[step, hop], recv_sem=out_recv.at[step, hop],
                    device_id=at(target), device_id_type=mesh_id))
        return copies

    def decoder(step, slot):
        w_edge = wei.at[slot]
        for t in range(TILES):
            recv[pl.ds(t * TILE, TILE), :] = dot(h[pl.ds(t * TILE, TILE), :], w_edge[pl.ds(LAT, LAT), :])
        in_mean = stats[0:1, :]
        in_std = stats[1:2, :]
        diff_mean = stats[2:3, :]
        diff_std = stats[3:4, :]
        items = []
        for t in range(TILES):
            for p in range(2):
                rows = pl.ds(t * TILE, TILE)

                def edge_first(i, rows=rows, t=t, p=p):
                    pre = dot(m2g[p, rows, :], w_edge[pl.ds(0, LAT), :]) + dot(vc[p, rows, :], w_edge[pl.ds(2 * LAT, LAT), :])
                    for c in chunks():
                        value = pre[c:c + CH] + recv[pl.ds(t * TILE + c, CH), :]
                        hid[i % 2, pl.ds(c, CH), :] = silu(value).astype(BF16)

                def edge_last(i, t=t, p=p):
                    y = dot(hid[i % 2], wedo[slot])
                    for c in chunks():
                        part = pl.ds(t * TILE + c, CH)
                        dec[i % 2, pl.ds(c, CH), :] = (m2g[p, part, :].astype(F32) + norm(y[c:c + CH])).astype(BF16)

                def node_first(i, rows=rows, p=p):
                    pre = dot(vc[p, rows, :], wni[slot, pl.ds(0, LAT), :]) + dot(dec[i % 2], wni[slot, pl.ds(LAT, LAT), :])
                    for c in chunks():
                        hid2[i % 2, pl.ds(c, CH), :] = silu(pre[c:c + CH]).astype(BF16)

                def node_last(i, t=t, p=p):
                    y = dot(hid2[i % 2], wno[slot])
                    for c in chunks():
                        part = pl.ds(t * TILE + c, CH)
                        v[p, part, :] = (vc[p, part, :].astype(F32) + norm(y[c:c + CH])).astype(BF16)

                def out_first(i, rows=rows, t=t, p=p):
                    pre = dot(v[p, rows, :], woh[...])
                    for c in chunks():
                        vc[p, pl.ds(t * TILE + c, CH), :] = silu(pre[c:c + CH]).astype(BF16)

                def out_last(i, rows=rows, t=t, p=p):
                    pred = dot(vc[p, rows, :], wof[...])
                    for c in chunks():
                        q = (t * TILE + c) // RUN
                        now = x_buf[step, q, pl.ds(p, RUN, stride=2), :][:, :VARS]
                        new = now + diff_std * pred[c:c + CH] + diff_mean
                        wide = jnp.concatenate([new, jnp.zeros((CH, 128 - VARS), F32)], axis=1)
                        x_buf[step + 1, q, pl.ds(p, RUN, stride=2), :] = wide
                        feat[p, pl.ds(t * TILE + c, CH), pl.ds(0, VARS)] = ((new - in_mean) / in_std).astype(BF16)

                items.append([edge_first, edge_last, node_first, node_last, out_first, out_last])
        pipeline(items)

    def one_step(step, carry):
        def fetch(block, slot):
            for copy in block_copies(block, slot):
                copy.wait()

        def prefetch(block, slot):
            for copy in block_copies(block, slot):
                copy.start()

        fetch(0, 0)
        prefetch(1, 1)
        encoder(step, 0)

        def one_layer(index, carry):
            block = index + 1
            slot = lax.rem(block, 2)
            fetch(block, slot)
            prefetch(block + 1, 1 - slot)
            layer(block, slot, lax.rem(index, 2), index < LAYERS - 1)
            return carry

        lax.fori_loop(0, LAYERS, one_layer, 0)
        fetch(BLOCKS - 1, 1)

        @pl.when(step == 0)
        def _():
            prefetch(0, 0)
            wait_in(2)
            for q in range(RUNS):
                x_buf[0, q, :, pl.ds(0, VARS)] = xc_buf[q]
                x_buf[0, q, :, pl.ds(VARS, 128 - VARS)] = jnp.zeros((2 * RUN, 128 - VARS), F32)

        decoder(step, 1)

        @pl.when(step == 0)
        def _():
            for copy in out_copies(0, out0):
                copy.start()

        @pl.when(step == 1)
        def _():
            for copy in out_copies(1, out1):
                copy.start()
        return carry

    lax.fori_loop(0, 2, one_step, 0)
    for part in range(3):
        for hop in range(1, RING):
            in_copies[part][hop].wait_send()
    for step, out in ((0, out0), (1, out1)):
        for copy in out_copies(step, out):
            copy.wait()


def solution(mesh):
    row_spec = P(("dp", "gp"))
    edge_spec = P(("dp", "gp"), None, None)
    whole = P()

    def local_run(x_prev, x_cur, forcing, grid_static, g2m_feat, m2g_feat, mesh_feat, mesh_edge_feat, norm_stats,
                  w_grid_in, w_mesh_in, w_eemb_in, w_embed_out, w_edge_in, w_edge_out, w_node_in, w_node_out,
                  w_grid_self, w_out_hidden, w_out_final):
        grid_dev = x_prev.shape[0]
        mesh_dev = mesh_feat.shape[0]
        mean, std = norm_stats[0], norm_stats[1]

        def lanes(pieces, width):
            have = sum(piece.shape[1] for piece in pieces)
            rows = pieces[0].shape[0]
            return jnp.concatenate([piece.astype(BF16) for piece in pieces] + [jnp.zeros((rows, width - have), BF16)], axis=1)

        grid_lanes = jnp.concatenate([
            lanes([(x_prev - mean) / std, forcing[:, 0], grid_static, forcing[:, 1], m2g_feat], 128),
            lanes([(x_cur - mean) / std], 128)], axis=1)
        mesh_lanes = lanes([mesh_feat, mesh_edge_feat.reshape(mesh_dev, 24), g2m_feat.reshape(mesh_dev, 8)], 128)

        def placed(rows, start, height=128):
            return jnp.pad(rows, ((start, height - start - rows.shape[0]), (0, 0)))

        prev_rows, cur_rows = w_grid_in[:VARS], w_grid_in[VARS:2 * VARS]
        force_rows, static_rows = w_grid_in[2 * VARS:2 * VARS + 5], w_grid_in[2 * VARS + 5:]
        first_step = [placed(jnp.concatenate([prev_rows, force_rows, static_rows], axis=0), 0), placed(cur_rows, 0)]
        second_step = [placed(cur_rows, 0) + placed(static_rows, 89) + placed(force_rows, 94), placed(prev_rows, 0)]
        wemb = jnp.stack(
            [placed(w_mesh_in, 0)] + [placed(w_eemb_in[0], 27 + 4 * p) for p in range(2)]
            + [placed(w_eemb_in[2], 3 + 4 * k) for k in range(6)] + [placed(w_eemb_in[1], 99)]
            + first_step + second_step)

        any_spec = pl.BlockSpec(memory_space=pl.ANY)
        vmem_spec = pl.BlockSpec(memory_space=pltpu.VMEM)
        dma = pltpu.SemaphoreType.DMA
        out = jax.ShapeDtypeStruct((2, RING, 2 * RUN, 128), F32)
        scratch = [
            pltpu.VMEM((RUNS, 2 * RUN, 256), BF16),
            pltpu.VMEM((RUNS, RUN, 128), BF16),
            pltpu.VMEM((RUNS, 2 * RUN, VARS), F32),
            pltpu.VMEM((3, RUNS, 2 * RUN, 128), F32),
            pltpu.VMEM((2, RUNS * 2 * RUN, 128), F32),
            pltpu.VMEM((2, ROWS, 256), BF16),
            pltpu.VMEM((14, 128, LAT), BF16),
            pltpu.VMEM((5, LAT, LAT), BF16),
            pltpu.VMEM((2, 3 * LAT, LAT), BF16),
            pltpu.VMEM((2, LAT, LAT), BF16),
            pltpu.VMEM((2, 2 * LAT, LAT), BF16),
            pltpu.VMEM((2, LAT, LAT), BF16),
            pltpu.VMEM((2, LAT, LAT), BF16),
            pltpu.VMEM((LAT, LAT), BF16),
            pltpu.VMEM((LAT, VARS), BF16),
            pltpu.VMEM((6, ROWS, LAT), BF16),
            pltpu.VMEM((6, ROWS, LAT), BF16),
            pltpu.VMEM((ROWS, LAT), BF16),
            pltpu.VMEM((ROWS, LAT), BF16),
            pltpu.VMEM((4, ROWS, 128), F32),
            pltpu.VMEM((2, ROWS, LAT), BF16),
            pltpu.VMEM((2, ROWS, LAT), BF16),
            pltpu.VMEM((2, ROWS, LAT), BF16),
            pltpu.VMEM((2, ROWS, LAT), BF16),
            pltpu.VMEM((4, RUNS * PAD, 128), F32),
            pltpu.VMEM((ROWS, LAT), F32),
            pltpu.VMEM((ROWS, LAT), F32),
            pltpu.VMEM((2, TILE, LAT), BF16),
            pltpu.VMEM((2, TILE, LAT), BF16),
            pltpu.VMEM((ROWS, LAT), BF16),
            pltpu.VMEM((2, TILE, LAT), BF16),
            pltpu.VMEM((2, RUNS, LAT), BF16),
            pltpu.VMEM((2, 2, RUNS, LAT), BF16),
            dma((3, RING)), dma((3, RING)), dma((5,)), dma((2, 4)), dma((2,)), dma((2, 2)), dma((2, RING)), dma((2, RING)),
        ]
        next_state, after_state = pl.pallas_call(
            kernel,
            out_shape=(out, out),
            in_specs=[any_spec, any_spec, any_spec, vmem_spec] + [any_spec] * 9,
            out_specs=(any_spec, any_spec),
            scratch_shapes=scratch,
            compiler_params=pltpu.CompilerParams(collective_id=0, has_side_effects=True, vmem_limit_bytes=60 << 20),
            name="forecast",
        )(grid_lanes.reshape(2, RING, 2 * RUN, 256), mesh_lanes.reshape(2, RING, RUN, 128),
          x_cur.reshape(2, RING, 2 * RUN, VARS), norm_stats, wemb, w_embed_out, w_edge_in, w_edge_out, w_node_in,
          w_node_out, w_grid_self, w_out_hidden, w_out_final)
        return next_state.reshape(grid_dev, 128)[:, :VARS], after_state.reshape(grid_dev, 128)[:, :VARS]

    in_specs = (row_spec, row_spec, edge_spec, row_spec, row_spec, row_spec, row_spec, edge_spec, whole) + (whole,) * 11
    return jax.shard_map(local_run, mesh=mesh, in_specs=in_specs, out_specs=(row_spec, row_spec), check_vma=False)
```

time: 2320 us -> 291 us (0.13)
  matrix products: 748 us -> 0 us
  waiting for transfers between devices: 661 us -> 0 us
  other arithmetic: 366 us -> 1.1 us
  local copies, waits for them, and re-layouts: 357 us -> 11.8 us
  Pallas kernels: 0 us -> 277 us
  starting transfers between devices: 174 us -> 0 us
    dot_general x187 -> x0, matrix products: 748 us -> none  [the longest x186 740 us: matmul_f32(): return jnp.dot(values, weight, preferred_element_type=jnp.float32)]
    ppermute x132 -> x0, waiting for transfers between devices: 661 us -> none  [the longest x32 654 us: local_run(): lax.ppermute(mesh_cur[mesh_dev - half_shard:], 'gp', shift_pairs(1))]
    reduce_sum x114 -> x0, other arithmetic: 337 us -> none  [the longest x32 186 us: local_run(): edge_sum = jnp.sum(edge_lat, axis=1, dtype=jnp.float32).astype(jnp.bfloat16)]
    pallas_call x0 -> x1, Pallas kernels: none -> 277 us  [local_run(): pl.pallas_call(kernel, out_shape=(out, out), in_specs=[any_spec, any_spec...]
    unnamed x477 -> x42, local copies, waits for them, and re-layouts: 275 us -> 6.67 us
    ppermute x132 -> x0, starting transfers between devices: 174 us -> none  [the longest x32 83.3 us: local_run(): next_head = lax.ppermute(mesh_cur[:half_shard], 'gp', shift_pairs(-1))]
    another operation x32 -> x0, local copies, waits for them, and re-layouts: 33.6 us -> none  [local_run(): jnp.stack([send_proj[half_shard + 1:half_shard + 1 + mesh_dev], send_proj...]
    convert_element_type x41 -> x6, other arithmetic: 26.5 us -> 0.18 us  [lanes(): piece.astype(BF16)]
  transfers between devices with their start and end apart: 132 -> 0, of which waited for: 36 -> 0; matrix products, arithmetic and copies ran while one was open for 12% -> 0% of each run, Pallas kernels for 0% -> 0%
where the time goes in v1:
time: 291 us
  Pallas kernels  277 us (95%)
  local copies, waits for them, and re-layouts  11.8 us (4%)
    pallas_call x1, Pallas kernels, local_run(): pl.pallas_call(kernel, out_shape=(out, out), in_specs=[any_spec, any_spec...  277 us
    unnamed x42, local copies, waits for them, and re-layouts  6.67 us

profile of v1, /device:TPU:0, one launch (start us, length us, event | category | flops | bytes accessed | tf_op | source)
XLA Modules:
  0.0 290.9 jit_solution(10484369923431770720)
XLA Ops:
  0.6 0.0 copy-start.12
  0.6 0.0 copy-start.2
  0.7 0.0 copy-start.11
  0.7 0.0 copy-start.3
  0.7 0.0 copy-start.1
  0.7 0.8 slice_bitcast_fusion.2
  1.5 0.7 bitcast_dynamic-update-slice_fusion.10
  2.2 0.0 copy-start.6
  2.2 0.0 copy-start.7
  2.3 0.0 copy-start.8
  2.4 1.0 fusion.10
  3.4 0.7 slice.61
  4.2 0.0 copy-done.2
  4.2 0.0 copy-done.12
  4.2 0.1 bitcast_dynamic-update-slice_fusion.wemb
  4.3 0.0 copy-done.11
  4.3 0.0 copy-start
  4.3 0.0 copy-start.9
  4.4 0.0 copy-done.3
  4.4 0.0 copy-done.1
  4.4 0.1 divide_convert_fusion
  4.5 0.0 copy-start.5
  4.5 0.0 copy-start.10
  4.6 0.0 copy-done.6
  4.6 0.0 copy-done.7
  4.6 0.0 copy-done.8
  4.7 0.8 concatenate.10
  5.5 0.0 copy-start.4
  5.5 1.0 copy.30
  6.5 0.0 copy-done.9
  6.5 0.2 copy.31
  6.8 0.0 copy-done
  6.8 0.1 convert_element_type.75
  6.9 0.0 copy-done.5
  7.0 0.1 copy.33
  7.1 0.0 copy-done.10
  7.1 0.2 copy.32
  7.3 0.1 pad.80.clone
  7.4 0.8 maximum_maximum_fusion
  8.2 1.0 copy.34
  9.2 0.0 copy-done.4
  9.2 0.8 copy.35.w_out_final
  10.0 276.9 %forecast.1 = (f32[2,8,64,128]{3,2,1,0:T(8,128)}, f32[2,8,64,128]{3,2,1,0:T(8,128)}) custom-call(bf16[2,8,64,256]{3,2,1,0:T(8,128)(2,1)} %bitcast.58, bf16[2,8,32,128]{3,2,1,0:T(8,128)(2,1)} %bitcast.59, f32[2,8,64,84]{3,2,1,0:T(8,128)} %bitcast.57, f32[4,84]{1,0:T(4,128)} %stats.1, bf16[14,128,512]{2,1,0:T(8,128)(2,1)} %copy-done, ...), custom_call_target="tpu_custom_call" | custom-call | tf_op jit(solution)/shard_map/forecast/pallas_call | solution.py:542
  286.9 2.0 copy.38
  288.9 2.0 copy.39
  (25 shorter events, 0.2 us)
Async XLA Ops:
  0.6 3.6 %copy-start.12 = (pred[128]{0:T(512)(128)(4,1)S(1)}, pred[128]{0:T(512)(128)(4,1)}, u32[]{:S(2)}) copy-start(pred[128]{0:T(512)(128)(4,1)} %constant.3.clone.1) | copy-start | bytes 388
  0.6 3.5 %copy-start.2 = (bf16[178,512]{1,0:T(8,128)(2,1)S(1)}, bf16[178,512]{1,0:T(8,128)(2,1)}, u32[]{:S(2)}) copy-start(bf16[178,512]{1,0:T(8,128)(2,1)} %param.29) | copy-start | bytes 546820
  0.7 3.7 %copy-start.11 = (f32[4,84]{1,0:T(4,128)S(1)}, f32[4,84]{1,0:T(4,128)}, u32[]{:S(2)}) copy-start(f32[4,84]{1,0:T(4,128)} %stats.1) | copy-start | bytes 4036
  0.7 3.7 %copy-start.3 = (f32[1024,84]{0,1:T(8,128)S(1)}, f32[1024,84]{0,1:T(8,128)}, u32[]{:S(2)}) copy-start(f32[1024,84]{0,1:T(8,128)} %param.20) | copy-start | bytes 1032196
  0.7 3.7 %copy-start.1 = (f32[1024,84]{0,1:T(8,128)S(1)}, f32[1024,84]{0,1:T(8,128)}, u32[]{:S(2)}) copy-start(f32[1024,84]{0,1:T(8,128)} %param.21) | copy-start | bytes 1032196
  2.2 2.4 copy-start.6
  2.2 2.4 copy-start.7
  2.3 2.4 copy-start.8
  4.3 2.4 copy-start
  4.3 2.2 copy-start.9
  4.5 2.4 copy-start.5
  4.5 2.6 copy-start.10
  5.5 3.7 %copy-start.4 = (bf16[512,84]{0,1:T(8,128)(2,1)S(1)}, bf16[512,84]{0,1:T(8,128)(2,1)}, u32[]{:S(2)}) copy-start(bf16[512,84]{0,1:T(8,128)(2,1)} %param.39) | copy-start | bytes 258052

commit v2 on v1

v2 whole, which is shorter than its diff:
```python
import functools

import jax
import jax.numpy as jnp
from jax import lax
from jax.experimental import pallas as pl
from jax.experimental.pallas import tpu as pltpu
from jax.sharding import PartitionSpec as P

F32 = jnp.float32
BF16 = jnp.bfloat16

RUNS = 16
RUN = 32
ROWS = RUNS * RUN
LAT = 512
VARS = 84
PAD0 = 32
PAD1 = 48
TILE = 256
TILES = 2
HALF = TILE // RUNS
CH = 32
RING = 8
LAYERS = 16
BLOCKS = LAYERS + 2
SLOTS = 4
FAR = ((2, 1), (3, -1), (4, 4), (5, -4))
NEAR = ((0, 1), (1, -1))
ORDER = (
    "before", "n1", "fx0", "bx0", "fx1", "bx1",
    "fn0", "fn1", "bn0", "bn1", "ax0", "fx2", "bx2",
    "ax1", "fx3", "bx3", "na", "ax2", "nb", "an0", "ax3", "project",
)


def dot(a, b):
    return jnp.dot(a, b, preferred_element_type=F32)


def silu(pre):
    return pre * jax.nn.sigmoid(pre)


def norm(y):
    centred = y - jnp.mean(y, axis=-1, keepdims=True)
    return centred * lax.rsqrt(jnp.mean(centred * centred, axis=-1, keepdims=True) + 1e-5)


def ring_place(dev):
    high = lax.div(dev, 4)
    return high * (4 + lax.rem(dev + 2, 4)) + (1 - high) * dev


def chunks():
    return range(0, TILE, CH)


def tile_rows(t):
    return pl.ds(t * TILE, TILE)


def part_rows(t, c):
    return pl.ds(t * TILE + c, CH)


def chunk_runs(c):
    return range(c // HALF, (c + CH) // HALF)


def pieces(t):
    return ((8, 16),) if t == 0 else ((0, 8), (24, 8))


def get_tiles(ref, rows):
    return jnp.concatenate([ref[j, rows, :] for j in range(ref.shape[0])], axis=1)


def set_tiles(ref, rows, value):
    for j in range(ref.shape[0]):
        ref[j, rows, :] = value[:, 128 * j:128 * j + 128]


def kernel(g_in, mf_in, xc_in, stats, wemb, w_embed_out, w_edge_in, w_edge_out, w_node_in, w_node_out, w_grid_self,
           w_out_hidden, w_out_final, out0, out1,
           g_buf, mf_buf, xc_buf, x_buf, gf, feat, we, weo, wself, woh, wof,
           enc_ei, enc_eo, enc_ni, enc_no, lay_ei, lay_eo, lay_ni, lay_no,
           edge_base, edge, h_mesh, h, hf, g2m, m2g, v, vc, proj0, proj1, recv, acc, hid, esum, dec, pre_buf,
           send_buf, halo_buf,
           in_send, in_recv, w_sem, enc_sem, lay_sem, halo_send, halo_recv, out_send, out_recv):
    me = lax.axis_index("gp")
    place = ring_place(me)

    def at(dev):
        return {"gp": dev}

    mesh_id = pl.DeviceIdType.MESH

    def block_copies(block, dst_refs, slot, sem):
        srcs = (w_edge_in, w_edge_out, w_node_in, w_node_out)
        return [pltpu.make_async_copy(src.at[block], dst.at[slot], sem.at[slot, i])
                for i, (src, dst) in enumerate(zip(srcs, dst_refs))]

    enc_refs = (enc_ei, enc_eo, enc_ni, enc_no)
    lay_refs = (lay_ei, lay_eo, lay_ni, lay_no)

    def enc_copies():
        return block_copies(0, enc_refs, 0, enc_sem)

    def slot_of(step, block):
        return lax.rem((BLOCKS - 1) * step + block - 1, SLOTS)

    def layer_copies(step, block):
        return block_copies(block, lay_refs, slot_of(step, block), lay_sem)

    class Weights:
        def __init__(self, refs, slot):
            self.edge = [refs[0].at[slot, pl.ds(i * LAT, LAT)] for i in range(3)]
            self.edge_out = refs[1].at[slot]
            self.node = [refs[2].at[slot, pl.ds(i * LAT, LAT)] for i in range(2)]
            self.node_out = refs[3].at[slot]

    def layer_weights(step, block):
        return Weights(lay_refs, slot_of(step, block))

    small = [
        pltpu.make_async_copy(wemb, we, w_sem.at[0]),
        pltpu.make_async_copy(w_embed_out, weo, w_sem.at[1]),
        pltpu.make_async_copy(w_grid_self, wself, w_sem.at[2]),
        pltpu.make_async_copy(w_out_hidden, woh, w_sem.at[3]),
        pltpu.make_async_copy(w_out_final, wof, w_sem.at[4]),
    ]
    for copy in small + enc_copies() + layer_copies(0, 1) + layer_copies(0, 2):
        copy.start()

    barrier = pltpu.get_barrier_semaphore()
    for hop in range(1, RING):
        pl.semaphore_signal(barrier, inc=1, device_id=at(lax.rem(me + hop, RING)), device_id_type=mesh_id)
    pl.semaphore_wait(barrier, RING - 1)

    parts = ((mf_in, mf_buf), (g_in, g_buf), (xc_in, xc_buf))

    def in_copy(part, hop):
        src, dst = parts[part]
        target = lax.rem(me + hop, RING)
        src = src.at[:, ring_place(target)]
        dst = dst.at[pl.ds(2 * me, 2)]
        if hop == 0:
            return pltpu.make_async_copy(src, dst, in_recv.at[part, 0])
        return pltpu.make_async_remote_copy(src_ref=src, dst_ref=dst, send_sem=in_send.at[part, hop],
                                            recv_sem=in_recv.at[part, hop], device_id=at(target),
                                            device_id_type=mesh_id)

    in_copies = [[in_copy(part, hop) for hop in range(RING)] for part in range(3)]
    for part in range(3):
        for copy in in_copies[part]:
            copy.start()

    def wait_in(part):
        in_copies[part][0].wait()
        for hop in range(1, RING):
            in_copies[part][hop].wait_recv()

    def pipeline(items):
        depth = max(len(item) for item in items)
        for beat in range(len(items) + depth - 1):
            for stage in range(depth):
                index = beat - stage
                if 0 <= index < len(items) and stage < len(items[index]):
                    items[index][stage](index)

    def hide(slot, pre, extra=None):
        for c in chunks():
            value = pre[c:c + CH]
            if extra is not None:
                value = value + extra(c)
            hid[slot, pl.ds(c, CH), :] = silu(value).astype(BF16)

    def embed_item(load, w_first, second, store):
        def first(i):
            hide(i % 2, dot(load(), we[w_first]))

        def last(i):
            y = dot(hid[i % 2], weo[second])
            for c in chunks():
                store(c, norm(y[c:c + CH]).astype(BF16))

        return [first, last]

    wait_in(0)
    for copy in small[:2]:
        copy.wait()
    mesh_feat = [jnp.concatenate([mf_buf[(q + 1) % RUNS].astype(F32)[r:r + n] for q in range(RUNS) for r, n in pieces(t)],
                                 axis=0).astype(BF16) for t in range(TILES)]
    items = []
    for t in range(TILES):
        def store_mesh(c, value, t=t):
            h_mesh[part_rows(t, c), :] = value
        items.append(embed_item(lambda t=t: mesh_feat[t], 0, 1, store_mesh))
        for p in range(2):
            def store_g2m(c, value, t=t, p=p):
                g2m[p, part_rows(t, c), :] = value
            items.append(embed_item(lambda t=t: mesh_feat[t], 1 + p, 2, store_g2m))
        for k in range(6):
            def store_edge(c, value, t=t, k=k):
                edge_base[k, part_rows(t, c), :] = value
            items.append(embed_item(lambda t=t: mesh_feat[t], 3 + k, 4, store_edge))
    pipeline(items)

    wait_in(1)
    for q in range(RUNS):
        set_tiles(gf, pl.ds(q * 2 * RUN, 2 * RUN), g_buf[q].astype(F32))
    for t in range(TILES):
        for p in range(2):
            for c in chunks():
                feat[p, part_rows(t, c), :] = jnp.concatenate(
                    [get_tiles(gf, pl.ds(q * 2 * RUN + 2 * r + p, n, stride=2)) for q in chunk_runs(c) for r, n in pieces(t)],
                    axis=0).astype(BF16)
    items = []
    for t in range(TILES):
        for p in range(2):
            def store_m2g(c, value, t=t, p=p):
                m2g[p, part_rows(t, c), :] = value
            items.append(embed_item(lambda t=t, p=p: feat[p, tile_rows(t), pl.ds(0, 128)], 9, 3, store_m2g))
    pipeline(items)
    for copy in small[2:] + enc_copies():
        copy.wait()

    left = ring_place(lax.rem(place + RING - 1, RING))
    right = ring_place(lax.rem(place + 1, RING))

    def halo_copies(slot):
        return [
            pltpu.make_async_remote_copy(src_ref=send_buf.at[side], dst_ref=halo_buf.at[slot, side],
                                         send_sem=halo_send.at[side], recv_sem=halo_recv.at[slot, side],
                                         device_id=at(target), device_id_type=mesh_id)
            for side, target in ((0, left), (1, right))
        ]

    def send_halo(slot):
        first = get_tiles(hf, pl.ds(0, RUNS, stride=HALF))
        final = get_tiles(hf, pl.ds(HALF - 1, RUNS, stride=HALF))
        first_on = jnp.concatenate([first[1:], first[:1]], axis=0)
        final_back = jnp.concatenate([final[-1:], final[:-1]], axis=0)
        send_buf[0] = jnp.where(place == 0, first_on, first).astype(BF16)
        send_buf[1] = jnp.where(place == RING - 1, final_back, final).astype(BF16)
        for copy in halo_copies(slot):
            copy.start()

    def wait_halo(slot):
        for copy in halo_copies(slot):
            copy.wait()

    def project_halo(slot, w):
        rows = jnp.concatenate([halo_buf[slot, 0], halo_buf[slot, 1]], axis=0)
        out = dot(rows, w.edge[1][...])
        set_tiles(proj1, pl.ds(8 + RUN, RUNS, stride=PAD1), out[:RUNS])
        set_tiles(proj1, pl.ds(7, RUNS, stride=PAD1), out[RUNS:])

    class Edge:
        def __init__(self, t, k, w, slot, run_shift=0, row_shift=0, source=None, first=False, final=False, keep=None):
            self.t, self.k, self.w, self.slot, self.keep = t, k, w, slot, keep
            self.run_shift, self.row_shift, self.first, self.final = run_shift, row_shift, first, final
            self.source = edge if source is None else source
            self.pre = None

        def a(self):
            self.pre = dot(self.source[self.k, tile_rows(self.t), :], self.w.edge[0][...])
            if self.keep is not None:
                for c in chunks():
                    pre_buf[self.keep, pl.ds(c, CH), :] = self.pre[c:c + CH]

        def resume(self):
            self.pre = pre_buf.at[self.keep]

        def extra(self, c):
            got = []
            for q in chunk_runs(c):
                base = (q + self.run_shift) % RUNS
                for r, n in pieces(self.t):
                    if self.t == 0:
                        got.append(get_tiles(proj0, pl.ds(base * PAD0 + r + self.row_shift, n)))
                    else:
                        got.append(get_tiles(proj1, pl.ds(base * PAD1 + 8 + r + self.row_shift, n)))
            return jnp.concatenate(got, axis=0) + recv[part_rows(self.t, c), :]

        def fin(self):
            hide(self.slot, self.pre, self.extra)

        def b(self):
            y = dot(hid[self.slot], self.w.edge_out[...])
            for c in chunks():
                part = part_rows(self.t, c)
                value = (self.source[self.k, part, :].astype(F32) + norm(y[c:c + CH])).astype(BF16)
                edge[self.k, part, :] = value
                total = value.astype(F32)
                if not self.first:
                    total = total + acc[part, :]
                if self.final:
                    esum[part, :] = total.astype(BF16)
                else:
                    acc[part, :] = total

    class Node:
        def __init__(self, t, base, w):
            self.t, self.base, self.w, self.slot = t, base, w, 6 + t

        def a(self):
            rows = tile_rows(self.t)
            hide(self.slot, dot(self.base[rows, :], self.w.node[0][...]) + dot(esum[rows, :], self.w.node[1][...]))

        def b(self):
            y = dot(hid[self.slot], self.w.node_out[...])
            for c in chunks():
                part = part_rows(self.t, c)
                value = (self.base[part, :].astype(F32) + norm(y[c:c + CH])).astype(BF16)
                h[part, :] = value
                if self.t == 1:
                    set_tiles(hf, pl.ds(c, CH), value.astype(F32))

    def project(t, w):
        out = dot(h[tile_rows(t), :], w.edge[1][...])
        for q in range(RUNS):
            row = q * HALF
            for r, n in pieces(t):
                if t == 0:
                    set_tiles(proj0, pl.ds(q * PAD0 + r, n), out[row:row + n])
                else:
                    set_tiles(proj1, pl.ds(q * PAD1 + 8 + r, n), out[row:row + n])
                row += n
        back = dot(h[tile_rows(t), :], w.edge[2][...])
        for c in chunks():
            recv[part_rows(t, c), :] = back[c:c + CH]
        if t == 1:
            for r in (7, 24):
                set_tiles(proj0, pl.ds(r, RUNS, stride=PAD0), get_tiles(proj1, pl.ds(8 + r, RUNS, stride=PAD1)))

    def share_rows():
        for r in (8, 23):
            set_tiles(proj1, pl.ds(8 + r, RUNS, stride=PAD1), get_tiles(proj0, pl.ds(r, RUNS, stride=PAD0)))

    def far_items(t, w, source=None, resume=False):
        items = [Edge(t, k, w, n, run_shift=s, source=source, first=n == 0, keep=4 * t + n) for n, (k, s) in enumerate(FAR)]
        if resume:
            for item in items:
                item.resume()
        return items

    def near_items(t, w, resume=False):
        items = [Edge(t, k, w, 4 + n, row_shift=s, final=n == 1, keep=8 + t if n == 0 else None)
                 for n, (k, s) in enumerate(NEAR)]
        if resume:
            items[0].resume()
        return items

    def nothing():
        pass


    def phase(x, n, node, next_x, next_n, before, after):
        table = {"before": before, "n1": n[1].a, "na": node.a, "nb": node.b, "project": after, "an0": next_n[0].a}
        for i in range(4):
            table[f"fx{i}"], table[f"bx{i}"] = x[i].fin, x[i].b
            table[f"ax{i}"] = next_x[i].a if next_x else nothing
        for i in range(2):
            table[f"fn{i}"], table[f"bn{i}"] = n[i].fin, n[i].b
        for name in ORDER:
            table[name]()

    def encoder(step):
        w = Weights(enc_refs, 0)
        w1 = layer_weights(step, 1)
        w2 = layer_weights(step, 2)
        for k in range(6):
            for t in range(TILES):
                if t == 1 or k < 2:
                    edge[k, tile_rows(t), :] = edge_base[k, tile_rows(t), :]
        for t in range(TILES):
            out = dot(h_mesh[tile_rows(t), :], w.edge[2][...])
            for c in chunks():
                recv[part_rows(t, c), :] = out[c:c + CH]
        items = []
        for t in range(TILES):
            for p in range(2):
                def in_first(i, t=t, p=p):
                    hide(i % 2, dot(feat[p, tile_rows(t), :], we[pl.ds(10 + 2 * step, 2)].reshape(256, LAT)))

                def in_last(i, t=t, p=p):
                    y = dot(hid[i % 2], weo[0])
                    for c in chunks():
                        v[p, part_rows(t, c), :] = norm(y[c:c + CH]).astype(BF16)

                def edge_first(i, t=t, p=p):
                    pre = dot(g2m[p, tile_rows(t), :], w.edge[0][...]) + dot(v[p, tile_rows(t), :], w.edge[1][...])
                    hide(2 + i % 2, pre, lambda c, t=t: recv[part_rows(t, c), :])

                def edge_last(i, t=t, p=p):
                    y = dot(hid[2 + i % 2], w.edge_out[...])
                    for c in chunks():
                        part = part_rows(t, c)
                        total = (g2m[p, part, :].astype(F32) + norm(y[c:c + CH])).astype(BF16).astype(F32)
                        if p == 0:
                            acc[part, :] = total
                        else:
                            esum[part, :] = (acc[part, :] + total).astype(BF16)

                items.append([in_first, in_last, edge_first, edge_last])
        pipeline(items)
        nodes = [Node(t, h_mesh, w) for t in range(TILES)]
        selfs = []
        for t in range(TILES):
            for p in range(2):
                def self_first(t=t, p=p):
                    hide(4 + p, dot(v[p, tile_rows(t), :], wself[0]))

                def self_last(t=t, p=p):
                    y = dot(hid[4 + p], wself[1])
                    for c in chunks():
                        part = part_rows(t, c)
                        vc[p, part, :] = (v[p, part, :].astype(F32) + norm(y[c:c + CH])).astype(BF16)

                selfs.append((self_first, self_last))
        y = far_items(0, w1, edge_base)
        x = far_items(1, w1)
        nodes[0].a()
        selfs[0][0]()
        nodes[1].a()
        selfs[1][0]()
        nodes[0].b()
        selfs[0][1]()
        nodes[1].b()
        selfs[1][1]()
        y[0].a()
        y[1].a()
        project(0, w1)
        y[2].a()
        y[3].a()
        project(1, w1)
        send_halo(0)
        share_rows()
        selfs[2][0]()
        selfs[3][0]()
        y[0].fin()
        y[0].b()
        y[1].fin()
        y[1].b()
        selfs[2][1]()
        y[2].fin()
        y[2].b()
        y[3].fin()
        y[3].b()
        selfs[3][1]()
        for item in x + far_items(0, w2) + near_items(0, w1)[:1]:
            item.a()

    def out_copies(step, out):
        copies = []
        for hop in range(RING):
            target = lax.rem(me + hop, RING)
            src, dst = x_buf.at[step + 1, pl.ds(2 * target, 2)], out.at[:, place]
            if hop == 0:
                copies.append(pltpu.make_async_copy(src, dst, out_recv.at[step, hop]))
            else:
                copies.append(pltpu.make_async_remote_copy(
                    src_ref=src, dst_ref=dst, send_sem=out_send.at[step, hop], recv_sem=out_recv.at[step, hop],
                    device_id=at(target), device_id_type=mesh_id))
        return copies

    def decoder_items(step):
        w = layer_weights(step, BLOCKS - 1)
        in_mean = stats[0:1, :]
        in_std = stats[1:2, :]
        diff_mean = stats[2:3, :]
        diff_std = stats[3:4, :]
        items = []
        for t in range(TILES):
            for p in range(2):
                def edge_first(i, t=t, p=p):
                    if p == 0 and t == 0:
                        for q in range(RUNS):
                            recv[pl.ds(q * HALF, HALF), :] = get_tiles(proj0, pl.ds(q * PAD0 + 8, HALF))
                    elif p == 0:
                        out = dot(h[tile_rows(t), :], w.edge[1][...])
                        for c in chunks():
                            recv[part_rows(t, c), :] = out[c:c + CH]
                    pre = dot(m2g[p, tile_rows(t), :], w.edge[0][...]) + dot(vc[p, tile_rows(t), :], w.edge[2][...])
                    hide(i % 2, pre, lambda c, t=t: recv[part_rows(t, c), :])

                def edge_last(i, t=t, p=p):
                    y = dot(hid[i % 2], w.edge_out[...])
                    for c in chunks():
                        part = part_rows(t, c)
                        dec[i % 2, pl.ds(c, CH), :] = (m2g[p, part, :].astype(F32) + norm(y[c:c + CH])).astype(BF16)

                def node_first(i, t=t, p=p):
                    hide(2 + i % 2, dot(vc[p, tile_rows(t), :], w.node[0][...]) + dot(dec[i % 2], w.node[1][...]))

                def node_last(i, t=t, p=p):
                    y = dot(hid[2 + i % 2], w.node_out[...])
                    for c in chunks():
                        part = part_rows(t, c)
                        v[p, part, :] = (vc[p, part, :].astype(F32) + norm(y[c:c + CH])).astype(BF16)

                def out_first(i, t=t, p=p):
                    hide(4 + i % 2, dot(v[p, tile_rows(t), :], woh[...]))

                def out_last(i, t=t, p=p):
                    pred = dot(hid[4 + i % 2], wof[...])
                    for c in chunks():
                        spots = [(q, pl.ds(2 * r + p, n, stride=2), n) for q in chunk_runs(c) for r, n in pieces(t)]
                        now = jnp.concatenate([x_buf[step, q, rows, :] for q, rows, n in spots], axis=0)[:, :VARS]
                        new = now + diff_std * pred[c:c + CH] + diff_mean
                        wide = jnp.concatenate([new, jnp.zeros((CH, 128 - VARS), F32)], axis=1)
                        row = 0
                        for q, rows, n in spots:
                            x_buf[step + 1, q, rows, :] = wide[row:row + n]
                            row += n
                        feat[p, part_rows(t, c), pl.ds(0, VARS)] = ((new - in_mean) / in_std).astype(BF16)

                items.append([edge_first, edge_last, node_first, node_last, out_first, out_last])
        return items

    def wait_all(copies):
        for copy in copies:
            copy.wait()

    def start_all(copies):
        for copy in copies:
            copy.start()

    def one_step(step, carry):
        wait_all(layer_copies(step, 1) + layer_copies(step, 2))
        start_all(layer_copies(step, 3))
        encoder(step)

        def one_layer(block, carry):
            halo_slot = lax.rem(block + 1, 2)
            wait_all(layer_copies(step, block + 2))

            @pl.when(block < LAYERS - 1)
            def _():
                start_all(layer_copies(step, block + 3))

            w, w1, w2 = (layer_weights(step, block + i) for i in range(3))
            phase(far_items(1, w, resume=True), near_items(0, w, resume=True), Node(0, h, w), far_items(1, w1),
                  near_items(1, w), share_rows, lambda: project(0, w1))
            wait_halo(halo_slot)
            phase(far_items(0, w1, resume=True), near_items(1, w, resume=True), Node(1, h, w), far_items(0, w2),
                  near_items(0, w1), lambda: project_halo(halo_slot, w), lambda: project(1, w1))
            send_halo(1 - halo_slot)
            return carry

        lax.fori_loop(1, LAYERS, one_layer, 0)
        @pl.when(step == 0)
        def _():
            start_all(layer_copies(1, 1) + layer_copies(1, 2))
            wait_in(2)
            for q in range(RUNS):
                x_buf[0, q, :, pl.ds(0, VARS)] = xc_buf[q]
                x_buf[0, q, :, pl.ds(VARS, 128 - VARS)] = jnp.zeros((2 * RUN, 128 - VARS), F32)

        w = layer_weights(step, LAYERS)
        w_last = layer_weights(step, BLOCKS - 1)
        n1 = near_items(1, w)
        phase(far_items(1, w, resume=True), near_items(0, w, resume=True), Node(0, h, w), None, n1, share_rows,
              lambda: project(0, w_last))
        n1[1].a()
        wait_halo(lax.rem(LAYERS + 1, 2))
        project_halo(lax.rem(LAYERS + 1, 2), w)
        last = Node(1, h, w)
        for item in n1:
            item.fin()
        for item in n1:
            item.b()
        last.a()
        last.b()
        pipeline(decoder_items(step))

        @pl.when(step == 0)
        def _():
            start_all(out_copies(0, out0))

        @pl.when(step == 1)
        def _():
            start_all(out_copies(1, out1))
        return carry

    lax.fori_loop(0, 2, one_step, 0)
    for part in range(3):
        for hop in range(1, RING):
            in_copies[part][hop].wait_send()
    for step, out in ((0, out0), (1, out1)):
        wait_all(out_copies(step, out))


def solution(mesh):
    row_spec = P(("dp", "gp"))
    edge_spec = P(("dp", "gp"), None, None)
    whole = P()

    def local_run(x_prev, x_cur, forcing, grid_static, g2m_feat, m2g_feat, mesh_feat, mesh_edge_feat, norm_stats,
                  w_grid_in, w_mesh_in, w_eemb_in, w_embed_out, w_edge_in, w_edge_out, w_node_in, w_node_out,
                  w_grid_self, w_out_hidden, w_out_final):
        grid_dev = x_prev.shape[0]
        mesh_dev = mesh_feat.shape[0]
        mean, std = norm_stats[0], norm_stats[1]

        def lanes(pieces, width):
            have = sum(piece.shape[1] for piece in pieces)
            rows = pieces[0].shape[0]
            return jnp.concatenate([piece.astype(BF16) for piece in pieces] + [jnp.zeros((rows, width - have), BF16)], axis=1)

        grid_lanes = jnp.concatenate([
            lanes([(x_prev - mean) / std, forcing[:, 0], grid_static, forcing[:, 1], m2g_feat], 128),
            lanes([(x_cur - mean) / std], 128)], axis=1)
        mesh_lanes = lanes([mesh_feat, mesh_edge_feat.reshape(mesh_dev, 24), g2m_feat.reshape(mesh_dev, 8)], 128)

        def placed(rows, start, height=128):
            return jnp.pad(rows, ((start, height - start - rows.shape[0]), (0, 0)))

        prev_rows, cur_rows = w_grid_in[:VARS], w_grid_in[VARS:2 * VARS]
        force_rows, static_rows = w_grid_in[2 * VARS:2 * VARS + 5], w_grid_in[2 * VARS + 5:]
        first_step = [placed(jnp.concatenate([prev_rows, force_rows, static_rows], axis=0), 0), placed(cur_rows, 0)]
        second_step = [placed(cur_rows, 0) + placed(static_rows, 89) + placed(force_rows, 94), placed(prev_rows, 0)]
        wemb = jnp.stack(
            [placed(w_mesh_in, 0)] + [placed(w_eemb_in[0], 27 + 4 * p) for p in range(2)]
            + [placed(w_eemb_in[2], 3 + 4 * k) for k in range(6)] + [placed(w_eemb_in[1], 99)]
            + first_step + second_step)

        any_spec = pl.BlockSpec(memory_space=pl.ANY)
        vmem_spec = pl.BlockSpec(memory_space=pltpu.VMEM)
        dma = pltpu.SemaphoreType.DMA
        out = jax.ShapeDtypeStruct((2, RING, 2 * RUN, 128), F32)
        scratch = [
            pltpu.VMEM((RUNS, 2 * RUN, 256), BF16),
            pltpu.VMEM((RUNS, RUN, 128), BF16),
            pltpu.VMEM((RUNS, 2 * RUN, VARS), F32),
            pltpu.VMEM((3, RUNS, 2 * RUN, 128), F32),
            pltpu.VMEM((2, RUNS * 2 * RUN, 128), F32),
            pltpu.VMEM((2, ROWS, 256), BF16),
            pltpu.VMEM((14, 128, LAT), BF16),
            pltpu.VMEM((5, LAT, LAT), BF16),
            pltpu.VMEM((2, LAT, LAT), BF16),
            pltpu.VMEM((LAT, LAT), BF16),
            pltpu.VMEM((LAT, VARS), BF16),
            pltpu.VMEM((1, 3 * LAT, LAT), BF16),
            pltpu.VMEM((1, LAT, LAT), BF16),
            pltpu.VMEM((1, 2 * LAT, LAT), BF16),
            pltpu.VMEM((1, LAT, LAT), BF16),
            pltpu.VMEM((SLOTS, 3 * LAT, LAT), BF16),
            pltpu.VMEM((SLOTS, LAT, LAT), BF16),
            pltpu.VMEM((SLOTS, 2 * LAT, LAT), BF16),
            pltpu.VMEM((SLOTS, LAT, LAT), BF16),
            pltpu.VMEM((6, ROWS, LAT), BF16),
            pltpu.VMEM((6, ROWS, LAT), BF16),
            pltpu.VMEM((ROWS, LAT), BF16),
            pltpu.VMEM((ROWS, LAT), BF16),
            pltpu.VMEM((LAT // 128, TILE, 128), F32),
            pltpu.VMEM((2, ROWS, LAT), BF16),
            pltpu.VMEM((2, ROWS, LAT), BF16),
            pltpu.VMEM((2, ROWS, LAT), BF16),
            pltpu.VMEM((2, ROWS, LAT), BF16),
            pltpu.VMEM((LAT // 128, RUNS * PAD0, 128), F32),
            pltpu.VMEM((LAT // 128, RUNS * PAD1, 128), F32),
            pltpu.VMEM((ROWS, LAT), F32),
            pltpu.VMEM((ROWS, LAT), F32),
            pltpu.VMEM((8, TILE, LAT), BF16),
            pltpu.VMEM((ROWS, LAT), BF16),
            pltpu.VMEM((2, TILE, LAT), BF16),
            pltpu.VMEM((10, TILE, LAT), F32),
            pltpu.VMEM((2, RUNS, LAT), BF16),
            pltpu.VMEM((2, 2, RUNS, LAT), BF16),
            dma((3, RING)), dma((3, RING)), dma((5,)), dma((1, 4)), dma((SLOTS, 4)), dma((2,)), dma((2, 2)),
            dma((2, RING)), dma((2, RING)),
        ]
        next_state, after_state = pl.pallas_call(
            kernel,
            out_shape=(out, out),
            in_specs=[any_spec, any_spec, any_spec, vmem_spec] + [any_spec] * 9,
            out_specs=(any_spec, any_spec),
            scratch_shapes=scratch,
            compiler_params=pltpu.CompilerParams(collective_id=0, has_side_effects=True, vmem_limit_bytes=60 << 20),
            name="forecast",
        )(grid_lanes.reshape(2, RING, 2 * RUN, 256), mesh_lanes.reshape(2, RING, RUN, 128),
          x_cur.reshape(2, RING, 2 * RUN, VARS), norm_stats, wemb, w_embed_out, w_edge_in, w_edge_out, w_node_in,
          w_node_out, w_grid_self, w_out_hidden, w_out_final)
        return next_state.reshape(grid_dev, 128)[:, :VARS], after_state.reshape(grid_dev, 128)[:, :VARS]

    in_specs = (row_spec, row_spec, edge_spec, row_spec, row_spec, row_spec, row_spec, edge_spec, whole) + (whole,) * 11
    return jax.shard_map(local_run, mesh=mesh, in_specs=in_specs, out_specs=(row_spec, row_spec), check_vma=False)
```

time: 291 us -> 266 us (0.914)
  Pallas kernels: 277 us -> 252 us
    pallas_call x1, Pallas kernels: 277 us -> 252 us  [local_run(): pl.pallas_call(kernel, out_shape=(out, out), in_specs=[any_spec, any_spec...]
where the time goes in v2:
time: 266 us
  Pallas kernels  252 us (95%)
  local copies, waits for them, and re-layouts  11.8 us (4%)
    pallas_call x1, Pallas kernels, local_run(): pl.pallas_call(kernel, out_shape=(out, out), in_specs=[any_spec, any_spec...  252 us
    unnamed x42, local copies, waits for them, and re-layouts  6.67 us

profile of v2, /device:TPU:0, one launch (start us, length us, event | category | flops | bytes accessed | tf_op | source)
XLA Modules:
  0.0 265.6 jit_solution(11461705203717128793)
XLA Ops:
  0.6 0.0 copy-start.12
  0.6 0.0 copy-start.2
  0.7 0.0 copy-start.11
  0.7 0.0 copy-start.3
  0.7 0.0 copy-start.1
  0.7 0.8 slice_bitcast_fusion.2
  1.5 0.7 bitcast_dynamic-update-slice_fusion.10
  2.2 0.0 copy-start.6
  2.2 0.0 copy-start.7
  2.3 0.0 copy-start.8
  2.4 1.0 fusion.10
  3.4 0.7 slice.61
  4.2 0.0 copy-done.2
  4.2 0.0 copy-done.12
  4.2 0.1 bitcast_dynamic-update-slice_fusion.wemb
  4.3 0.0 copy-done.11
  4.3 0.0 copy-start
  4.3 0.0 copy-start.9
  4.4 0.0 copy-done.3
  4.4 0.0 copy-done.1
  4.4 0.1 divide_convert_fusion
  4.5 0.0 copy-start.5
  4.5 0.0 copy-start.10
  4.6 0.0 copy-done.6
  4.6 0.0 copy-done.7
  4.6 0.0 copy-done.8
  4.7 0.8 concatenate.10
  5.5 0.0 copy-start.4
  5.5 1.0 copy.30
  6.5 0.0 copy-done.9
  6.5 0.2 copy.31
  6.8 0.0 copy-done
  6.8 0.1 convert_element_type.75
  6.9 0.0 copy-done.5
  7.0 0.1 copy.33
  7.1 0.0 copy-done.10
  7.1 0.2 copy.32
  7.3 0.1 pad.80.clone
  7.4 0.8 maximum_maximum_fusion
  8.2 1.0 copy.34
  9.2 0.0 copy-done.4
  9.2 0.8 copy.35.w_out_final
  10.0 251.6 %forecast.1 = (f32[2,8,64,128]{3,2,1,0:T(8,128)}, f32[2,8,64,128]{3,2,1,0:T(8,128)}) custom-call(bf16[2,8,64,256]{3,2,1,0:T(8,128)(2,1)} %bitcast.58, bf16[2,8,32,128]{3,2,1,0:T(8,128)(2,1)} %bitcast.59, f32[2,8,64,84]{3,2,1,0:T(8,128)} %bitcast.57, f32[4,84]{1,0:T(4,128)} %stats.1, bf16[14,128,512]{2,1,0:T(8,128)(2,1)} %copy-done, ...), custom_call_target="tpu_custom_call" | custom-call | tf_op jit(solution)/shard_map/forecast/pallas_call | solution.py:676
  261.6 2.0 copy.38
  263.6 2.0 copy.39
  (25 shorter events, 0.2 us)
Async XLA Ops:
  0.6 3.6 %copy-start.12 = (pred[128]{0:T(512)(128)(4,1)S(1)}, pred[128]{0:T(512)(128)(4,1)}, u32[]{:S(2)}) copy-start(pred[128]{0:T(512)(128)(4,1)} %constant.3.clone.1) | copy-start | bytes 388
  0.6 3.5 %copy-start.2 = (bf16[178,512]{1,0:T(8,128)(2,1)S(1)}, bf16[178,512]{1,0:T(8,128)(2,1)}, u32[]{:S(2)}) copy-start(bf16[178,512]{1,0:T(8,128)(2,1)} %param.29) | copy-start | bytes 546820
  0.7 3.7 %copy-start.11 = (f32[4,84]{1,0:T(4,128)S(1)}, f32[4,84]{1,0:T(4,128)}, u32[]{:S(2)}) copy-start(f32[4,84]{1,0:T(4,128)} %stats.1) | copy-start | bytes 4036
  0.7 3.7 %copy-start.3 = (f32[1024,84]{0,1:T(8,128)S(1)}, f32[1024,84]{0,1:T(8,128)}, u32[]{:S(2)}) copy-start(f32[1024,84]{0,1:T(8,128)} %param.20) | copy-start | bytes 1032196
  0.7 3.7 %copy-start.1 = (f32[1024,84]{0,1:T(8,128)S(1)}, f32[1024,84]{0,1:T(8,128)}, u32[]{:S(2)}) copy-start(f32[1024,84]{0,1:T(8,128)} %param.21) | copy-start | bytes 1032196
  2.2 2.4 copy-start.6
  2.2 2.4 copy-start.7
  2.3 2.4 copy-start.8
  4.3 2.4 copy-start
  4.3 2.2 copy-start.9
  4.5 2.4 copy-start.5
  4.5 2.6 copy-start.10
  5.5 3.7 %copy-start.4 = (bf16[512,84]{0,1:T(8,128)(2,1)S(1)}, bf16[512,84]{0,1:T(8,128)(2,1)}, u32[]{:S(2)}) copy-start(bf16[512,84]{0,1:T(8,128)(2,1)} %param.39) | copy-start | bytes 258052

commit v3 on v2

--- a/solution.py
+++ b/solution.py
@@ -12,8 +12,12 @@
 
 RUNS = 16
 RUN = 32
+GRID_RUN = 2 * RUN
 ROWS = RUNS * RUN
+ZERO, ONE, LAST = 0, 1, -1
 LAT = 512
+LANES = 128
+PAIR = 2
 VARS = 84
 PAD0 = 32
 PAD1 = 48
@@ -27,10 +31,13 @@
 SLOTS = 4
 FAR = ((2, 1), (3, -1), (4, 4), (5, -4))
 NEAR = ((0, 1), (1, -1))
-ORDER = (
-    "before", "n1", "fx0", "bx0", "fx1", "bx1",
-    "fn0", "fn1", "bn0", "bn1", "ax0", "fx2", "bx2",
-    "ax1", "fx3", "bx3", "na", "ax2", "nb", "an0", "ax3", "project",
+ORDER_A = (
+    "nh", "before", "fx0", "bx0", "n1", "fx1", "bx1", "fn0", "fn1", "bn0", "bn1", "ax0", "fx2", "ax1", "fx3",
+    "bx2", "na", "bx3", "ax2", "nb", "an0", "ax3", "pr", "ps",
+)
+ORDER_B = (
+    "n1", "nh", "fx0", "bx0", "before", "fx1", "bx1", "fn0", "fn1", "bn0", "bn1", "ax0", "fx2", "bx2", "ax1",
+    "fx3", "bx3", "na", "ax2", "nb", "an0", "ax3", "ps", "pr",
 )
 
 
@@ -43,8 +50,8 @@
 
 
 def norm(y):
-    centred = y - jnp.mean(y, axis=-1, keepdims=True)
-    return centred * lax.rsqrt(jnp.mean(centred * centred, axis=-1, keepdims=True) + 1e-5)
+    centred = y - jnp.mean(y, axis=LAST, keepdims=True)
+    return centred * lax.rsqrt(jnp.mean(centred * centred, axis=LAST, keepdims=True) + 1e-5)
 
 
 def ring_place(dev):
@@ -73,21 +80,85 @@
 
 
 def get_tiles(ref, rows):
-    return jnp.concatenate([ref[j, rows, :] for j in range(ref.shape[0])], axis=1)
+    return jnp.concatenate([ref[j, rows, :] for j in range(ref.shape[0])], axis=ONE)
 
 
 def set_tiles(ref, rows, value):
     for j in range(ref.shape[0]):
-        ref[j, rows, :] = value[:, 128 * j:128 * j + 128]
-
-
-def kernel(g_in, mf_in, xc_in, stats, wemb, w_embed_out, w_edge_in, w_edge_out, w_node_in, w_node_out, w_grid_self,
-           w_out_hidden, w_out_final, out0, out1,
-           g_buf, mf_buf, xc_buf, x_buf, gf, feat, we, weo, wself, woh, wof,
+        ref[j, rows, :] = value[:, LANES * j:LANES * j + LANES]
+
+
+def columns(n):
+    return pl.ds(LANES * n, LANES)
+
+
+def stack(ref, n, rows):
+    base = LANES * n
+    end = 0
+    for at_row, value in rows:
+        first = at_row // 8 * 8
+        last = (at_row + value.shape[0]) // 8 * 8
+        if first > end:
+            ref[pl.ds(base + end, first - end), :] = jnp.zeros((first - end, LANES), F32)
+        if last < at_row + value.shape[0]:
+            ref[pl.ds(base + last, 8), :] = jnp.zeros((8, LANES), F32)
+            end = last + 8
+        else:
+            end = last
+        ref[pl.ds(base + at_row, value.shape[0]), :] = value
+    if end < LANES:
+        ref[pl.ds(base + end, LANES - end), :] = jnp.zeros((LANES - end, LANES), F32)
+
+
+def pack_kernel(x_prev, x_cur, forcing, static, g2m_feat, m2g_feat, mesh_feat, mesh_edge_feat, stats, w_out_final,
+                g_home, m_home, x_home, w_final, area):
+    def turned(slot, n):
+        return jnp.transpose(area[slot, pl.ds(LANES * n, LANES), :])
+
+    for n in range(4):
+        stack(area.at[2], n, [(0, mesh_feat[:, columns(n)])] + [(16 + 16 * k, mesh_edge_feat[k, :, columns(n)]) for k in range(6)])
+    for n in range(LAT // LANES):
+        stack(area.at[3], n, [(0, w_out_final[:, columns(n)].astype(F32))])
+    for n in range(8):
+        stack(area.at[0], n, [(0, x_prev[:, columns(n)]), (88, forcing[:, 0, columns(n)]), (96, static[:, columns(n)]),
+                              (104, forcing[:, 1, columns(n)]), (112, m2g_feat[:, columns(n)]), (120, g2m_feat[:, columns(n)])])
+        stack(area.at[1], n, [(0, x_cur[:, columns(n)])])
+    for n in range(4):
+        rows = turned(2, n).astype(BF16)
+        for i in range(4):
+            m_home[n // 2, 4 * (n % 2) + i] = rows[RUN * i:RUN * i + RUN]
+    for n in range(LAT // LANES):
+        w_final[columns(n), :] = turned(3, n).astype(BF16)
+    rest = LANES - VARS
+    wide_mean = jnp.concatenate([stats[0:1, :], jnp.zeros((1, rest), F32)], axis=ONE)
+    wide_std = jnp.concatenate([stats[1:2, :], jnp.ones((1, rest), F32)], axis=ONE)
+    for n in range(8):
+        prev_rows = ((turned(0, n) - wide_mean) / wide_std).astype(BF16)
+        cur = turned(1, n)
+        cur_rows = ((cur - wide_mean) / wide_std).astype(BF16)
+        for i in range(2):
+            t, k, half = n // 4, 2 * (n % 4) + i, slice(GRID_RUN * i, GRID_RUN * i + GRID_RUN)
+            g_home[t, k, :, pl.ds(ZERO, LANES)] = prev_rows[half]
+            g_home[t, k, :, pl.ds(LANES, LANES)] = cur_rows[half]
+            x_home[t, k] = cur[half]
+
+
+def unpack_kernel(home0, home1, out0, out1):
+    for home, out in ((home0, out0), (home1, out1)):
+        for n in range(8):
+            rows = jnp.concatenate([home[n // 4, 2 * (n % 4) + i] for i in range(2)], axis=ZERO)
+            out[:, columns(n)] = jnp.transpose(rows)[:VARS]
+
+
+def kernel(g_home, m_home, x_home, stats, w_grid_in, w_mesh_in,
+           w_eemb_in, w_embed_out, w_edge_in, w_edge_out, w_node_in, w_node_out, w_grid_self, w_out_hidden, w_out_final,
+           out0, out1,
+           wgrid_raw, wmesh_raw, weemb_raw,
+           g_buf, m_buf, x_buf, gf, feat, we, weo, wself, woh, wof,
            enc_ei, enc_eo, enc_ni, enc_no, lay_ei, lay_eo, lay_ni, lay_no,
            edge_base, edge, h_mesh, h, hf, g2m, m2g, v, vc, proj0, proj1, recv, acc, hid, esum, dec, pre_buf,
            send_buf, halo_buf,
-           in_send, in_recv, w_sem, enc_sem, lay_sem, halo_send, halo_recv, out_send, out_recv):
+           raw_sem, in_send, in_recv, w_sem, enc_sem, lay_sem, halo_send, halo_recv, out_send, out_recv):
     me = lax.axis_index("gp")
     place = ring_place(me)
 
@@ -123,12 +194,15 @@
     def layer_weights(step, block):
         return Weights(lay_refs, slot_of(step, block))
 
+    raw = [pltpu.make_async_copy(src, dst, raw_sem.at[i]) for i, (src, dst) in enumerate(
+        ((w_grid_in, wgrid_raw), (w_mesh_in, wmesh_raw), (w_eemb_in, weemb_raw)))]
+    for copy in raw:
+        copy.start()
     small = [
-        pltpu.make_async_copy(wemb, we, w_sem.at[0]),
-        pltpu.make_async_copy(w_embed_out, weo, w_sem.at[1]),
-        pltpu.make_async_copy(w_grid_self, wself, w_sem.at[2]),
-        pltpu.make_async_copy(w_out_hidden, woh, w_sem.at[3]),
-        pltpu.make_async_copy(w_out_final, wof, w_sem.at[4]),
+        pltpu.make_async_copy(w_embed_out, weo, w_sem.at[0]),
+        pltpu.make_async_copy(w_grid_self, wself, w_sem.at[1]),
+        pltpu.make_async_copy(w_out_hidden, woh, w_sem.at[2]),
+        pltpu.make_async_copy(w_out_final, wof, w_sem.at[3]),
     ]
     for copy in small + enc_copies() + layer_copies(0, 1) + layer_copies(0, 2):
         copy.start()
@@ -136,9 +210,8 @@
     barrier = pltpu.get_barrier_semaphore()
     for hop in range(1, RING):
         pl.semaphore_signal(barrier, inc=1, device_id=at(lax.rem(me + hop, RING)), device_id_type=mesh_id)
-    pl.semaphore_wait(barrier, RING - 1)
-
-    parts = ((mf_in, mf_buf), (g_in, g_buf), (xc_in, xc_buf))
+
+    parts = ((m_home, m_buf), (g_home, g_buf), (x_home, x_buf.at[0]))
 
     def in_copy(part, hop):
         src, dst = parts[part]
@@ -152,14 +225,33 @@
                                             device_id_type=mesh_id)
 
     in_copies = [[in_copy(part, hop) for hop in range(RING)] for part in range(3)]
+
+    def wait_in(part):
+        in_copies[part][0].wait()
+        for copy in in_copies[part][1:]:
+            copy.wait_recv()
+
+    pl.semaphore_wait(barrier, RING - 1)
     for part in range(3):
         for copy in in_copies[part]:
             copy.start()
 
-    def wait_in(part):
-        in_copies[part][0].wait()
-        for hop in range(1, RING):
-            in_copies[part][hop].wait_recv()
+    for copy in raw:
+        copy.wait()
+    wide = wgrid_raw[...].astype(F32)
+    recv[pl.ds(ZERO, wide.shape[0]), :] = wide
+    prev_w, cur_w = recv[pl.ds(ZERO, VARS), :], recv[pl.ds(VARS, VARS), :]
+    force_w, static_w = recv[pl.ds(2 * VARS, 5), :], recv[pl.ds(2 * VARS + 5, 5), :]
+    spread = [[(0, wmesh_raw[...].astype(F32))], [(120, weemb_raw[0].astype(F32))], [(112, weemb_raw[1].astype(F32))]]
+    spread += [[(16 + 16 * k, weemb_raw[2].astype(F32))] for k in range(6)]
+    spread += [[(0, prev_w), (88, force_w), (96, static_w)], [(0, cur_w)]]
+    spread += [[(0, cur_w), (96, static_w), (104, force_w)], [(0, prev_w)]]
+    for i, rows in enumerate(spread):
+        base = LANES * (i % 4)
+        acc[pl.ds(base, LANES), :] = jnp.zeros((LANES, LAT), F32)
+        for at_row, value in rows:
+            acc[pl.ds(base + at_row, value.shape[0]), :] = value
+        we[i] = acc[pl.ds(base, LANES), :].astype(BF16)
 
     def pipeline(items):
         depth = max(len(item) for item in items)
@@ -188,42 +280,46 @@
         return [first, last]
 
     wait_in(0)
-    for copy in small[:2]:
-        copy.wait()
-    mesh_feat = [jnp.concatenate([mf_buf[(q + 1) % RUNS].astype(F32)[r:r + n] for q in range(RUNS) for r, n in pieces(t)],
-                                 axis=0).astype(BF16) for t in range(TILES)]
+    small[0].wait()
+    mesh_rows = [jnp.concatenate([m_buf[(q + 1) % RUNS].astype(F32)[r:r + n] for q in range(RUNS) for r, n in pieces(t)],
+                                 axis=ZERO).astype(BF16) for t in range(TILES)]
     items = []
     for t in range(TILES):
         def store_mesh(c, value, t=t):
             h_mesh[part_rows(t, c), :] = value
-        items.append(embed_item(lambda t=t: mesh_feat[t], 0, 1, store_mesh))
-        for p in range(2):
-            def store_g2m(c, value, t=t, p=p):
-                g2m[p, part_rows(t, c), :] = value
-            items.append(embed_item(lambda t=t: mesh_feat[t], 1 + p, 2, store_g2m))
+        items.append(embed_item(lambda t=t: mesh_rows[t], 0, 1, store_mesh))
         for k in range(6):
             def store_edge(c, value, t=t, k=k):
                 edge_base[k, part_rows(t, c), :] = value
-            items.append(embed_item(lambda t=t: mesh_feat[t], 3 + k, 4, store_edge))
+            items.append(embed_item(lambda t=t: mesh_rows[t], 3 + k, 4, store_edge))
     pipeline(items)
 
     wait_in(1)
     for q in range(RUNS):
-        set_tiles(gf, pl.ds(q * 2 * RUN, 2 * RUN), g_buf[q].astype(F32))
+        set_tiles(gf, pl.ds(q * GRID_RUN, GRID_RUN), g_buf[q].astype(F32))
     for t in range(TILES):
-        for p in range(2):
+        for p in range(PAIR):
             for c in chunks():
                 feat[p, part_rows(t, c), :] = jnp.concatenate(
-                    [get_tiles(gf, pl.ds(q * 2 * RUN + 2 * r + p, n, stride=2)) for q in chunk_runs(c) for r, n in pieces(t)],
-                    axis=0).astype(BF16)
+                    [get_tiles(gf, pl.ds(q * GRID_RUN + 2 * r + p, n, stride=2)) for q in chunk_runs(c) for r, n in pieces(t)],
+                    axis=ZERO).astype(BF16)
+
+    def next_run(t, p):
+        lanes = pl.ds(ZERO, LANES)
+        return jnp.concatenate([feat[p, pl.ds(t * TILE + HALF, TILE - HALF), lanes], feat[p, pl.ds(t * TILE, HALF), lanes]],
+                               axis=ZERO)
+
     items = []
     for t in range(TILES):
-        for p in range(2):
+        for p in range(PAIR):
             def store_m2g(c, value, t=t, p=p):
                 m2g[p, part_rows(t, c), :] = value
-            items.append(embed_item(lambda t=t, p=p: feat[p, tile_rows(t), pl.ds(0, 128)], 9, 3, store_m2g))
+            def store_g2m(c, value, t=t, p=p):
+                g2m[p, part_rows(t, c), :] = value
+            items.append(embed_item(lambda t=t, p=p: next_run(t, p), 1, 2, store_g2m))
+            items.append(embed_item(lambda t=t, p=p: feat[p, tile_rows(t), pl.ds(ZERO, LANES)], 2, 3, store_m2g))
     pipeline(items)
-    for copy in small[2:] + enc_copies():
+    for copy in small[1:] + enc_copies():
         copy.wait()
 
     left = ring_place(lax.rem(place + RING - 1, RING))
@@ -238,10 +334,10 @@
         ]
 
     def send_halo(slot):
-        first = get_tiles(hf, pl.ds(0, RUNS, stride=HALF))
+        first = get_tiles(hf, pl.ds(ZERO, RUNS, stride=HALF))
         final = get_tiles(hf, pl.ds(HALF - 1, RUNS, stride=HALF))
-        first_on = jnp.concatenate([first[1:], first[:1]], axis=0)
-        final_back = jnp.concatenate([final[-1:], final[:-1]], axis=0)
+        first_on = jnp.concatenate([first[1:], first[:1]], axis=ZERO)
+        final_back = jnp.concatenate([final[-1:], final[:-1]], axis=ZERO)
         send_buf[0] = jnp.where(place == 0, first_on, first).astype(BF16)
         send_buf[1] = jnp.where(place == RING - 1, final_back, final).astype(BF16)
         for copy in halo_copies(slot):
@@ -252,7 +348,7 @@
             copy.wait()
 
     def project_halo(slot, w):
-        rows = jnp.concatenate([halo_buf[slot, 0], halo_buf[slot, 1]], axis=0)
+        rows = jnp.concatenate([halo_buf[slot, 0], halo_buf[slot, 1]], axis=ZERO)
         out = dot(rows, w.edge[1][...])
         set_tiles(proj1, pl.ds(8 + RUN, RUNS, stride=PAD1), out[:RUNS])
         set_tiles(proj1, pl.ds(7, RUNS, stride=PAD1), out[RUNS:])
@@ -282,7 +378,7 @@
                         got.append(get_tiles(proj0, pl.ds(base * PAD0 + r + self.row_shift, n)))
                     else:
                         got.append(get_tiles(proj1, pl.ds(base * PAD1 + 8 + r + self.row_shift, n)))
-            return jnp.concatenate(got, axis=0) + recv[part_rows(self.t, c), :]
+            return jnp.concatenate(got, axis=ZERO) + recv[part_rows(self.t, c), :]
 
         def fin(self):
             hide(self.slot, self.pre, self.extra)
@@ -305,9 +401,11 @@
         def __init__(self, t, base, w):
             self.t, self.base, self.w, self.slot = t, base, w, 6 + t
 
+        def own(self):
+            self.pre = dot(self.base[tile_rows(self.t), :], self.w.node[0][...])
+
         def a(self):
-            rows = tile_rows(self.t)
-            hide(self.slot, dot(self.base[rows, :], self.w.node[0][...]) + dot(esum[rows, :], self.w.node[1][...]))
+            hide(self.slot, self.pre + dot(esum[tile_rows(self.t), :], self.w.node[1][...]))
 
         def b(self):
             y = dot(hid[self.slot], self.w.node_out[...])
@@ -318,7 +416,7 @@
                 if self.t == 1:
                     set_tiles(hf, pl.ds(c, CH), value.astype(F32))
 
-    def project(t, w):
+    def project_send(t, w):
         out = dot(h[tile_rows(t), :], w.edge[1][...])
         for q in range(RUNS):
             row = q * HALF
@@ -328,12 +426,18 @@
                 else:
                     set_tiles(proj1, pl.ds(q * PAD1 + 8 + r, n), out[row:row + n])
                 row += n
-        back = dot(h[tile_rows(t), :], w.edge[2][...])
-        for c in chunks():
-            recv[part_rows(t, c), :] = back[c:c + CH]
         if t == 1:
             for r in (7, 24):
                 set_tiles(proj0, pl.ds(r, RUNS, stride=PAD0), get_tiles(proj1, pl.ds(8 + r, RUNS, stride=PAD1)))
+
+    def project_recv(t, w):
+        out = dot(h[tile_rows(t), :], w.edge[2][...])
+        for c in chunks():
+            recv[part_rows(t, c), :] = out[c:c + CH]
+
+    def project(t, w):
+        project_send(t, w)
+        project_recv(t, w)
 
     def share_rows():
         for r in (8, 23):
@@ -357,14 +461,15 @@
         pass
 
 
-    def phase(x, n, node, next_x, next_n, before, after):
-        table = {"before": before, "n1": n[1].a, "na": node.a, "nb": node.b, "project": after, "an0": next_n[0].a}
+    def phase(order, x, n, node, next_x, next_n, before, w_next):
+        table = {"before": before, "n1": n[1].a, "nh": node.own, "na": node.a, "nb": node.b, "an0": next_n[0].a,
+                 "ps": lambda: project_send(node.t, w_next), "pr": lambda: project_recv(node.t, w_next)}
         for i in range(4):
             table[f"fx{i}"], table[f"bx{i}"] = x[i].fin, x[i].b
             table[f"ax{i}"] = next_x[i].a if next_x else nothing
         for i in range(2):
             table[f"fn{i}"], table[f"bn{i}"] = n[i].fin, n[i].b
-        for name in ORDER:
+        for name in order:
             table[name]()
 
     def encoder(step):
@@ -381,9 +486,9 @@
                 recv[part_rows(t, c), :] = out[c:c + CH]
         items = []
         for t in range(TILES):
-            for p in range(2):
+            for p in range(PAIR):
                 def in_first(i, t=t, p=p):
-                    hide(i % 2, dot(feat[p, tile_rows(t), :], we[pl.ds(10 + 2 * step, 2)].reshape(256, LAT)))
+                    hide(i % 2, dot(feat[p, tile_rows(t), :], we[pl.ds(9 + 2 * step, 2)].reshape(256, LAT)))
 
                 def in_last(i, t=t, p=p):
                     y = dot(hid[i % 2], weo[0])
@@ -409,7 +514,7 @@
         nodes = [Node(t, h_mesh, w) for t in range(TILES)]
         selfs = []
         for t in range(TILES):
-            for p in range(2):
+            for p in range(PAIR):
                 def self_first(t=t, p=p):
                     hide(4 + p, dot(v[p, tile_rows(t), :], wself[0]))
 
@@ -422,8 +527,10 @@
                 selfs.append((self_first, self_last))
         y = far_items(0, w1, edge_base)
         x = far_items(1, w1)
+        nodes[0].own()
         nodes[0].a()
         selfs[0][0]()
+        nodes[1].own()
         nodes[1].a()
         selfs[1][0]()
         nodes[0].b()
@@ -470,11 +577,10 @@
         w = layer_weights(step, BLOCKS - 1)
         in_mean = stats[0:1, :]
         in_std = stats[1:2, :]
-        diff_mean = stats[2:3, :]
-        diff_std = stats[3:4, :]
+        diff_mean, diff_std = (jnp.concatenate([stats[i:i + 1, :], jnp.zeros((1, LANES - VARS), F32)], axis=ONE) for i in (2, 3))
         items = []
         for t in range(TILES):
-            for p in range(2):
+            for p in range(PAIR):
                 def edge_first(i, t=t, p=p):
                     if p == 0 and t == 0:
                         for q in range(RUNS):
@@ -508,14 +614,14 @@
                     pred = dot(hid[4 + i % 2], wof[...])
                     for c in chunks():
                         spots = [(q, pl.ds(2 * r + p, n, stride=2), n) for q in chunk_runs(c) for r, n in pieces(t)]
-                        now = jnp.concatenate([x_buf[step, q, rows, :] for q, rows, n in spots], axis=0)[:, :VARS]
+                        now = jnp.concatenate([x_buf[step, q, rows, :] for q, rows, n in spots], axis=ZERO)
                         new = now + diff_std * pred[c:c + CH] + diff_mean
-                        wide = jnp.concatenate([new, jnp.zeros((CH, 128 - VARS), F32)], axis=1)
                         row = 0
                         for q, rows, n in spots:
-                            x_buf[step + 1, q, rows, :] = wide[row:row + n]
+                            x_buf[step + 1, q, rows, :] = new[row:row + n]
                             row += n
-                        feat[p, part_rows(t, c), pl.ds(0, VARS)] = ((new - in_mean) / in_std).astype(BF16)
+                        scaled = (new[:, :VARS] - in_mean) / in_std
+                        feat[p, part_rows(t, c), pl.ds(ZERO, VARS)] = scaled.astype(BF16)
 
                 items.append([edge_first, edge_last, node_first, node_last, out_first, out_last])
         return items
@@ -542,11 +648,11 @@
                 start_all(layer_copies(step, block + 3))
 
             w, w1, w2 = (layer_weights(step, block + i) for i in range(3))
-            phase(far_items(1, w, resume=True), near_items(0, w, resume=True), Node(0, h, w), far_items(1, w1),
-                  near_items(1, w), share_rows, lambda: project(0, w1))
+            phase(ORDER_A, far_items(1, w, resume=True), near_items(0, w, resume=True), Node(0, h, w), far_items(1, w1),
+                  near_items(1, w), share_rows, w1)
             wait_halo(halo_slot)
-            phase(far_items(0, w1, resume=True), near_items(1, w, resume=True), Node(1, h, w), far_items(0, w2),
-                  near_items(0, w1), lambda: project_halo(halo_slot, w), lambda: project(1, w1))
+            phase(ORDER_B, far_items(0, w1, resume=True), near_items(1, w, resume=True), Node(1, h, w), far_items(0, w2),
+                  near_items(0, w1), lambda: project_halo(halo_slot, w), w1)
             send_halo(1 - halo_slot)
             return carry
 
@@ -555,15 +661,11 @@
         def _():
             start_all(layer_copies(1, 1) + layer_copies(1, 2))
             wait_in(2)
-            for q in range(RUNS):
-                x_buf[0, q, :, pl.ds(0, VARS)] = xc_buf[q]
-                x_buf[0, q, :, pl.ds(VARS, 128 - VARS)] = jnp.zeros((2 * RUN, 128 - VARS), F32)
 
         w = layer_weights(step, LAYERS)
         w_last = layer_weights(step, BLOCKS - 1)
         n1 = near_items(1, w)
-        phase(far_items(1, w, resume=True), near_items(0, w, resume=True), Node(0, h, w), None, n1, share_rows,
-              lambda: project(0, w_last))
+        phase(ORDER_A, far_items(1, w, resume=True), near_items(0, w, resume=True), Node(0, h, w), None, n1, share_rows, w_last)
         n1[1].a()
         wait_halo(lax.rem(LAYERS + 1, 2))
         project_halo(lax.rem(LAYERS + 1, 2), w)
@@ -572,25 +674,22 @@
             item.fin()
         for item in n1:
             item.b()
+        last.own()
         last.a()
         last.b()
         pipeline(decoder_items(step))
 
-        @pl.when(step == 0)
-        def _():
-            start_all(out_copies(0, out0))
-
-        @pl.when(step == 1)
-        def _():
-            start_all(out_copies(1, out1))
+        for which, out in ((0, out0), (1, out1)):
+            @pl.when(step == which)
+            def _():
+                start_all(out_copies(which, out))
         return carry
 
     lax.fori_loop(0, 2, one_step, 0)
     for part in range(3):
-        for hop in range(1, RING):
-            in_copies[part][hop].wait_send()
-    for step, out in ((0, out0), (1, out1)):
-        wait_all(out_copies(step, out))
+        for copy in in_copies[part][1:]:
+            copy.wait_send()
+    wait_all(out_copies(0, out0) + out_copies(1, out1))
 
 
 def solution(mesh):
@@ -601,48 +700,35 @@
     def local_run(x_prev, x_cur, forcing, grid_static, g2m_feat, m2g_feat, mesh_feat, mesh_edge_feat, norm_stats,
                   w_grid_in, w_mesh_in, w_eemb_in, w_embed_out, w_edge_in, w_edge_out, w_node_in, w_node_out,
                   w_grid_self, w_out_hidden, w_out_final):
-        grid_dev = x_prev.shape[0]
-        mesh_dev = mesh_feat.shape[0]
-        mean, std = norm_stats[0], norm_stats[1]
-
-        def lanes(pieces, width):
-            have = sum(piece.shape[1] for piece in pieces)
-            rows = pieces[0].shape[0]
-            return jnp.concatenate([piece.astype(BF16) for piece in pieces] + [jnp.zeros((rows, width - have), BF16)], axis=1)
-
-        grid_lanes = jnp.concatenate([
-            lanes([(x_prev - mean) / std, forcing[:, 0], grid_static, forcing[:, 1], m2g_feat], 128),
-            lanes([(x_cur - mean) / std], 128)], axis=1)
-        mesh_lanes = lanes([mesh_feat, mesh_edge_feat.reshape(mesh_dev, 24), g2m_feat.reshape(mesh_dev, 8)], 128)
-
-        def placed(rows, start, height=128):
-            return jnp.pad(rows, ((start, height - start - rows.shape[0]), (0, 0)))
-
-        prev_rows, cur_rows = w_grid_in[:VARS], w_grid_in[VARS:2 * VARS]
-        force_rows, static_rows = w_grid_in[2 * VARS:2 * VARS + 5], w_grid_in[2 * VARS + 5:]
-        first_step = [placed(jnp.concatenate([prev_rows, force_rows, static_rows], axis=0), 0), placed(cur_rows, 0)]
-        second_step = [placed(cur_rows, 0) + placed(static_rows, 89) + placed(force_rows, 94), placed(prev_rows, 0)]
-        wemb = jnp.stack(
-            [placed(w_mesh_in, 0)] + [placed(w_eemb_in[0], 27 + 4 * p) for p in range(2)]
-            + [placed(w_eemb_in[2], 3 + 4 * k) for k in range(6)] + [placed(w_eemb_in[1], 99)]
-            + first_step + second_step)
-
         any_spec = pl.BlockSpec(memory_space=pl.ANY)
         vmem_spec = pl.BlockSpec(memory_space=pltpu.VMEM)
         dma = pltpu.SemaphoreType.DMA
-        out = jax.ShapeDtypeStruct((2, RING, 2 * RUN, 128), F32)
+        grid_dev = x_prev.shape[0]
+        shape = jax.ShapeDtypeStruct
+        home = shape((PAIR, RING, GRID_RUN, LANES), F32)
+        g_home, m_home, x_home, w_final = pl.pallas_call(
+            pack_kernel,
+            out_shape=(shape((PAIR, RING, GRID_RUN, 256), BF16), shape((PAIR, RING, RUN, LANES), BF16), home, shape((LAT, LANES), BF16)),
+            in_specs=[vmem_spec] * 10,
+            out_specs=(vmem_spec,) * 4,
+            scratch_shapes=[pltpu.VMEM((4, grid_dev, LANES), F32)],
+            name="pack",
+        )(x_prev.T, x_cur.T, forcing.T, grid_static.T, g2m_feat.T, m2g_feat.T, mesh_feat.T,
+          jnp.transpose(mesh_edge_feat, (1, 2, 0)), norm_stats, w_out_final.T)
         scratch = [
-            pltpu.VMEM((RUNS, 2 * RUN, 256), BF16),
-            pltpu.VMEM((RUNS, RUN, 128), BF16),
-            pltpu.VMEM((RUNS, 2 * RUN, VARS), F32),
-            pltpu.VMEM((3, RUNS, 2 * RUN, 128), F32),
-            pltpu.VMEM((2, RUNS * 2 * RUN, 128), F32),
-            pltpu.VMEM((2, ROWS, 256), BF16),
-            pltpu.VMEM((14, 128, LAT), BF16),
+            pltpu.VMEM((2 * VARS + 10, LAT), BF16),
+            pltpu.VMEM((3, LAT), BF16),
+            pltpu.VMEM((3, 4, LAT), BF16),
+            pltpu.VMEM((RUNS, GRID_RUN, 256), BF16),
+            pltpu.VMEM((RUNS, RUN, LANES), BF16),
+            pltpu.VMEM((3, RUNS, GRID_RUN, LANES), F32),
+            pltpu.VMEM((PAIR, RUNS * GRID_RUN, LANES), F32),
+            pltpu.VMEM((PAIR, ROWS, 256), BF16),
+            pltpu.VMEM((13, LANES, LAT), BF16),
             pltpu.VMEM((5, LAT, LAT), BF16),
-            pltpu.VMEM((2, LAT, LAT), BF16),
+            pltpu.VMEM((PAIR, LAT, LAT), BF16),
             pltpu.VMEM((LAT, LAT), BF16),
-            pltpu.VMEM((LAT, VARS), BF16),
+            pltpu.VMEM((LAT, LANES), BF16),
             pltpu.VMEM((1, 3 * LAT, LAT), BF16),
             pltpu.VMEM((1, LAT, LAT), BF16),
             pltpu.VMEM((1, 2 * LAT, LAT), BF16),
@@ -655,36 +741,39 @@
             pltpu.VMEM((6, ROWS, LAT), BF16),
             pltpu.VMEM((ROWS, LAT), BF16),
             pltpu.VMEM((ROWS, LAT), BF16),
-            pltpu.VMEM((LAT // 128, TILE, 128), F32),
-            pltpu.VMEM((2, ROWS, LAT), BF16),
-            pltpu.VMEM((2, ROWS, LAT), BF16),
-            pltpu.VMEM((2, ROWS, LAT), BF16),
-            pltpu.VMEM((2, ROWS, LAT), BF16),
-            pltpu.VMEM((LAT // 128, RUNS * PAD0, 128), F32),
-            pltpu.VMEM((LAT // 128, RUNS * PAD1, 128), F32),
+            pltpu.VMEM((LAT // LANES, TILE, LANES), F32),
+            pltpu.VMEM((PAIR, ROWS, LAT), BF16),
+            pltpu.VMEM((PAIR, ROWS, LAT), BF16),
+            pltpu.VMEM((PAIR, ROWS, LAT), BF16),
+            pltpu.VMEM((PAIR, ROWS, LAT), BF16),
+            pltpu.VMEM((LAT // LANES, RUNS * PAD0, LANES), F32),
+            pltpu.VMEM((LAT // LANES, RUNS * PAD1, LANES), F32),
             pltpu.VMEM((ROWS, LAT), F32),
             pltpu.VMEM((ROWS, LAT), F32),
             pltpu.VMEM((8, TILE, LAT), BF16),
             pltpu.VMEM((ROWS, LAT), BF16),
-            pltpu.VMEM((2, TILE, LAT), BF16),
+            pltpu.VMEM((PAIR, TILE, LAT), BF16),
             pltpu.VMEM((10, TILE, LAT), F32),
-            pltpu.VMEM((2, RUNS, LAT), BF16),
-            pltpu.VMEM((2, 2, RUNS, LAT), BF16),
-            dma((3, RING)), dma((3, RING)), dma((5,)), dma((1, 4)), dma((SLOTS, 4)), dma((2,)), dma((2, 2)),
+            pltpu.VMEM((PAIR, RUNS, LAT), BF16),
+            pltpu.VMEM((PAIR, 2, RUNS, LAT), BF16),
+            dma((3,)), dma((3, RING)), dma((3, RING)), dma((4,)), dma((1, 4)), dma((SLOTS, 4)), dma((2,)), dma((2, 2)),
             dma((2, RING)), dma((2, RING)),
         ]
-        next_state, after_state = pl.pallas_call(
+        home0, home1 = pl.pallas_call(
             kernel,
-            out_shape=(out, out),
-            in_specs=[any_spec, any_spec, any_spec, vmem_spec] + [any_spec] * 9,
+            out_shape=(home, home),
+            in_specs=[any_spec] * 3 + [vmem_spec] + [any_spec] * 11,
             out_specs=(any_spec, any_spec),
             scratch_shapes=scratch,
-            compiler_params=pltpu.CompilerParams(collective_id=0, has_side_effects=True, vmem_limit_bytes=60 << 20),
+            compiler_params=pltpu.CompilerParams(collective_id=0, has_side_effects=True, vmem_limit_bytes=63 << 20),
             name="forecast",
-        )(grid_lanes.reshape(2, RING, 2 * RUN, 256), mesh_lanes.reshape(2, RING, RUN, 128),
-          x_cur.reshape(2, RING, 2 * RUN, VARS), norm_stats, wemb, w_embed_out, w_edge_in, w_edge_out, w_node_in,
-          w_node_out, w_grid_self, w_out_hidden, w_out_final)
-        return next_state.reshape(grid_dev, 128)[:, :VARS], after_state.reshape(grid_dev, 128)[:, :VARS]
+        )(g_home, m_home, x_home, norm_stats, w_grid_in, w_mesh_in, w_eemb_in, w_embed_out, w_edge_in, w_edge_out, w_node_in,
+          w_node_out, w_grid_self, w_out_hidden, w_final)
+        out = shape((VARS, grid_dev), F32)
+        next_state, after_state = pl.pallas_call(
+            unpack_kernel, out_shape=(out, out), in_specs=[vmem_spec] * 2, out_specs=(vmem_spec,) * 2, name="unpack",
+        )(home0, home1)
+        return next_state.T, after_state.T
 
     in_specs = (row_spec, row_spec, edge_spec, row_spec, row_spec, row_spec, row_spec, edge_spec, whole) + (whole,) * 11
     return jax.shard_map(local_run, mesh=mesh, in_specs=in_specs, out_specs=(row_spec, row_spec), check_vma=False)

time: 266 us -> 254 us (0.955)
  local copies, waits for them, and re-layouts: 11.8 us -> 0 us
    unnamed x42 -> x0, local copies, waits for them, and re-layouts: 6.67 us -> none
    pallas_call x1 -> x3, Pallas kernels: 252 us -> 253 us  [the longest x1 248 us: local_run(): pl.pallas_call(kernel, out_shape=(home, home), in_specs=[any_spec] * 3 +...]
where the time goes in v3:
time: 254 us
  Pallas kernels  253 us (100%)
    pallas_call x1, Pallas kernels, local_run(): pl.pallas_call(kernel, out_shape=(home, home), in_specs=[any_spec] * 3 +...  248 us

profile of v3, /device:TPU:0, one launch (start us, length us, event | category | flops | bytes accessed | tf_op | source)
XLA Modules:
  0.0 253.8 jit_solution(15366428508879301037)
XLA Ops:
  0.6 2.6 %pack.1 = (bf16[2,8,64,256]{3,2,1,0:T(8,128)(2,1)}, bf16[2,8,32,128]{3,2,1,0:T(8,128)(2,1)}, f32[2,8,64,128]{3,2,1,0:T(8,128)}, bf16[512,128]{1,0:T(8,128)(2,1)}) custom-call(f32[84,1024]{1,0:T(8,128)} %bitcast.11, f32[84,1024]{1,0:T(8,128)} %bitcast.12, f32[5,2,1024]{2,1,0:T(2,128)} %bitcast.15, f32[5,1024]{1,0:T(8,128)} %bitcast.16, f32[4,1024]{1,0:T(4,128)} %bitcast.17, ...), custom_call_target="tpu_custom_call" | custom-call | tf_op jit(solution)/shard_map/pack/pallas_call | solution.py:709
  3.3 248.3 %forecast.1 = (f32[2,8,64,128]{3,2,1,0:T(8,128)}, f32[2,8,64,128]{3,2,1,0:T(8,128)}) custom-call(bf16[2,8,64,256]{3,2,1,0:T(8,128)(2,1)} %get-tuple-element.10.g_home, bf16[2,8,32,128]{3,2,1,0:T(8,128)(2,1)} %get-tuple-element.11.m_home, f32[2,8,64,128]{3,2,1,0:T(8,128)} %get-tuple-element.12.x_home, f32[4,84]{1,0:T(4,128)} %stats.3, ...), custom_call_target="tpu_custom_call" | custom-call | tf_op jit(solution)/shard_map/forecast/pallas_call | solution.py:762
  251.5 2.3 unpack.1

commit v4 on v3

--- a/solution.py
+++ b/solution.py
@@ -33,11 +33,24 @@
 NEAR = ((0, 1), (1, -1))
 ORDER_A = (
     "nh", "before", "fx0", "bx0", "n1", "fx1", "bx1", "fn0", "fn1", "bn0", "bn1", "ax0", "fx2", "ax1", "fx3",
-    "bx2", "na", "bx3", "ax2", "nb", "an0", "ax3", "pr", "ps",
+    "bx2", "na", "bx3", "ax2", "nb", "an0", "ax3", "ps", "pr",
 )
 ORDER_B = (
-    "n1", "nh", "fx0", "bx0", "before", "fx1", "bx1", "fn0", "fn1", "bn0", "bn1", "ax0", "fx2", "bx2", "ax1",
-    "fx3", "bx3", "na", "ax2", "nb", "an0", "ax3", "ps", "pr",
+    "nh", "before", "fx0", "bx0", "n1", "fx1", "bx1", "fn0", "fn1", "bn0", "bn1", "ax0", "fx2", "ax1", "fx3",
+    "bx2", "na", "bx3", "ax2", "nb", "an0", "ax3", "ps", "pr",
+)
+ORDER_E = (
+    "copy", "r0", "va0", "va1", "r1", "vb0", "va2", "vb1", "va3", "vb2", "vb3", "ea0", "sa0", "ea1", "eb0",
+    "sa1", "eb1", "ea2", "sb0", "ea3", "sb1", "nh0", "na0", "eb2", "sa2", "eb3", "nb0", "sa3", "sb2", "sb3",
+    "ya0", "nh1", "na1", "ps0", "pr0", "ya1", "ya2", "nb1", "yf0", "yb0", "yf1", "yb1", "ya3", "ps1", "pr1",
+    "yf2", "yb2", "yf3", "yb3", "xa0", "xa1", "xa2", "xa3", "za0", "za1", "za2", "za3", "n0", "share", "send",
+)
+ORDER_D = (
+    "share", "nh0", "fx0", "bx0", "n01", "fx1", "bx1", "fn00", "fn01", "bn00", "bn01", "em0", "fx2", "bx2",
+    "fx3", "bx3", "na0", "em1", "nb0", "n10", "n11", "dm0", "t0", "wait", "halo", "ea0", "fn10", "fn11",
+    "bn10", "bn11", "ea1", "eb0", "eb1", "nh1", "na1", "dm1", "em2", "da0", "nb1", "da1", "dm2", "em3", "db0",
+    "t1", "db1", "dm3", "oa0", "ea2", "oa1", "eb2", "ob0", "ea3", "ob1", "send0", "eb3", "da2", "da3", "db2",
+    "db3", "oa2", "oa3", "ob2", "ob3", "send1",
 )
 
 
@@ -86,6 +99,10 @@
 def set_tiles(ref, rows, value):
     for j in range(ref.shape[0]):
         ref[j, rows, :] = value[:, LANES * j:LANES * j + LANES]
+
+
+AT_FORCE, AT_STATIC, AT_NEXT, AT_M2G, AT_G2M = 88, 96, 104, 112, 120
+PREV_AREA, CUR_AREA, NORM_AREA, MESH_AREA, OUT_AREA = range(5)
 
 
 def columns(n):
@@ -113,48 +130,71 @@
 def pack_kernel(x_prev, x_cur, forcing, static, g2m_feat, m2g_feat, mesh_feat, mesh_edge_feat, stats, w_out_final,
                 g_home, m_home, x_home, w_final, area):
     def turned(slot, n):
-        return jnp.transpose(area[slot, pl.ds(LANES * n, LANES), :])
-
-    for n in range(4):
-        stack(area.at[2], n, [(0, mesh_feat[:, columns(n)])] + [(16 + 16 * k, mesh_edge_feat[k, :, columns(n)]) for k in range(6)])
-    for n in range(LAT // LANES):
-        stack(area.at[3], n, [(0, w_out_final[:, columns(n)].astype(F32))])
-    for n in range(8):
-        stack(area.at[0], n, [(0, x_prev[:, columns(n)]), (88, forcing[:, 0, columns(n)]), (96, static[:, columns(n)]),
-                              (104, forcing[:, 1, columns(n)]), (112, m2g_feat[:, columns(n)]), (120, g2m_feat[:, columns(n)])])
-        stack(area.at[1], n, [(0, x_cur[:, columns(n)])])
-    for n in range(4):
-        rows = turned(2, n).astype(BF16)
-        for i in range(4):
-            m_home[n // 2, 4 * (n % 2) + i] = rows[RUN * i:RUN * i + RUN]
-    for n in range(LAT // LANES):
-        w_final[columns(n), :] = turned(3, n).astype(BF16)
+        return jnp.transpose(area[slot, columns(n), :])
+
+    blocks = range(x_cur.shape[1] // LANES)
+    mesh_blocks = range(mesh_feat.shape[1] // LANES)
+    weight_blocks = range(LAT // LANES)
+    for n in mesh_blocks:
+        stack(area.at[MESH_AREA], n, [(ZERO, mesh_feat[:, columns(n)])] + [
+            (16 + 16 * k, mesh_edge_feat[k, :, columns(n)]) for k in range(6)])
+    for n in weight_blocks:
+        stack(area.at[OUT_AREA], n, [(ZERO, w_out_final[:, columns(n)].astype(F32))])
+    for n in blocks:
+        stack(area.at[PREV_AREA], n, [
+            (ZERO, x_prev[:, columns(n)]), (AT_FORCE, forcing[:, ZERO, columns(n)]), (AT_STATIC, static[:, columns(n)]),
+            (AT_NEXT, forcing[:, ONE, columns(n)]), (AT_M2G, m2g_feat[:, columns(n)]), (AT_G2M, g2m_feat[:, columns(n)])])
+        stack(area.at[CUR_AREA], n, [(ZERO, x_cur[:, columns(n)])])
+    for n in mesh_blocks:
+        turned_rows = turned(MESH_AREA, n)
+        for i in range(LANES // RUN):
+            band, k = divmod(n * LANES + i * RUN, RING * RUN)
+            for t in range(TILES):
+                m_home[k // RUN, t, band] = jnp.concatenate(
+                    [turned_rows[i * RUN + r:i * RUN + r + rows] for r, rows in pieces(t)], axis=ZERO).astype(BF16)
+    for n in weight_blocks:
+        w_final[columns(n), :] = turned(OUT_AREA, n).astype(BF16)
     rest = LANES - VARS
-    wide_mean = jnp.concatenate([stats[0:1, :], jnp.zeros((1, rest), F32)], axis=ONE)
-    wide_std = jnp.concatenate([stats[1:2, :], jnp.ones((1, rest), F32)], axis=ONE)
-    for n in range(8):
-        prev_rows = ((turned(0, n) - wide_mean) / wide_std).astype(BF16)
-        cur = turned(1, n)
-        cur_rows = ((cur - wide_mean) / wide_std).astype(BF16)
-        for i in range(2):
-            t, k, half = n // 4, 2 * (n % 4) + i, slice(GRID_RUN * i, GRID_RUN * i + GRID_RUN)
-            g_home[t, k, :, pl.ds(ZERO, LANES)] = prev_rows[half]
-            g_home[t, k, :, pl.ds(LANES, LANES)] = cur_rows[half]
-            x_home[t, k] = cur[half]
-
-
-def unpack_kernel(home0, home1, out0, out1):
+    wide_mean = jnp.concatenate([stats[ZERO:ONE, :], jnp.zeros((ONE, rest), F32)], axis=ONE)
+    wide_std = jnp.concatenate([stats[ONE:PAIR, :], jnp.ones((ONE, rest), F32)], axis=ONE)
+    for n in blocks:
+        prev, cur = turned(PREV_AREA, n), turned(CUR_AREA, n)
+        area[PREV_AREA, columns(n), :] = (prev - wide_mean) / wide_std
+        area[CUR_AREA, columns(n), :] = cur
+        area[NORM_AREA, columns(n), :] = (cur - wide_mean) / wide_std
+    for band in range(PAIR):
+        for k in range(RING):
+            base = (band * RING + k) * GRID_RUN
+            for p in range(PAIR):
+                for t in range(TILES):
+                    def rows_of(slot):
+                        return jnp.concatenate([area[slot, pl.ds(base + PAIR * r + p, rows, stride=PAIR), :]
+                                                for r, rows in pieces(t)], axis=ZERO)
+                    g_home[k, p, t, band, :, pl.ds(ZERO, LANES)] = rows_of(PREV_AREA).astype(BF16)
+                    g_home[k, p, t, band, :, pl.ds(LANES, LANES)] = rows_of(NORM_AREA).astype(BF16)
+                    x_home[k, p, t, band] = rows_of(CUR_AREA)
+
+
+def unpack_kernel(home0, home1, out0, out1, area):
     for home, out in ((home0, out0), (home1, out1)):
-        for n in range(8):
-            rows = jnp.concatenate([home[n // 4, 2 * (n % 4) + i] for i in range(2)], axis=ZERO)
-            out[:, columns(n)] = jnp.transpose(rows)[:VARS]
+        for band in range(PAIR):
+            for k in range(RING):
+                for p in range(PAIR):
+                    for t in range(TILES):
+                        row = 0
+                        for r, rows in pieces(t):
+                            spot = pl.ds((band * RING + k) * GRID_RUN + PAIR * r + p, rows, stride=PAIR)
+                            area[spot, :] = home[k, p, t, band, pl.ds(row, rows), :]
+                            row += rows
+        for n in range(out.shape[1] // LANES):
+            out[:, columns(n)] = jnp.transpose(area[columns(n), :])[:VARS]
 
 
 def kernel(g_home, m_home, x_home, stats, w_grid_in, w_mesh_in,
            w_eemb_in, w_embed_out, w_edge_in, w_edge_out, w_node_in, w_node_out, w_grid_self, w_out_hidden, w_out_final,
            out0, out1,
            wgrid_raw, wmesh_raw, weemb_raw,
-           g_buf, m_buf, x_buf, gf, feat, we, weo, wself, woh, wof,
+           m_buf, x_buf, feat, we, weo, wself, woh, wof,
            enc_ei, enc_eo, enc_ni, enc_no, lay_ei, lay_eo, lay_ni, lay_no,
            edge_base, edge, h_mesh, h, hf, g2m, m2g, v, vc, proj0, proj1, recv, acc, hid, esum, dec, pre_buf,
            send_buf, halo_buf,
@@ -211,15 +251,15 @@
     for hop in range(1, RING):
         pl.semaphore_signal(barrier, inc=1, device_id=at(lax.rem(me + hop, RING)), device_id_type=mesh_id)
 
-    parts = ((m_home, m_buf), (g_home, g_buf), (x_home, x_buf.at[0]))
+    mine = pl.ds(PAIR * me, PAIR)
+    parts = ((m_home, m_buf.at[:, mine]), (g_home, feat.at[:, :, mine]), (x_home, x_buf.at[ZERO, :, :, mine]))
 
     def in_copy(part, hop):
         src, dst = parts[part]
         target = lax.rem(me + hop, RING)
-        src = src.at[:, ring_place(target)]
-        dst = dst.at[pl.ds(2 * me, 2)]
+        src = src.at[ring_place(target)]
         if hop == 0:
-            return pltpu.make_async_copy(src, dst, in_recv.at[part, 0])
+            return pltpu.make_async_copy(src, dst, in_recv.at[part, hop])
         return pltpu.make_async_remote_copy(src_ref=src, dst_ref=dst, send_sem=in_send.at[part, hop],
                                             recv_sem=in_recv.at[part, hop], device_id=at(target),
                                             device_id_type=mesh_id)
@@ -231,10 +271,13 @@
         for copy in in_copies[part][1:]:
             copy.wait_recv()
 
-    pl.semaphore_wait(barrier, RING - 1)
-    for part in range(3):
+    def start_in(part):
         for copy in in_copies[part]:
             copy.start()
+
+    pl.semaphore_wait(barrier, RING - 1)
+    start_in(0)
+    start_in(1)
 
     for copy in raw:
         copy.wait()
@@ -242,10 +285,10 @@
     recv[pl.ds(ZERO, wide.shape[0]), :] = wide
     prev_w, cur_w = recv[pl.ds(ZERO, VARS), :], recv[pl.ds(VARS, VARS), :]
     force_w, static_w = recv[pl.ds(2 * VARS, 5), :], recv[pl.ds(2 * VARS + 5, 5), :]
-    spread = [[(0, wmesh_raw[...].astype(F32))], [(120, weemb_raw[0].astype(F32))], [(112, weemb_raw[1].astype(F32))]]
+    spread = [[(0, wmesh_raw[...].astype(F32))], [(AT_G2M, weemb_raw[0].astype(F32))], [(AT_M2G, weemb_raw[1].astype(F32))]]
     spread += [[(16 + 16 * k, weemb_raw[2].astype(F32))] for k in range(6)]
-    spread += [[(0, prev_w), (88, force_w), (96, static_w)], [(0, cur_w)]]
-    spread += [[(0, cur_w), (96, static_w), (104, force_w)], [(0, prev_w)]]
+    spread += [[(0, prev_w), (AT_FORCE, force_w), (AT_STATIC, static_w)], [(0, cur_w)]]
+    spread += [[(0, cur_w), (AT_STATIC, static_w), (AT_NEXT, force_w)], [(0, prev_w)]]
     for i, rows in enumerate(spread):
         base = LANES * (i % 4)
         acc[pl.ds(base, LANES), :] = jnp.zeros((LANES, LAT), F32)
@@ -270,7 +313,7 @@
 
     def embed_item(load, w_first, second, store):
         def first(i):
-            hide(i % 2, dot(load(), we[w_first]))
+            hide(i % PAIR, dot(load(), we[w_first]))
 
         def last(i):
             y = dot(hid[i % 2], weo[second])
@@ -281,8 +324,12 @@
 
     wait_in(0)
     small[0].wait()
-    mesh_rows = [jnp.concatenate([m_buf[(q + 1) % RUNS].astype(F32)[r:r + n] for q in range(RUNS) for r, n in pieces(t)],
-                                 axis=ZERO).astype(BF16) for t in range(TILES)]
+    def next_run(ref, *index):
+        first = ref[(*index, pl.ds(ONE, RUNS - 1), slice(None), pl.ds(ZERO, LANES))]
+        last = ref[(*index, pl.ds(ZERO, ONE), slice(None), pl.ds(ZERO, LANES))]
+        return jnp.concatenate([first, last], axis=ZERO).reshape(TILE, LANES)
+
+    mesh_rows = [next_run(m_buf, t) for t in range(TILES)]
     items = []
     for t in range(TILES):
         def store_mesh(c, value, t=t):
@@ -295,20 +342,7 @@
     pipeline(items)
 
     wait_in(1)
-    for q in range(RUNS):
-        set_tiles(gf, pl.ds(q * GRID_RUN, GRID_RUN), g_buf[q].astype(F32))
-    for t in range(TILES):
-        for p in range(PAIR):
-            for c in chunks():
-                feat[p, part_rows(t, c), :] = jnp.concatenate(
-                    [get_tiles(gf, pl.ds(q * GRID_RUN + 2 * r + p, n, stride=2)) for q in chunk_runs(c) for r, n in pieces(t)],
-                    axis=ZERO).astype(BF16)
-
-    def next_run(t, p):
-        lanes = pl.ds(ZERO, LANES)
-        return jnp.concatenate([feat[p, pl.ds(t * TILE + HALF, TILE - HALF), lanes], feat[p, pl.ds(t * TILE, HALF), lanes]],
-                               axis=ZERO)
-
+    start_in(PAIR)
     items = []
     for t in range(TILES):
         for p in range(PAIR):
@@ -316,8 +350,8 @@
                 m2g[p, part_rows(t, c), :] = value
             def store_g2m(c, value, t=t, p=p):
                 g2m[p, part_rows(t, c), :] = value
-            items.append(embed_item(lambda t=t, p=p: next_run(t, p), 1, 2, store_g2m))
-            items.append(embed_item(lambda t=t, p=p: feat[p, tile_rows(t), pl.ds(ZERO, LANES)], 2, 3, store_m2g))
+            items.append(embed_item(lambda t=t, p=p: next_run(feat, p, t), 1, 2, store_g2m))
+            items.append(embed_item(lambda t=t, p=p: feat[p, t, :, :, pl.ds(ZERO, LANES)].reshape(TILE, LANES), 2, 3, store_m2g))
     pipeline(items)
     for copy in small[1:] + enc_copies():
         copy.wait()
@@ -457,50 +491,64 @@
             items[0].resume()
         return items
 
-    def nothing():
-        pass
-
-
     def phase(order, x, n, node, next_x, next_n, before, w_next):
         table = {"before": before, "n1": n[1].a, "nh": node.own, "na": node.a, "nb": node.b, "an0": next_n[0].a,
                  "ps": lambda: project_send(node.t, w_next), "pr": lambda: project_recv(node.t, w_next)}
         for i in range(4):
-            table[f"fx{i}"], table[f"bx{i}"] = x[i].fin, x[i].b
-            table[f"ax{i}"] = next_x[i].a if next_x else nothing
-        for i in range(2):
+            table[f"fx{i}"], table[f"bx{i}"], table[f"ax{i}"] = x[i].fin, x[i].b, next_x[i].a
+        for i in range(PAIR):
             table[f"fn{i}"], table[f"bn{i}"] = n[i].fin, n[i].b
+        run(order, table)
+
+    def run(order, table):
         for name in order:
             table[name]()
 
     def encoder(step):
-        w = Weights(enc_refs, 0)
+        w = Weights(enc_refs, ZERO)
         w1 = layer_weights(step, 1)
         w2 = layer_weights(step, 2)
-        for k in range(6):
-            for t in range(TILES):
-                if t == 1 or k < 2:
-                    edge[k, tile_rows(t), :] = edge_base[k, tile_rows(t), :]
+        table = {"send": lambda: send_halo(ZERO), "share": share_rows}
+
+        def spread():
+            for k in range(6):
+                for t in range(TILES):
+                    if t == 1 or k < PAIR:
+                        edge[k, tile_rows(t), :] = edge_base[k, tile_rows(t), :]
+
+        table["copy"] = spread
+        y, x, z, n = far_items(0, w1, edge_base), far_items(1, w1), far_items(0, w2), near_items(0, w1)
+        for k in range(4):
+            table[f"ya{k}"], table[f"yf{k}"], table[f"yb{k}"] = y[k].a, y[k].fin, y[k].b
+            table[f"xa{k}"], table[f"za{k}"] = x[k].a, z[k].a
+        table["n0"] = n[0].a
         for t in range(TILES):
-            out = dot(h_mesh[tile_rows(t), :], w.edge[2][...])
-            for c in chunks():
-                recv[part_rows(t, c), :] = out[c:c + CH]
-        items = []
-        for t in range(TILES):
+            def back(t=t):
+                out = dot(h_mesh[tile_rows(t), :], w.edge[2][...])
+                for c in chunks():
+                    recv[part_rows(t, c), :] = out[c:c + CH]
+
+            node = Node(t, h_mesh, w)
+            table[f"r{t}"], table[f"nh{t}"], table[f"na{t}"], table[f"nb{t}"] = back, node.own, node.a, node.b
+            table[f"ps{t}"], table[f"pr{t}"] = functools.partial(project_send, t, w1), functools.partial(project_recv, t, w1)
             for p in range(PAIR):
-                def in_first(i, t=t, p=p):
-                    hide(i % 2, dot(feat[p, tile_rows(t), :], we[pl.ds(9 + 2 * step, 2)].reshape(256, LAT)))
-
-                def in_last(i, t=t, p=p):
-                    y = dot(hid[i % 2], weo[0])
+                i = PAIR * t + p
+                low, high = 8 + i, 12 + i
+
+                def in_first(t=t, p=p, low=low):
+                    hide(low, dot(feat[p, t].reshape(TILE, 2 * LANES), we[pl.ds(9 + PAIR * step, PAIR)].reshape(2 * LANES, LAT)))
+
+                def in_last(t=t, p=p, low=low):
+                    y = dot(hid[low], weo[ZERO])
                     for c in chunks():
                         v[p, part_rows(t, c), :] = norm(y[c:c + CH]).astype(BF16)
 
-                def edge_first(i, t=t, p=p):
+                def edge_first(t=t, p=p, high=high):
                     pre = dot(g2m[p, tile_rows(t), :], w.edge[0][...]) + dot(v[p, tile_rows(t), :], w.edge[1][...])
-                    hide(2 + i % 2, pre, lambda c, t=t: recv[part_rows(t, c), :])
-
-                def edge_last(i, t=t, p=p):
-                    y = dot(hid[2 + i % 2], w.edge_out[...])
+                    hide(high, pre, lambda c: recv[part_rows(t, c), :])
+
+                def edge_last(t=t, p=p, high=high):
+                    y = dot(hid[high], w.edge_out[...])
                     for c in chunks():
                         part = part_rows(t, c)
                         total = (g2m[p, part, :].astype(F32) + norm(y[c:c + CH])).astype(BF16).astype(F32)
@@ -509,122 +557,108 @@
                         else:
                             esum[part, :] = (acc[part, :] + total).astype(BF16)
 
-                items.append([in_first, in_last, edge_first, edge_last])
-        pipeline(items)
-        nodes = [Node(t, h_mesh, w) for t in range(TILES)]
-        selfs = []
-        for t in range(TILES):
-            for p in range(PAIR):
-                def self_first(t=t, p=p):
-                    hide(4 + p, dot(v[p, tile_rows(t), :], wself[0]))
-
-                def self_last(t=t, p=p):
-                    y = dot(hid[4 + p], wself[1])
+                def self_first(t=t, p=p, low=low):
+                    hide(low, dot(v[p, tile_rows(t), :], wself[ZERO]))
+
+                def self_last(t=t, p=p, low=low):
+                    y = dot(hid[low], wself[ONE])
                     for c in chunks():
                         part = part_rows(t, c)
                         vc[p, part, :] = (v[p, part, :].astype(F32) + norm(y[c:c + CH])).astype(BF16)
 
-                selfs.append((self_first, self_last))
-        y = far_items(0, w1, edge_base)
-        x = far_items(1, w1)
-        nodes[0].own()
-        nodes[0].a()
-        selfs[0][0]()
-        nodes[1].own()
-        nodes[1].a()
-        selfs[1][0]()
-        nodes[0].b()
-        selfs[0][1]()
-        nodes[1].b()
-        selfs[1][1]()
-        y[0].a()
-        y[1].a()
-        project(0, w1)
-        y[2].a()
-        y[3].a()
-        project(1, w1)
-        send_halo(0)
-        share_rows()
-        selfs[2][0]()
-        selfs[3][0]()
-        y[0].fin()
-        y[0].b()
-        y[1].fin()
-        y[1].b()
-        selfs[2][1]()
-        y[2].fin()
-        y[2].b()
-        y[3].fin()
-        y[3].b()
-        selfs[3][1]()
-        for item in x + far_items(0, w2) + near_items(0, w1)[:1]:
-            item.a()
-
-    def out_copies(step, out):
+                table[f"va{i}"], table[f"vb{i}"], table[f"ea{i}"], table[f"eb{i}"] = in_first, in_last, edge_first, edge_last
+                table[f"sa{i}"], table[f"sb{i}"] = self_first, self_last
+        run(ORDER_E, table)
+
+    def out_copies(step, out, t):
         copies = []
         for hop in range(RING):
             target = lax.rem(me + hop, RING)
-            src, dst = x_buf.at[step + 1, pl.ds(2 * target, 2)], out.at[:, place]
+            src, dst = x_buf.at[step + 1, :, t, pl.ds(PAIR * target, PAIR)], out.at[place, :, t]
             if hop == 0:
-                copies.append(pltpu.make_async_copy(src, dst, out_recv.at[step, hop]))
+                copies.append(pltpu.make_async_copy(src, dst, out_recv.at[step, t, hop]))
             else:
                 copies.append(pltpu.make_async_remote_copy(
-                    src_ref=src, dst_ref=dst, send_sem=out_send.at[step, hop], recv_sem=out_recv.at[step, hop],
+                    src_ref=src, dst_ref=dst, send_sem=out_send.at[step, t, hop], recv_sem=out_recv.at[step, t, hop],
                     device_id=at(target), device_id_type=mesh_id))
         return copies
 
-    def decoder_items(step):
+    def decoder(step):
+        w16 = layer_weights(step, LAYERS)
         w = layer_weights(step, BLOCKS - 1)
-        in_mean = stats[0:1, :]
-        in_std = stats[1:2, :]
-        diff_mean, diff_std = (jnp.concatenate([stats[i:i + 1, :], jnp.zeros((1, LANES - VARS), F32)], axis=ONE) for i in (2, 3))
-        items = []
+        in_mean = stats[ZERO:ONE, :]
+        in_std = stats[ONE:PAIR, :]
+        diff_mean, diff_std = (jnp.concatenate([stats[i:i + 1, :], jnp.zeros((ONE, LANES - VARS), F32)], axis=ONE) for i in (2, 3))
+        halo_slot = lax.rem(LAYERS + 1, 2)
+        table = {"share": share_rows, "wait": lambda: wait_halo(halo_slot), "halo": lambda: project_halo(halo_slot, w16)}
+        x = far_items(1, w16, resume=True)
+        for k in range(4):
+            table[f"fx{k}"], table[f"bx{k}"] = x[k].fin, x[k].b
         for t in range(TILES):
+            node = Node(t, h, w16)
+            table[f"nh{t}"], table[f"na{t}"], table[f"nb{t}"] = node.own, node.a, node.b
+            near = near_items(t, w16, resume=t == 0)
+            for k in range(PAIR):
+                table[f"n{t}{k}"], table[f"fn{t}{k}"], table[f"bn{t}{k}"] = near[k].a, near[k].fin, near[k].b
+
+            def back(t=t):
+                out = dot(h[tile_rows(t), :], w.edge[1][...])
+                for c in chunks():
+                    recv[part_rows(t, c), :] = out[c:c + CH]
+
+            def send(t=t):
+                for which, out in enumerate((out0, out1)):
+                    @pl.when(step == which)
+                    def _():
+                        start_all(out_copies(which, out, t))
+
+            table[f"t{t}"], table[f"send{t}"] = back, send
             for p in range(PAIR):
-                def edge_first(i, t=t, p=p):
-                    if p == 0 and t == 0:
-                        for q in range(RUNS):
-                            recv[pl.ds(q * HALF, HALF), :] = get_tiles(proj0, pl.ds(q * PAD0 + 8, HALF))
-                    elif p == 0:
-                        out = dot(h[tile_rows(t), :], w.edge[1][...])
-                        for c in chunks():
-                            recv[part_rows(t, c), :] = out[c:c + CH]
-                    pre = dot(m2g[p, tile_rows(t), :], w.edge[0][...]) + dot(vc[p, tile_rows(t), :], w.edge[2][...])
-                    hide(i % 2, pre, lambda c, t=t: recv[part_rows(t, c), :])
-
-                def edge_last(i, t=t, p=p):
-                    y = dot(hid[i % 2], w.edge_out[...])
+                i = PAIR * t + p
+                low, high = 8 + i, 12 + i
+                held = {}
+
+                def edge_own(t=t, p=p, held=held):
+                    held["edge"] = dot(m2g[p, tile_rows(t), :], w.edge[0][...]) + dot(vc[p, tile_rows(t), :], w.edge[2][...])
+
+                def edge_first(t=t, low=low, held=held):
+                    hide(low, held["edge"], lambda c: recv[part_rows(t, c), :])
+
+                def edge_last(t=t, p=p, low=low, i=i):
+                    y = dot(hid[low], w.edge_out[...])
                     for c in chunks():
                         part = part_rows(t, c)
-                        dec[i % 2, pl.ds(c, CH), :] = (m2g[p, part, :].astype(F32) + norm(y[c:c + CH])).astype(BF16)
-
-                def node_first(i, t=t, p=p):
-                    hide(2 + i % 2, dot(vc[p, tile_rows(t), :], w.node[0][...]) + dot(dec[i % 2], w.node[1][...]))
-
-                def node_last(i, t=t, p=p):
-                    y = dot(hid[2 + i % 2], w.node_out[...])
+                        dec[i, pl.ds(c, CH), :] = (m2g[p, part, :].astype(F32) + norm(y[c:c + CH])).astype(BF16)
+
+                def node_own(t=t, p=p, held=held):
+                    held["node"] = dot(vc[p, tile_rows(t), :], w.node[0][...])
+
+                def node_first(high=high, i=i, held=held):
+                    hide(high, held["node"] + dot(dec[i], w.node[1][...]))
+
+                def node_last(t=t, p=p, high=high):
+                    y = dot(hid[high], w.node_out[...])
                     for c in chunks():
                         part = part_rows(t, c)
                         v[p, part, :] = (vc[p, part, :].astype(F32) + norm(y[c:c + CH])).astype(BF16)
 
-                def out_first(i, t=t, p=p):
-                    hide(4 + i % 2, dot(v[p, tile_rows(t), :], woh[...]))
-
-                def out_last(i, t=t, p=p):
-                    pred = dot(hid[4 + i % 2], wof[...])
+                def out_first(t=t, p=p, low=low):
+                    hide(low, dot(v[p, tile_rows(t), :], woh[...]))
+
+                def out_last(t=t, p=p, low=low):
+                    pred = dot(hid[low], wof[...])
                     for c in chunks():
-                        spots = [(q, pl.ds(2 * r + p, n, stride=2), n) for q in chunk_runs(c) for r, n in pieces(t)]
-                        now = jnp.concatenate([x_buf[step, q, rows, :] for q, rows, n in spots], axis=ZERO)
+                        runs = pl.ds(c // HALF, CH // HALF)
+                        now = x_buf[step, p, t, runs].reshape(CH, LANES)
                         new = now + diff_std * pred[c:c + CH] + diff_mean
-                        row = 0
-                        for q, rows, n in spots:
-                            x_buf[step + 1, q, rows, :] = new[row:row + n]
-                            row += n
-                        scaled = (new[:, :VARS] - in_mean) / in_std
-                        feat[p, part_rows(t, c), pl.ds(ZERO, VARS)] = scaled.astype(BF16)
-
-                items.append([edge_first, edge_last, node_first, node_last, out_first, out_last])
-        return items
+                        x_buf[step + 1, p, t, runs] = new.reshape(CH // HALF, HALF, LANES)
+                        scaled = ((new[:, :VARS] - in_mean) / in_std).astype(BF16)
+                        feat[p, t, runs, :, pl.ds(ZERO, VARS)] = scaled.reshape(CH // HALF, HALF, VARS)
+
+                table[f"em{i}"], table[f"ea{i}"], table[f"eb{i}"] = edge_own, edge_first, edge_last
+                table[f"dm{i}"], table[f"da{i}"], table[f"db{i}"] = node_own, node_first, node_last
+                table[f"oa{i}"], table[f"ob{i}"] = out_first, out_last
+        run(ORDER_D, table)
 
     def wait_all(copies):
         for copy in copies:
@@ -660,36 +694,17 @@
         @pl.when(step == 0)
         def _():
             start_all(layer_copies(1, 1) + layer_copies(1, 2))
-            wait_in(2)
-
-        w = layer_weights(step, LAYERS)
-        w_last = layer_weights(step, BLOCKS - 1)
-        n1 = near_items(1, w)
-        phase(ORDER_A, far_items(1, w, resume=True), near_items(0, w, resume=True), Node(0, h, w), None, n1, share_rows, w_last)
-        n1[1].a()
-        wait_halo(lax.rem(LAYERS + 1, 2))
-        project_halo(lax.rem(LAYERS + 1, 2), w)
-        last = Node(1, h, w)
-        for item in n1:
-            item.fin()
-        for item in n1:
-            item.b()
-        last.own()
-        last.a()
-        last.b()
-        pipeline(decoder_items(step))
-
-        for which, out in ((0, out0), (1, out1)):
-            @pl.when(step == which)
-            def _():
-                start_all(out_copies(which, out))
+            wait_in(PAIR)
+
+        decoder(step)
         return carry
 
     lax.fori_loop(0, 2, one_step, 0)
     for part in range(3):
         for copy in in_copies[part][1:]:
             copy.wait_send()
-    wait_all(out_copies(0, out0) + out_copies(1, out1))
+    for t in range(TILES):
+        wait_all(out_copies(0, out0, t) + out_copies(1, out1, t))
 
 
 def solution(mesh):
@@ -705,13 +720,14 @@
         dma = pltpu.SemaphoreType.DMA
         grid_dev = x_prev.shape[0]
         shape = jax.ShapeDtypeStruct
-        home = shape((PAIR, RING, GRID_RUN, LANES), F32)
+        home = shape((RING, PAIR, TILES, PAIR, HALF, LANES), F32)
         g_home, m_home, x_home, w_final = pl.pallas_call(
             pack_kernel,
-            out_shape=(shape((PAIR, RING, GRID_RUN, 256), BF16), shape((PAIR, RING, RUN, LANES), BF16), home, shape((LAT, LANES), BF16)),
+            out_shape=(shape((*home.shape[:-1], 2 * LANES), BF16), shape((RING, TILES, PAIR, HALF, LANES), BF16), home,
+                       shape((LAT, LANES), BF16)),
             in_specs=[vmem_spec] * 10,
             out_specs=(vmem_spec,) * 4,
-            scratch_shapes=[pltpu.VMEM((4, grid_dev, LANES), F32)],
+            scratch_shapes=[pltpu.VMEM((5, grid_dev, LANES), F32)],
             name="pack",
         )(x_prev.T, x_cur.T, forcing.T, grid_static.T, g2m_feat.T, m2g_feat.T, mesh_feat.T,
           jnp.transpose(mesh_edge_feat, (1, 2, 0)), norm_stats, w_out_final.T)
@@ -719,11 +735,9 @@
             pltpu.VMEM((2 * VARS + 10, LAT), BF16),
             pltpu.VMEM((3, LAT), BF16),
             pltpu.VMEM((3, 4, LAT), BF16),
-            pltpu.VMEM((RUNS, GRID_RUN, 256), BF16),
-            pltpu.VMEM((RUNS, RUN, LANES), BF16),
-            pltpu.VMEM((3, RUNS, GRID_RUN, LANES), F32),
-            pltpu.VMEM((PAIR, RUNS * GRID_RUN, LANES), F32),
-            pltpu.VMEM((PAIR, ROWS, 256), BF16),
+            pltpu.VMEM((TILES, RUNS, HALF, LANES), BF16),
+            pltpu.VMEM((3, PAIR, TILES, RUNS, HALF, LANES), F32),
+            pltpu.VMEM((PAIR, TILES, RUNS, HALF, 2 * LANES), BF16),
             pltpu.VMEM((13, LANES, LAT), BF16),
             pltpu.VMEM((5, LAT, LAT), BF16),
             pltpu.VMEM((PAIR, LAT, LAT), BF16),
@@ -750,14 +764,14 @@
             pltpu.VMEM((LAT // LANES, RUNS * PAD1, LANES), F32),
             pltpu.VMEM((ROWS, LAT), F32),
             pltpu.VMEM((ROWS, LAT), F32),
-            pltpu.VMEM((8, TILE, LAT), BF16),
+            pltpu.VMEM((16, TILE, LAT), BF16),
             pltpu.VMEM((ROWS, LAT), BF16),
-            pltpu.VMEM((PAIR, TILE, LAT), BF16),
+            pltpu.VMEM((4, TILE, LAT), BF16),
             pltpu.VMEM((10, TILE, LAT), F32),
             pltpu.VMEM((PAIR, RUNS, LAT), BF16),
             pltpu.VMEM((PAIR, 2, RUNS, LAT), BF16),
-            dma((3,)), dma((3, RING)), dma((3, RING)), dma((4,)), dma((1, 4)), dma((SLOTS, 4)), dma((2,)), dma((2, 2)),
-            dma((2, RING)), dma((2, RING)),
+            dma((3,)), dma((3, RING)), dma((3, RING)), dma((4,)), dma((1, 4)), dma((SLOTS, 4)), dma((PAIR,)), dma((PAIR, PAIR)),
+            dma((PAIR, TILES, RING)), dma((PAIR, TILES, RING)),
         ]
         home0, home1 = pl.pallas_call(
             kernel,
@@ -771,7 +785,8 @@
           w_node_out, w_grid_self, w_out_hidden, w_final)
         out = shape((VARS, grid_dev), F32)
         next_state, after_state = pl.pallas_call(
-            unpack_kernel, out_shape=(out, out), in_specs=[vmem_spec] * 2, out_specs=(vmem_spec,) * 2, name="unpack",
+            unpack_kernel, out_shape=(out, out), in_specs=[vmem_spec] * 2, out_specs=(vmem_spec,) * 2,
+            scratch_shapes=[pltpu.VMEM((grid_dev, LANES), F32)], name="unpack",
         )(home0, home1)
         return next_state.T, after_state.T
 

time: 254 us -> 254 us (level)
  no operation moved by 1% of the time
where the time goes in v4:
time: 254 us; the launch traced here: 253 us
  Pallas kernels  253 us (100%)
    pallas_call x1, Pallas kernels, local_run(): pl.pallas_call(kernel, out_shape=(home, home), in_specs=[any_spec] * 3 +...  248 us

profile of v4, /device:TPU:0, one launch (start us, length us, event | category | flops | bytes accessed | tf_op | source)
XLA Modules:
  0.0 253.3 jit_solution(5041343987074370263)
XLA Ops:
  0.6 2.8 %pack.1 = (bf16[8,2,2,2,16,256]{5,4,3,2,1,0:T(8,128)(2,1)}, bf16[8,2,2,16,128]{4,3,2,1,0:T(8,128)(2,1)}, f32[8,2,2,2,16,128]{5,4,3,2,1,0:T(8,128)}, bf16[512,128]{1,0:T(8,128)(2,1)}) custom-call(f32[84,1024]{1,0:T(8,128)} %bitcast.11, f32[84,1024]{1,0:T(8,128)} %bitcast.12, f32[5,2,1024]{2,1,0:T(2,128)} %bitcast.15, f32[5,1024]{1,0:T(8,128)} %bitcast.16, ...), custom_call_target="tpu_custom_call" | custom-call | tf_op jit(solution)/shard_map/pack/pallas_call | solution.py:724
  3.4 247.6 %forecast.1 = (f32[8,2,2,2,16,128]{5,4,3,2,1,0:T(8,128)}, f32[8,2,2,2,16,128]{5,4,3,2,1,0:T(8,128)}) custom-call(bf16[8,2,2,2,16,256]{5,4,3,2,1,0:T(8,128)(2,1)} %get-tuple-element.10.g_home, bf16[8,2,2,16,128]{4,3,2,1,0:T(8,128)(2,1)} %get-tuple-element.11.m_home, f32[8,2,2,2,16,128]{5,4,3,2,1,0:T(8,128)} %get-tuple-element.12.x_home, f32[4,84]{1,0:T(4,128)} %stats.3, ...), custom_call_target="tpu_custom_call" | custom-call | tf_op jit(solution)/shard_map/forecast/pallas_call | solution.py:776
  251.0 2.3 unpack.1

commit v5 on v4

--- a/solution.py
+++ b/solution.py
@@ -24,7 +24,7 @@
 TILE = 256
 TILES = 2
 HALF = TILE // RUNS
-CH = 32
+CH = 128
 RING = 8
 LAYERS = 16
 BLOCKS = LAYERS + 2
@@ -40,16 +40,16 @@
     "bx2", "na", "bx3", "ax2", "nb", "an0", "ax3", "ps", "pr",
 )
 ORDER_E = (
-    "copy", "r0", "va0", "va1", "r1", "vb0", "va2", "vb1", "va3", "vb2", "vb3", "ea0", "sa0", "ea1", "eb0",
-    "sa1", "eb1", "ea2", "sb0", "ea3", "sb1", "nh0", "na0", "eb2", "sa2", "eb3", "nb0", "sa3", "sb2", "sb3",
-    "ya0", "nh1", "na1", "ps0", "pr0", "ya1", "ya2", "nb1", "yf0", "yb0", "yf1", "yb1", "ya3", "ps1", "pr1",
-    "yf2", "yb2", "yf3", "yb3", "xa0", "xa1", "xa2", "xa3", "za0", "za1", "za2", "za3", "n0", "share", "send",
+    "copy", "r0", "va0", "va1", "vb0", "va2", "vb1", "va3", "r1", "vb2", "vb3", "ea0", "sa0", "ea3", "ea1",
+    "eb0", "sa1", "eb1", "sb0", "ea2", "sb1", "nh0", "na0", "eb2", "sa2", "eb3", "nb0", "sa3", "sb2", "sb3",
+    "ya2", "ya0", "nh1", "ya1", "na1", "ps0", "pr0", "nb1", "yf0", "yb0", "yf1", "yb1", "ps1", "ya3", "pr1",
+    "yf2", "yb2", "yf3", "yb3", "xa0", "xa1", "za1", "xa2", "xa3", "za0", "za2", "za3", "n0", "share", "send",
 )
 ORDER_D = (
-    "share", "nh0", "fx0", "bx0", "n01", "fx1", "bx1", "fn00", "fn01", "bn00", "bn01", "em0", "fx2", "bx2",
-    "fx3", "bx3", "na0", "em1", "nb0", "n10", "n11", "dm0", "t0", "wait", "halo", "ea0", "fn10", "fn11",
-    "bn10", "bn11", "ea1", "eb0", "eb1", "nh1", "na1", "dm1", "em2", "da0", "nb1", "da1", "dm2", "em3", "db0",
-    "t1", "db1", "dm3", "oa0", "ea2", "oa1", "eb2", "ob0", "ea3", "ob1", "send0", "eb3", "da2", "da3", "db2",
+    "fx0", "share", "nh0", "fx1", "bx0", "n01", "fn00", "fn01", "bn00", "bn01", "bx1", "em0", "fx2", "bx2",
+    "fx3", "bx3", "na0", "em1", "nb0", "n11", "dm0", "wait", "n10", "t0", "halo", "ea0", "fn11", "fn10",
+    "bn10", "bn11", "ea1", "eb0", "eb1", "nh1", "na1", "em2", "da0", "dm1", "nb1", "da1", "dm2", "em3", "db0",
+    "t1", "db1", "oa0", "ea2", "eb2", "oa1", "ob0", "ea3", "ob1", "send0", "eb3", "da2", "dm3", "da3", "db2",
     "db3", "oa2", "oa3", "ob2", "ob3", "send1",
 )
 
@@ -102,77 +102,27 @@
 
 
 AT_FORCE, AT_STATIC, AT_NEXT, AT_M2G, AT_G2M = 88, 96, 104, 112, 120
-PREV_AREA, CUR_AREA, NORM_AREA, MESH_AREA, OUT_AREA = range(5)
 
 
 def columns(n):
     return pl.ds(LANES * n, LANES)
 
 
-def stack(ref, n, rows):
-    base = LANES * n
+def stack(ref, rows):
     end = 0
     for at_row, value in rows:
         first = at_row // 8 * 8
         last = (at_row + value.shape[0]) // 8 * 8
         if first > end:
-            ref[pl.ds(base + end, first - end), :] = jnp.zeros((first - end, LANES), F32)
+            ref[pl.ds(end, first - end), :] = jnp.zeros((first - end, LANES), F32)
         if last < at_row + value.shape[0]:
-            ref[pl.ds(base + last, 8), :] = jnp.zeros((8, LANES), F32)
+            ref[pl.ds(last, 8), :] = jnp.zeros((8, LANES), F32)
             end = last + 8
         else:
             end = last
-        ref[pl.ds(base + at_row, value.shape[0]), :] = value
+        ref[pl.ds(at_row, value.shape[0]), :] = value
     if end < LANES:
-        ref[pl.ds(base + end, LANES - end), :] = jnp.zeros((LANES - end, LANES), F32)
-
-
-def pack_kernel(x_prev, x_cur, forcing, static, g2m_feat, m2g_feat, mesh_feat, mesh_edge_feat, stats, w_out_final,
-                g_home, m_home, x_home, w_final, area):
-    def turned(slot, n):
-        return jnp.transpose(area[slot, columns(n), :])
-
-    blocks = range(x_cur.shape[1] // LANES)
-    mesh_blocks = range(mesh_feat.shape[1] // LANES)
-    weight_blocks = range(LAT // LANES)
-    for n in mesh_blocks:
-        stack(area.at[MESH_AREA], n, [(ZERO, mesh_feat[:, columns(n)])] + [
-            (16 + 16 * k, mesh_edge_feat[k, :, columns(n)]) for k in range(6)])
-    for n in weight_blocks:
-        stack(area.at[OUT_AREA], n, [(ZERO, w_out_final[:, columns(n)].astype(F32))])
-    for n in blocks:
-        stack(area.at[PREV_AREA], n, [
-            (ZERO, x_prev[:, columns(n)]), (AT_FORCE, forcing[:, ZERO, columns(n)]), (AT_STATIC, static[:, columns(n)]),
-            (AT_NEXT, forcing[:, ONE, columns(n)]), (AT_M2G, m2g_feat[:, columns(n)]), (AT_G2M, g2m_feat[:, columns(n)])])
-        stack(area.at[CUR_AREA], n, [(ZERO, x_cur[:, columns(n)])])
-    for n in mesh_blocks:
-        turned_rows = turned(MESH_AREA, n)
-        for i in range(LANES // RUN):
-            band, k = divmod(n * LANES + i * RUN, RING * RUN)
-            for t in range(TILES):
-                m_home[k // RUN, t, band] = jnp.concatenate(
-                    [turned_rows[i * RUN + r:i * RUN + r + rows] for r, rows in pieces(t)], axis=ZERO).astype(BF16)
-    for n in weight_blocks:
-        w_final[columns(n), :] = turned(OUT_AREA, n).astype(BF16)
-    rest = LANES - VARS
-    wide_mean = jnp.concatenate([stats[ZERO:ONE, :], jnp.zeros((ONE, rest), F32)], axis=ONE)
-    wide_std = jnp.concatenate([stats[ONE:PAIR, :], jnp.ones((ONE, rest), F32)], axis=ONE)
-    for n in blocks:
-        prev, cur = turned(PREV_AREA, n), turned(CUR_AREA, n)
-        area[PREV_AREA, columns(n), :] = (prev - wide_mean) / wide_std
-        area[CUR_AREA, columns(n), :] = cur
-        area[NORM_AREA, columns(n), :] = (cur - wide_mean) / wide_std
-    for band in range(PAIR):
-        for k in range(RING):
-            base = (band * RING + k) * GRID_RUN
-            for p in range(PAIR):
-                for t in range(TILES):
-                    def rows_of(slot):
-                        return jnp.concatenate([area[slot, pl.ds(base + PAIR * r + p, rows, stride=PAIR), :]
-                                                for r, rows in pieces(t)], axis=ZERO)
-                    g_home[k, p, t, band, :, pl.ds(ZERO, LANES)] = rows_of(PREV_AREA).astype(BF16)
-                    g_home[k, p, t, band, :, pl.ds(LANES, LANES)] = rows_of(NORM_AREA).astype(BF16)
-                    x_home[k, p, t, band] = rows_of(CUR_AREA)
+        ref[pl.ds(end, LANES - end), :] = jnp.zeros((LANES - end, LANES), F32)
 
 
 def unpack_kernel(home0, home1, out0, out1, area):
@@ -190,10 +140,11 @@
             out[:, columns(n)] = jnp.transpose(area[columns(n), :])[:VARS]
 
 
-def kernel(g_home, m_home, x_home, stats, w_grid_in, w_mesh_in,
+def kernel(x_prev, x_cur, forcing, static, g2m_feat, m2g_feat, mesh_feat, mesh_edge_feat, stats, w_grid_in, w_mesh_in,
            w_eemb_in, w_embed_out, w_edge_in, w_edge_out, w_node_in, w_node_out, w_grid_self, w_out_hidden, w_out_final,
            out0, out1,
-           wgrid_raw, wmesh_raw, weemb_raw,
+           mesh_raw, medge_raw, prev_raw, cur_raw, force_raw, static_raw, g2m_raw, m2g_raw,
+           wgrid_raw, wmesh_raw, weemb_raw, wfin_raw, g_home, m_home, x_home,
            m_buf, x_buf, feat, we, weo, wself, woh, wof,
            enc_ei, enc_eo, enc_ni, enc_no, lay_ei, lay_eo, lay_ni, lay_no,
            edge_base, edge, h_mesh, h, hf, g2m, m2g, v, vc, proj0, proj1, recv, acc, hid, esum, dec, pre_buf,
@@ -235,17 +186,17 @@
         return Weights(lay_refs, slot_of(step, block))
 
     raw = [pltpu.make_async_copy(src, dst, raw_sem.at[i]) for i, (src, dst) in enumerate(
-        ((w_grid_in, wgrid_raw), (w_mesh_in, wmesh_raw), (w_eemb_in, weemb_raw)))]
+        ((mesh_feat, mesh_raw), (mesh_edge_feat, medge_raw), (x_prev, prev_raw), (x_cur, cur_raw), (forcing, force_raw),
+         (static, static_raw), (g2m_feat, g2m_raw), (m2g_feat, m2g_raw),
+         (w_grid_in, wgrid_raw), (w_mesh_in, wmesh_raw), (w_eemb_in, weemb_raw), (w_out_final, wfin_raw)))]
     for copy in raw:
         copy.start()
     small = [
         pltpu.make_async_copy(w_embed_out, weo, w_sem.at[0]),
         pltpu.make_async_copy(w_grid_self, wself, w_sem.at[1]),
         pltpu.make_async_copy(w_out_hidden, woh, w_sem.at[2]),
-        pltpu.make_async_copy(w_out_final, wof, w_sem.at[3]),
     ]
-    for copy in small + enc_copies() + layer_copies(0, 1) + layer_copies(0, 2):
-        copy.start()
+    small[0].start()
 
     barrier = pltpu.get_barrier_semaphore()
     for hop in range(1, RING):
@@ -275,12 +226,65 @@
         for copy in in_copies[part]:
             copy.start()
 
+    def place_of(area, n):
+        ref, first = area
+        return ref.at[first + n // 4, columns(n % 4)]
+
+    prev_area, cur_area, norm_area, mesh_area, final_area = (proj0, 0), (proj0, PAIR), (proj1, 0), (proj1, 2), (proj1, 3)
+
+    def turned(area, n):
+        return jnp.transpose(place_of(area, n)[...])
+
+    for copy in raw[:2]:
+        copy.wait()
+    for n in range(mesh_raw.shape[1] // LANES):
+        stack(place_of(mesh_area, n), [(ZERO, mesh_raw[:, columns(n)])] + [
+            (16 + 16 * k, medge_raw[k, :, columns(n)]) for k in range(6)])
+    for n in range(mesh_raw.shape[1] // LANES):
+        turned_rows = turned(mesh_area, n)
+        for i in range(LANES // RUN):
+            band, k = divmod(n * LANES + i * RUN, RING * RUN)
+            for t in range(TILES):
+                m_home[k // RUN, t, band] = jnp.concatenate(
+                    [turned_rows[i * RUN + r:i * RUN + r + rows] for r, rows in pieces(t)], axis=ZERO).astype(BF16)
     pl.semaphore_wait(barrier, RING - 1)
     start_in(0)
+    for copy in raw[2:8]:
+        copy.wait()
+    blocks = range(cur_raw.shape[1] // LANES)
+    for n in blocks:
+        stack(place_of(prev_area, n), [
+            (ZERO, prev_raw[:, columns(n)]), (AT_FORCE, force_raw[:, ZERO, columns(n)]), (AT_STATIC, static_raw[:, columns(n)]),
+            (AT_NEXT, force_raw[:, ONE, columns(n)]), (AT_M2G, m2g_raw[:, columns(n)]), (AT_G2M, g2m_raw[:, columns(n)])])
+        stack(place_of(cur_area, n), [(ZERO, cur_raw[:, columns(n)])])
+    rest = LANES - VARS
+    wide_mean = jnp.concatenate([stats[ZERO:ONE, :], jnp.zeros((ONE, rest), F32)], axis=ONE)
+    wide_std = jnp.concatenate([stats[ONE:PAIR, :], jnp.ones((ONE, rest), F32)], axis=ONE)
+    for n in blocks:
+        prev, cur = turned(prev_area, n), turned(cur_area, n)
+        place_of(prev_area, n)[...] = (prev - wide_mean) / wide_std
+        place_of(cur_area, n)[...] = cur
+        place_of(norm_area, n)[...] = (cur - wide_mean) / wide_std
+    for k in range(RING):
+        for p in range(PAIR):
+            for t in range(TILES):
+                for band in range(PAIR):
+                    def rows_of(area):
+                        ref, first = area
+                        return jnp.concatenate([ref[first + band, pl.ds(k * GRID_RUN + PAIR * r + p, rows, stride=PAIR), :]
+                                                for r, rows in pieces(t)], axis=ZERO)
+                    g_home[k, p, t, band, :, pl.ds(ZERO, LANES)] = rows_of(prev_area).astype(BF16)
+                    g_home[k, p, t, band, :, pl.ds(LANES, LANES)] = rows_of(norm_area).astype(BF16)
+                    x_home[k, p, t, band] = rows_of(cur_area)
     start_in(1)
-
-    for copy in raw:
+    for copy in small[1:] + enc_copies() + layer_copies(0, 1) + layer_copies(0, 2):
+        copy.start()
+
+    for copy in raw[8:]:
         copy.wait()
+    for n in range(LAT // LANES):
+        stack(place_of(final_area, n), [(ZERO, wfin_raw[:, columns(n)].astype(F32))])
+        wof[columns(n), :] = turned(final_area, n).astype(BF16)
     wide = wgrid_raw[...].astype(F32)
     recv[pl.ds(ZERO, wide.shape[0]), :] = wide
     prev_w, cur_w = recv[pl.ds(ZERO, VARS), :], recv[pl.ds(VARS, VARS), :]
@@ -675,16 +679,16 @@
 
         def one_layer(block, carry):
             halo_slot = lax.rem(block + 1, 2)
-            wait_all(layer_copies(step, block + 2))
-
-            @pl.when(block < LAYERS - 1)
-            def _():
-                start_all(layer_copies(step, block + 3))
-
             w, w1, w2 = (layer_weights(step, block + i) for i in range(3))
             phase(ORDER_A, far_items(1, w, resume=True), near_items(0, w, resume=True), Node(0, h, w), far_items(1, w1),
                   near_items(1, w), share_rows, w1)
             wait_halo(halo_slot)
+            wait_all(layer_copies(step, block + 2))
+
+            @pl.when(block < LAYERS - 1)
+            def _():
+                start_all(layer_copies(step, block + 3))
+
             phase(ORDER_B, far_items(0, w1, resume=True), near_items(1, w, resume=True), Node(1, h, w), far_items(0, w2),
                   near_items(0, w1), lambda: project_halo(halo_slot, w), w1)
             send_halo(1 - halo_slot)
@@ -721,20 +725,19 @@
         grid_dev = x_prev.shape[0]
         shape = jax.ShapeDtypeStruct
         home = shape((RING, PAIR, TILES, PAIR, HALF, LANES), F32)
-        g_home, m_home, x_home, w_final = pl.pallas_call(
-            pack_kernel,
-            out_shape=(shape((*home.shape[:-1], 2 * LANES), BF16), shape((RING, TILES, PAIR, HALF, LANES), BF16), home,
-                       shape((LAT, LANES), BF16)),
-            in_specs=[vmem_spec] * 10,
-            out_specs=(vmem_spec,) * 4,
-            scratch_shapes=[pltpu.VMEM((5, grid_dev, LANES), F32)],
-            name="pack",
-        )(x_prev.T, x_cur.T, forcing.T, grid_static.T, g2m_feat.T, m2g_feat.T, mesh_feat.T,
-          jnp.transpose(mesh_edge_feat, (1, 2, 0)), norm_stats, w_out_final.T)
-        scratch = [
+        bulk = [
+            pltpu.VMEM(shape_, F32) for shape_ in (
+                (3, mesh_feat.shape[0]), (6, 4, mesh_feat.shape[0]), (VARS, grid_dev), (VARS, grid_dev), (5, PAIR, grid_dev),
+                (5, grid_dev), (4, grid_dev), (4, grid_dev))
+        ]
+        scratch = bulk + [
             pltpu.VMEM((2 * VARS + 10, LAT), BF16),
             pltpu.VMEM((3, LAT), BF16),
             pltpu.VMEM((3, 4, LAT), BF16),
+            pltpu.VMEM((VARS, LAT), BF16),
+            pltpu.VMEM((*home.shape[:-1], 2 * LANES), BF16),
+            pltpu.VMEM((RING, TILES, PAIR, HALF, LANES), BF16),
+            pltpu.VMEM(home.shape, F32),
             pltpu.VMEM((TILES, RUNS, HALF, LANES), BF16),
             pltpu.VMEM((3, PAIR, TILES, RUNS, HALF, LANES), F32),
             pltpu.VMEM((PAIR, TILES, RUNS, HALF, 2 * LANES), BF16),
@@ -770,19 +773,20 @@
             pltpu.VMEM((10, TILE, LAT), F32),
             pltpu.VMEM((PAIR, RUNS, LAT), BF16),
             pltpu.VMEM((PAIR, 2, RUNS, LAT), BF16),
-            dma((3,)), dma((3, RING)), dma((3, RING)), dma((4,)), dma((1, 4)), dma((SLOTS, 4)), dma((PAIR,)), dma((PAIR, PAIR)),
+            dma((12,)), dma((3, RING)), dma((3, RING)), dma((4,)), dma((1, 4)), dma((SLOTS, 4)), dma((PAIR,)), dma((PAIR, PAIR)),
             dma((PAIR, TILES, RING)), dma((PAIR, TILES, RING)),
         ]
         home0, home1 = pl.pallas_call(
             kernel,
             out_shape=(home, home),
-            in_specs=[any_spec] * 3 + [vmem_spec] + [any_spec] * 11,
+            in_specs=[any_spec] * 8 + [vmem_spec] + [any_spec] * 11,
             out_specs=(any_spec, any_spec),
             scratch_shapes=scratch,
             compiler_params=pltpu.CompilerParams(collective_id=0, has_side_effects=True, vmem_limit_bytes=63 << 20),
             name="forecast",
-        )(g_home, m_home, x_home, norm_stats, w_grid_in, w_mesh_in, w_eemb_in, w_embed_out, w_edge_in, w_edge_out, w_node_in,
-          w_node_out, w_grid_self, w_out_hidden, w_final)
+        )(x_prev.T, x_cur.T, forcing.T, grid_static.T, g2m_feat.T, m2g_feat.T, mesh_feat.T,
+          jnp.transpose(mesh_edge_feat, (1, 2, 0)), norm_stats, w_grid_in, w_mesh_in, w_eemb_in, w_embed_out, w_edge_in,
+          w_edge_out, w_node_in, w_node_out, w_grid_self, w_out_hidden, w_out_final.T)
         out = shape((VARS, grid_dev), F32)
         next_state, after_state = pl.pallas_call(
             unpack_kernel, out_shape=(out, out), in_specs=[vmem_spec] * 2, out_specs=(vmem_spec,) * 2,

time: 254 us -> 247 us (0.972)
  Pallas kernels: 253 us -> 246 us
    pallas_call x2 -> x1, Pallas kernels: 250 us -> 243 us  [local_run(): pl.pallas_call(kernel, out_shape=(home, home), in_specs=[any_spec] * 8 +...]
where the time goes in v5:
time: 247 us; the launch traced here: 246 us
  Pallas kernels  246 us (100%)
    pallas_call x1, Pallas kernels, local_run(): pl.pallas_call(kernel, out_shape=(home, home), in_specs=[any_spec] * 8 +...  243 us

profile of v5, /device:TPU:0, one launch (start us, length us, event | category | flops | bytes accessed | tf_op | source)
XLA Modules:
  0.0 246.4 jit_solution(626062302990269843)
XLA Ops:
  0.6 243.5 %forecast.1 = (f32[8,2,2,2,16,128]{5,4,3,2,1,0:T(8,128)}, f32[8,2,2,2,16,128]{5,4,3,2,1,0:T(8,128)}) custom-call(f32[84,1024]{1,0:T(8,128)} %bitcast.11, f32[84,1024]{1,0:T(8,128)} %bitcast.12, f32[5,2,1024]{2,1,0:T(2,128)} %bitcast.15, f32[5,1024]{1,0:T(8,128)} %bitcast.16, f32[4,1024]{1,0:T(4,128)} %bitcast.17, f32[4,1024]{1,0:T(4,128)} %bitcast.18, ...), custom_call_target="tpu_custom_call" | custom-call | tf_op jit(solution)/shard_map/forecast/pallas_call | solution.py:779
  244.1 2.3 unpack.1

commit v6 on v5

--- a/solution.py
+++ b/solution.py
@@ -32,12 +32,12 @@
 FAR = ((2, 1), (3, -1), (4, 4), (5, -4))
 NEAR = ((0, 1), (1, -1))
 ORDER_A = (
-    "nh", "before", "fx0", "bx0", "n1", "fx1", "bx1", "fn0", "fn1", "bn0", "bn1", "ax0", "fx2", "ax1", "fx3",
-    "bx2", "na", "bx3", "ax2", "nb", "an0", "ax3", "ps", "pr",
+    "nh", "before", "fx0", "n1", "fx1", "bx0", "bx1", "fn0", "bn0", "fn1", "bn1", "ax0", "fx2", "fx3", "bx2",
+    "na", "ax1", "bx3", "ax2", "nb", "an0", "ax3", "pr", "ps",
 )
 ORDER_B = (
-    "nh", "before", "fx0", "bx0", "n1", "fx1", "bx1", "fn0", "fn1", "bn0", "bn1", "ax0", "fx2", "ax1", "fx3",
-    "bx2", "na", "bx3", "ax2", "nb", "an0", "ax3", "ps", "pr",
+    "nh", "before", "fx0", "fx1", "bx0", "n1", "fn1", "bx1", "fn0", "bn0", "bn1", "ax0", "fx2", "ax1", "fx3",
+    "bx2", "na", "bx3", "ax2", "nb", "ax3", "an0", "ps", "pr",
 )
 ORDER_E = (
     "copy", "r0", "va0", "va1", "vb0", "va2", "vb1", "va3", "r1", "vb2", "vb3", "ea0", "sa0", "ea3", "ea1",
@@ -46,11 +46,11 @@
     "yf2", "yb2", "yf3", "yb3", "xa0", "xa1", "za1", "xa2", "xa3", "za0", "za2", "za3", "n0", "share", "send",
 )
 ORDER_D = (
-    "fx0", "share", "nh0", "fx1", "bx0", "n01", "fn00", "fn01", "bn00", "bn01", "bx1", "em0", "fx2", "bx2",
-    "fx3", "bx3", "na0", "em1", "nb0", "n11", "dm0", "wait", "n10", "t0", "halo", "ea0", "fn11", "fn10",
-    "bn10", "bn11", "ea1", "eb0", "eb1", "nh1", "na1", "em2", "da0", "dm1", "nb1", "da1", "dm2", "em3", "db0",
-    "t1", "db1", "oa0", "ea2", "eb2", "oa1", "ob0", "ea3", "ob1", "send0", "eb3", "da2", "dm3", "da3", "db2",
-    "db3", "oa2", "oa3", "ob2", "ob3", "send1",
+    "n01", "fx1", "nh0", "fx0", "share", "bx0", "fn00", "fn01", "bn00", "bn01", "bx1", "em0", "fx2", "bx2",
+    "fx3", "na0", "em1", "nb0", "n11", "wait", "dm0", "n10", "t0", "halo", "bx3", "ea0", "fn11", "fn10",
+    "bn10", "eb0", "bn11", "ea1", "eb1", "nh1", "em2", "em3", "na1", "da0", "dm1", "nb1", "da1", "dm2", "db0",
+    "t1", "db1", "oa0", "ea2", "eb2", "oa1", "ob0", "ea3", "dm3", "ob1", "send0", "send1", "eb3", "da2", "da3",
+    "db2", "db3", "oa2", "oa3", "ob2", "send2", "ob3", "send3",
 )
 
 
@@ -125,8 +125,8 @@
         ref[pl.ds(end, LANES - end), :] = jnp.zeros((LANES - end, LANES), F32)
 
 
-def unpack_kernel(home0, home1, out0, out1, area):
-    for home, out in ((home0, out0), (home1, out1)):
+def unpack_kernel(homes, out0, out1, area):
+    for home, out in ((homes.at[ZERO], out0), (homes.at[ONE], out1)):
         for band in range(PAIR):
             for k in range(RING):
                 for p in range(PAIR):
@@ -142,7 +142,7 @@
 
 def kernel(x_prev, x_cur, forcing, static, g2m_feat, m2g_feat, mesh_feat, mesh_edge_feat, stats, w_grid_in, w_mesh_in,
            w_eemb_in, w_embed_out, w_edge_in, w_edge_out, w_node_in, w_node_out, w_grid_self, w_out_hidden, w_out_final,
-           out0, out1,
+           out,
            mesh_raw, medge_raw, prev_raw, cur_raw, force_raw, static_raw, g2m_raw, m2g_raw,
            wgrid_raw, wmesh_raw, weemb_raw, wfin_raw, g_home, m_home, x_home,
            m_buf, x_buf, feat, we, weo, wself, woh, wof,
@@ -203,7 +203,9 @@
         pl.semaphore_signal(barrier, inc=1, device_id=at(lax.rem(me + hop, RING)), device_id_type=mesh_id)
 
     mine = pl.ds(PAIR * me, PAIR)
-    parts = ((m_home, m_buf.at[:, mine]), (g_home, feat.at[:, :, mine]), (x_home, x_buf.at[ZERO, :, :, mine]))
+    prev_lanes, cur_lanes = pl.ds(ZERO, LANES), pl.ds(LANES, LANES)
+    parts = ((m_home, m_buf.at[:, mine]), (g_home.at[..., prev_lanes], feat.at[:, :, mine, :, prev_lanes]),
+             (g_home.at[..., cur_lanes], feat.at[:, :, mine, :, cur_lanes]), (x_home, x_buf.at[ZERO, :, :, mine]))
 
     def in_copy(part, hop):
         src, dst = parts[part]
@@ -215,7 +217,7 @@
                                             recv_sem=in_recv.at[part, hop], device_id=at(target),
                                             device_id_type=mesh_id)
 
-    in_copies = [[in_copy(part, hop) for hop in range(RING)] for part in range(3)]
+    in_copies = [[in_copy(part, hop) for hop in range(RING)] for part in range(len(parts))]
 
     def wait_in(part):
         in_copies[part][0].wait()
@@ -252,31 +254,46 @@
     for copy in raw[2:8]:
         copy.wait()
     blocks = range(cur_raw.shape[1] // LANES)
+    rest = LANES - VARS
+    wide_mean = jnp.concatenate([stats[ZERO:ONE, :], jnp.zeros((ONE, rest), F32)], axis=ONE)
+    wide_std = jnp.concatenate([stats[ONE:PAIR, :], jnp.ones((ONE, rest), F32)], axis=ONE)
+
+    def spread(area, store):
+        ref, first = area
+        for k in range(RING):
+            for p in range(PAIR):
+                for t in range(TILES):
+                    for band in range(PAIR):
+                        store((k, p, t, band), jnp.concatenate(
+                            [ref[first + band, pl.ds(k * GRID_RUN + PAIR * r + p, rows, stride=PAIR), :] for r, rows in pieces(t)],
+                            axis=ZERO))
+
+    def store_prev(spot, rows):
+        g_home[(*spot, slice(None), prev_lanes)] = rows.astype(BF16)
+
+    def store_norm(spot, rows):
+        g_home[(*spot, slice(None), cur_lanes)] = rows.astype(BF16)
+
+    def store_cur(spot, rows):
+        x_home[spot] = rows
+
     for n in blocks:
         stack(place_of(prev_area, n), [
             (ZERO, prev_raw[:, columns(n)]), (AT_FORCE, force_raw[:, ZERO, columns(n)]), (AT_STATIC, static_raw[:, columns(n)]),
             (AT_NEXT, force_raw[:, ONE, columns(n)]), (AT_M2G, m2g_raw[:, columns(n)]), (AT_G2M, g2m_raw[:, columns(n)])])
+    for n in blocks:
+        place_of(prev_area, n)[...] = (turned(prev_area, n) - wide_mean) / wide_std
+    spread(prev_area, store_prev)
+    start_in(1)
+    for n in blocks:
         stack(place_of(cur_area, n), [(ZERO, cur_raw[:, columns(n)])])
-    rest = LANES - VARS
-    wide_mean = jnp.concatenate([stats[ZERO:ONE, :], jnp.zeros((ONE, rest), F32)], axis=ONE)
-    wide_std = jnp.concatenate([stats[ONE:PAIR, :], jnp.ones((ONE, rest), F32)], axis=ONE)
     for n in blocks:
-        prev, cur = turned(prev_area, n), turned(cur_area, n)
-        place_of(prev_area, n)[...] = (prev - wide_mean) / wide_std
+        cur = turned(cur_area, n)
         place_of(cur_area, n)[...] = cur
         place_of(norm_area, n)[...] = (cur - wide_mean) / wide_std
-    for k in range(RING):
-        for p in range(PAIR):
-            for t in range(TILES):
-                for band in range(PAIR):
-                    def rows_of(area):
-                        ref, first = area
-                        return jnp.concatenate([ref[first + band, pl.ds(k * GRID_RUN + PAIR * r + p, rows, stride=PAIR), :]
-                                                for r, rows in pieces(t)], axis=ZERO)
-                    g_home[k, p, t, band, :, pl.ds(ZERO, LANES)] = rows_of(prev_area).astype(BF16)
-                    g_home[k, p, t, band, :, pl.ds(LANES, LANES)] = rows_of(norm_area).astype(BF16)
-                    x_home[k, p, t, band] = rows_of(cur_area)
-    start_in(1)
+    spread(norm_area, store_norm)
+    start_in(2)
+    spread(cur_area, store_cur)
     for copy in small[1:] + enc_copies() + layer_copies(0, 1) + layer_copies(0, 2):
         copy.start()
 
@@ -346,7 +363,6 @@
     pipeline(items)
 
     wait_in(1)
-    start_in(PAIR)
     items = []
     for t in range(TILES):
         for p in range(PAIR):
@@ -357,6 +373,8 @@
             items.append(embed_item(lambda t=t, p=p: next_run(feat, p, t), 1, 2, store_g2m))
             items.append(embed_item(lambda t=t, p=p: feat[p, t, :, :, pl.ds(ZERO, LANES)].reshape(TILE, LANES), 2, 3, store_m2g))
     pipeline(items)
+    wait_in(2)
+    start_in(3)
     for copy in small[1:] + enc_copies():
         copy.wait()
 
@@ -574,16 +592,17 @@
                 table[f"sa{i}"], table[f"sb{i}"] = self_first, self_last
         run(ORDER_E, table)
 
-    def out_copies(step, out, t):
+    def out_copies(step, i):
+        t, p = divmod(i, PAIR)
         copies = []
         for hop in range(RING):
             target = lax.rem(me + hop, RING)
-            src, dst = x_buf.at[step + 1, :, t, pl.ds(PAIR * target, PAIR)], out.at[place, :, t]
+            src, dst = x_buf.at[step + 1, p, t, pl.ds(PAIR * target, PAIR)], out.at[step, place, p, t]
             if hop == 0:
-                copies.append(pltpu.make_async_copy(src, dst, out_recv.at[step, t, hop]))
+                copies.append(pltpu.make_async_copy(src, dst, out_recv.at[step, i, hop]))
             else:
                 copies.append(pltpu.make_async_remote_copy(
-                    src_ref=src, dst_ref=dst, send_sem=out_send.at[step, t, hop], recv_sem=out_recv.at[step, t, hop],
+                    src_ref=src, dst_ref=dst, send_sem=out_send.at[step, i, hop], recv_sem=out_recv.at[step, i, hop],
                     device_id=at(target), device_id_type=mesh_id))
         return copies
 
@@ -610,13 +629,7 @@
                 for c in chunks():
                     recv[part_rows(t, c), :] = out[c:c + CH]
 
-            def send(t=t):
-                for which, out in enumerate((out0, out1)):
-                    @pl.when(step == which)
-                    def _():
-                        start_all(out_copies(which, out, t))
-
-            table[f"t{t}"], table[f"send{t}"] = back, send
+            table[f"t{t}"] = back
             for p in range(PAIR):
                 i = PAIR * t + p
                 low, high = 8 + i, 12 + i
@@ -661,7 +674,10 @@
 
                 table[f"em{i}"], table[f"ea{i}"], table[f"eb{i}"] = edge_own, edge_first, edge_last
                 table[f"dm{i}"], table[f"da{i}"], table[f"db{i}"] = node_own, node_first, node_last
-                table[f"oa{i}"], table[f"ob{i}"] = out_first, out_last
+                def send(i=i):
+                    start_all(out_copies(step, i))
+
+                table[f"oa{i}"], table[f"ob{i}"], table[f"send{i}"] = out_first, out_last, send
         run(ORDER_D, table)
 
     def wait_all(copies):
@@ -698,17 +714,17 @@
         @pl.when(step == 0)
         def _():
             start_all(layer_copies(1, 1) + layer_copies(1, 2))
-            wait_in(PAIR)
+            wait_in(3)
 
         decoder(step)
         return carry
 
     lax.fori_loop(0, 2, one_step, 0)
-    for part in range(3):
-        for copy in in_copies[part][1:]:
+    for copies in in_copies:
+        for copy in copies[1:]:
             copy.wait_send()
-    for t in range(TILES):
-        wait_all(out_copies(0, out0, t) + out_copies(1, out1, t))
+    for i in range(PAIR * TILES):
+        wait_all(out_copies(0, i) + out_copies(1, i))
 
 
 def solution(mesh):
@@ -773,14 +789,14 @@
             pltpu.VMEM((10, TILE, LAT), F32),
             pltpu.VMEM((PAIR, RUNS, LAT), BF16),
             pltpu.VMEM((PAIR, 2, RUNS, LAT), BF16),
-            dma((12,)), dma((3, RING)), dma((3, RING)), dma((4,)), dma((1, 4)), dma((SLOTS, 4)), dma((PAIR,)), dma((PAIR, PAIR)),
-            dma((PAIR, TILES, RING)), dma((PAIR, TILES, RING)),
+            dma((12,)), dma((4, RING)), dma((4, RING)), dma((4,)), dma((1, 4)), dma((SLOTS, 4)), dma((PAIR,)), dma((PAIR, PAIR)),
+            dma((PAIR, PAIR * TILES, RING)), dma((PAIR, PAIR * TILES, RING)),
         ]
-        home0, home1 = pl.pallas_call(
+        homes = pl.pallas_call(
             kernel,
-            out_shape=(home, home),
+            out_shape=shape((PAIR, *home.shape), F32),
             in_specs=[any_spec] * 8 + [vmem_spec] + [any_spec] * 11,
-            out_specs=(any_spec, any_spec),
+            out_specs=any_spec,
             scratch_shapes=scratch,
             compiler_params=pltpu.CompilerParams(collective_id=0, has_side_effects=True, vmem_limit_bytes=63 << 20),
             name="forecast",
@@ -789,9 +805,9 @@
           w_edge_out, w_node_in, w_node_out, w_grid_self, w_out_hidden, w_out_final.T)
         out = shape((VARS, grid_dev), F32)
         next_state, after_state = pl.pallas_call(
-            unpack_kernel, out_shape=(out, out), in_specs=[vmem_spec] * 2, out_specs=(vmem_spec,) * 2,
+            unpack_kernel, out_shape=(out, out), in_specs=[vmem_spec], out_specs=(vmem_spec,) * 2,
             scratch_shapes=[pltpu.VMEM((grid_dev, LANES), F32)], name="unpack",
-        )(home0, home1)
+        )(homes)
         return next_state.T, after_state.T
 
     in_specs = (row_spec, row_spec, edge_spec, row_spec, row_spec, row_spec, row_spec, edge_spec, whole) + (whole,) * 11

time: 247 us -> 247 us (level)
  no operation moved by 1% of the time
where the time goes in v6:
time: 247 us
  Pallas kernels  246 us (100%)
    pallas_call x1, Pallas kernels, local_run(): pl.pallas_call(kernel, out_shape=shape((PAIR, *home.shape), F32), in_spec...  244 us

profile of v6, /device:TPU:0, one launch (start us, length us, event | category | flops | bytes accessed | tf_op | source)
XLA Modules:
  0.0 246.6 jit_solution(15045352229088571407)
XLA Ops:
  0.6 243.6 %forecast.1.homes = f32[2,8,2,2,2,16,128]{6,5,4,3,2,1,0:T(8,128)} custom-call(f32[84,1024]{1,0:T(8,128)} %bitcast.11, f32[84,1024]{1,0:T(8,128)} %bitcast.12, f32[5,2,1024]{2,1,0:T(2,128)} %bitcast.15, f32[5,1024]{1,0:T(8,128)} %bitcast.16, f32[4,1024]{1,0:T(4,128)} %bitcast.17, f32[4,1024]{1,0:T(4,128)} %bitcast.18, f32[3,512]{1,0:T(4,128)} %bitcast.19, ...), custom_call_target="tpu_custom_call" | custom-call | tf_op jit(solution)/shard_map/forecast/pallas_call | solution.py:795
  244.2 2.3 unpack.1

commit v7 on v5

--- a/solution.py
+++ b/solution.py
@@ -32,24 +32,24 @@
 FAR = ((2, 1), (3, -1), (4, 4), (5, -4))
 NEAR = ((0, 1), (1, -1))
 ORDER_A = (
-    "nh", "before", "fx0", "bx0", "n1", "fx1", "bx1", "fn0", "fn1", "bn0", "bn1", "ax0", "fx2", "ax1", "fx3",
-    "bx2", "na", "bx3", "ax2", "nb", "an0", "ax3", "ps", "pr",
+    "nh", "before", "fx0", "n1", "fx1", "bx0", "bx1", "fn0", "bn0", "fn1", "bn1", "ax0", "fx2", "fx3", "bx2",
+    "na", "ax1", "bx3", "ax2", "nb", "an0", "ax3", "pr", "ps",
 )
 ORDER_B = (
-    "nh", "before", "fx0", "bx0", "n1", "fx1", "bx1", "fn0", "fn1", "bn0", "bn1", "ax0", "fx2", "ax1", "fx3",
-    "bx2", "na", "bx3", "ax2", "nb", "an0", "ax3", "ps", "pr",
+    "nh", "before", "fx0", "fx1", "bx0", "n1", "fn1", "bx1", "fn0", "bn0", "bn1", "ax0", "fx2", "ax1", "fx3",
+    "bx2", "na", "bx3", "ax2", "nb", "ax3", "an0", "ps", "pr",
 )
 ORDER_E = (
-    "copy", "r0", "va0", "va1", "vb0", "va2", "vb1", "va3", "r1", "vb2", "vb3", "ea0", "sa0", "ea3", "ea1",
-    "eb0", "sa1", "eb1", "sb0", "ea2", "sb1", "nh0", "na0", "eb2", "sa2", "eb3", "nb0", "sa3", "sb2", "sb3",
-    "ya2", "ya0", "nh1", "ya1", "na1", "ps0", "pr0", "nb1", "yf0", "yb0", "yf1", "yb1", "ps1", "ya3", "pr1",
-    "yf2", "yb2", "yf3", "yb3", "xa0", "xa1", "za1", "xa2", "xa3", "za0", "za2", "za3", "n0", "share", "send",
+    "copy", "r0", "va1", "va0", "va2", "vb1", "vb0", "va3", "r1", "vb2", "vb3", "ea0", "sa0", "ea1", "sa1",
+    "eb0", "ea3", "sa2", "eb1", "sb0", "ea2", "sb1", "ya2", "nh0", "eb2", "na0", "sa3", "eb3", "nb0", "sb2",
+    "sb3", "ya0", "nh1", "ya1", "na1", "ps0", "pr0", "nb1", "yf0", "yb0", "yf1", "yb1", "ps1", "ya3", "pr1",
+    "yf2", "za1", "yb2", "yf3", "yb3", "xa0", "share", "xa1", "za3", "xa3", "za0", "za2", "xa2", "n0", "send",
 )
 ORDER_D = (
-    "fx0", "share", "nh0", "fx1", "bx0", "n01", "fn00", "fn01", "bn00", "bn01", "bx1", "em0", "fx2", "bx2",
-    "fx3", "bx3", "na0", "em1", "nb0", "n11", "dm0", "wait", "n10", "t0", "halo", "ea0", "fn11", "fn10",
-    "bn10", "bn11", "ea1", "eb0", "eb1", "nh1", "na1", "em2", "da0", "dm1", "nb1", "da1", "dm2", "em3", "db0",
-    "t1", "db1", "oa0", "ea2", "eb2", "oa1", "ob0", "ea3", "ob1", "send0", "eb3", "da2", "dm3", "da3", "db2",
+    "n01", "fx1", "nh0", "fx0", "share", "bx0", "fn00", "fn01", "bn00", "bn01", "bx1", "em0", "fx2", "bx2",
+    "fx3", "na0", "em1", "nb0", "n11", "wait", "dm0", "n10", "t0", "halo", "bx3", "ea0", "fn11", "fn10",
+    "bn10", "eb0", "bn11", "ea1", "eb1", "nh1", "em2", "em3", "na1", "da0", "dm1", "nb1", "da1", "dm2", "db0",
+    "t1", "db1", "oa0", "ea2", "eb2", "oa1", "ob0", "ea3", "dm3", "ob1", "send0", "eb3", "da2", "da3", "db2",
     "db3", "oa2", "oa3", "ob2", "ob3", "send1",
 )
 
@@ -125,8 +125,8 @@
         ref[pl.ds(end, LANES - end), :] = jnp.zeros((LANES - end, LANES), F32)
 
 
-def unpack_kernel(home0, home1, out0, out1, area):
-    for home, out in ((home0, out0), (home1, out1)):
+def unpack_kernel(homes, out0, out1, area):
+    for home, out in ((homes.at[ZERO], out0), (homes.at[ONE], out1)):
         for band in range(PAIR):
             for k in range(RING):
                 for p in range(PAIR):
@@ -142,7 +142,7 @@
 
 def kernel(x_prev, x_cur, forcing, static, g2m_feat, m2g_feat, mesh_feat, mesh_edge_feat, stats, w_grid_in, w_mesh_in,
            w_eemb_in, w_embed_out, w_edge_in, w_edge_out, w_node_in, w_node_out, w_grid_self, w_out_hidden, w_out_final,
-           out0, out1,
+           out,
            mesh_raw, medge_raw, prev_raw, cur_raw, force_raw, static_raw, g2m_raw, m2g_raw,
            wgrid_raw, wmesh_raw, weemb_raw, wfin_raw, g_home, m_home, x_home,
            m_buf, x_buf, feat, we, weo, wself, woh, wof,
@@ -574,11 +574,11 @@
                 table[f"sa{i}"], table[f"sb{i}"] = self_first, self_last
         run(ORDER_E, table)
 
-    def out_copies(step, out, t):
+    def out_copies(step, t):
         copies = []
         for hop in range(RING):
             target = lax.rem(me + hop, RING)
-            src, dst = x_buf.at[step + 1, :, t, pl.ds(PAIR * target, PAIR)], out.at[place, :, t]
+            src, dst = x_buf.at[step + 1, :, t, pl.ds(PAIR * target, PAIR)], out.at[step, place, :, t]
             if hop == 0:
                 copies.append(pltpu.make_async_copy(src, dst, out_recv.at[step, t, hop]))
             else:
@@ -611,10 +611,7 @@
                     recv[part_rows(t, c), :] = out[c:c + CH]
 
             def send(t=t):
-                for which, out in enumerate((out0, out1)):
-                    @pl.when(step == which)
-                    def _():
-                        start_all(out_copies(which, out, t))
+                start_all(out_copies(step, t))
 
             table[f"t{t}"], table[f"send{t}"] = back, send
             for p in range(PAIR):
@@ -708,7 +705,7 @@
         for copy in in_copies[part][1:]:
             copy.wait_send()
     for t in range(TILES):
-        wait_all(out_copies(0, out0, t) + out_copies(1, out1, t))
+        wait_all(out_copies(0, t) + out_copies(1, t))
 
 
 def solution(mesh):
@@ -776,11 +773,11 @@
             dma((12,)), dma((3, RING)), dma((3, RING)), dma((4,)), dma((1, 4)), dma((SLOTS, 4)), dma((PAIR,)), dma((PAIR, PAIR)),
             dma((PAIR, TILES, RING)), dma((PAIR, TILES, RING)),
         ]
-        home0, home1 = pl.pallas_call(
+        homes = pl.pallas_call(
             kernel,
-            out_shape=(home, home),
+            out_shape=shape((PAIR, *home.shape), F32),
             in_specs=[any_spec] * 8 + [vmem_spec] + [any_spec] * 11,
-            out_specs=(any_spec, any_spec),
+            out_specs=any_spec,
             scratch_shapes=scratch,
             compiler_params=pltpu.CompilerParams(collective_id=0, has_side_effects=True, vmem_limit_bytes=63 << 20),
             name="forecast",
@@ -789,9 +786,9 @@
           w_edge_out, w_node_in, w_node_out, w_grid_self, w_out_hidden, w_out_final.T)
         out = shape((VARS, grid_dev), F32)
         next_state, after_state = pl.pallas_call(
-            unpack_kernel, out_shape=(out, out), in_specs=[vmem_spec] * 2, out_specs=(vmem_spec,) * 2,
+            unpack_kernel, out_shape=(out, out), in_specs=[vmem_spec], out_specs=(vmem_spec,) * 2,
             scratch_shapes=[pltpu.VMEM((grid_dev, LANES), F32)], name="unpack",
-        )(home0, home1)
+        )(homes)
         return next_state.T, after_state.T
 
     in_specs = (row_spec, row_spec, edge_spec, row_spec, row_spec, row_spec, row_spec, edge_spec, whole) + (whole,) * 11

time: 247 us -> 245 us (level)
  no operation moved by 1% of the time
where the time goes in v7:
time: 245 us
  Pallas kernels  245 us (100%)
    pallas_call x1, Pallas kernels, local_run(): pl.pallas_call(kernel, out_shape=shape((PAIR, *home.shape), F32), in_spec...  242 us

profile of v7, /device:TPU:0, one launch (start us, length us, event | category | flops | bytes accessed | tf_op | source)
XLA Modules:
  0.0 245.2 jit_solution(4022211376167425208)
XLA Ops:
  0.6 242.2 %forecast.1.homes = f32[2,8,2,2,2,16,128]{6,5,4,3,2,1,0:T(8,128)} custom-call(f32[84,1024]{1,0:T(8,128)} %bitcast.11, f32[84,1024]{1,0:T(8,128)} %bitcast.12, f32[5,2,1024]{2,1,0:T(2,128)} %bitcast.15, f32[5,1024]{1,0:T(8,128)} %bitcast.16, f32[4,1024]{1,0:T(4,128)} %bitcast.17, f32[4,1024]{1,0:T(4,128)} %bitcast.18, f32[3,512]{1,0:T(4,128)} %bitcast.19, ...), custom_call_target="tpu_custom_call" | custom-call | tf_op jit(solution)/shard_map/forecast/pallas_call | solution.py:776
  242.8 2.3 unpack.1
